TPU v7x, 32 devices: a whole 2x2x4 slice. The times are simulated.
32 devices in a mesh: groups: 2 (over x), width: 8 (over z, y), guide: 2 (over core).
Axes of the slice: x: 2, y: 2, z: 4, core: 2. Of those that a mesh axis runs over, the one named last changes fastest.
Arguments:
- latent: float32 [16, 8, 2048], P(None, None, ('groups', 'width')), parts along dimension 2, may hold values from -6 to 6
- starts: int32 [16], P(('groups', 'width')), parts along dimension 0, may hold values from 0 to 1023, as said below
- counts: int32 [2048], P(('groups', 'width')), parts along dimension 0, may hold values from 1 to 3, as said below
- step_index: int32 [2], P('groups'), parts along dimension 0, may hold values from 0 to 27
- cond_mod: float32 [2, 3, 2432], P('guide'), may hold values from -3 to 3
- w_patch: bfloat16 [64, 2432], replicated, may hold values from -0.75 to 0.75
- w_qkv: bfloat16 [2432, 3840], P('width'), may hold values from -0.125 to 0.125
- w_out: bfloat16 [1280, 2432], replicated, may hold values from -0.15625 to 0.15625
- w_final: bfloat16 [2432, 64], replicated, may hold values from -0.125 to 0.125
- w_dec: bfloat16 [144, 512], replicated, may hold values from -0.5 to 0.5
Outputs:
- denoised: float32 [16, 8, 2048], P(None, 'guide', ('groups', 'width')), parts along dimension 2
- features: bfloat16 [8, 2048, 512], P('guide', ('groups', 'width')), parts along dimension 1
There are 2 independent parts, one for each index of `groups`. A program takes and returns all parts, laid end to end along the dimension named above; an argument that names none is the same for every part. Nothing has to cross between parts.
Inputs may be any that keep to these rules, and one draw needn't show every extreme that they name: window k starts between column k * 128 and column (k + 1) * 128 - 1 and covers 2 * 128 columns, wrapping around the panorama. `counts`: the number of windows whose columns, as given by starts, include the column.
All inputs are finite; a program needn't handle non-finite values.
Results may differ from a plain program's by a relative error of at most 0.013.
Values may be sent and summed in bfloat16 or wider, within the bound.
No kernel may reach another device: no remote copies, remote signals or barrier semaphores. Data moves between devices by JAX's collectives and lax.ppermute only.
A program may use at most 128 MiB of HBM per device.

v0:
```python
import jax
import jax.numpy as jnp
from jax import lax
from jax.sharding import PartitionSpec as P

HEADS = 20
HEAD = 64
STEPS = 28


guidance = 4.0
epsilon = 1e-06


def from_behind(x, axis, by):
    peers = lax.axis_size(axis)
    return lax.ppermute(x, axis, [(i, (i + by) % peers) for i in range(peers)])


def from_partner(block, axis, stride):
    count = lax.axis_size(axis)
    route = []
    for low in range(count):
        high = low | 1 << stride
        if high != low and high < count:
            route += [(low, high), (high, low)]
    return lax.ppermute(block, axis, route)


def extended(block, sides, width):
    for axis, dim in sides:
        count = lax.axis_size(axis)
        forward = [(i, i + 1) for i in range(count - 1)]
        backward = [(target, source) for source, target in forward]
        low = lax.ppermute(
            lax.slice_in_dim(block, block.shape[dim] - width, None, axis=dim), axis, forward
        )
        high = lax.ppermute(lax.slice_in_dim(block, 0, width, axis=dim), axis, backward)
        block = jnp.concatenate([low, block, high], axis=dim)
    return block


def layer_norm(values):
    centered = values - jnp.mean(values, axis=-1, keepdims=True)
    spread = jnp.mean(centered * centered, axis=-1, keepdims=True)
    return centered * lax.rsqrt(spread + epsilon)


def head_norm(values):
    return values * lax.rsqrt(jnp.mean(values * values, axis=-1, keepdims=True) + epsilon)


def patchify(window):
    channels, height, breadth = window.shape
    folded = window.reshape(channels, height // 2, 2, breadth // 2, 2).transpose(1, 3, 2, 4, 0)
    return folded.reshape(height // 2 * (breadth // 2), 4 * channels)


def unpatchify(tokens, channels, height, breadth):
    folded = tokens.reshape(height // 2, breadth // 2, 2, 2, channels).transpose(4, 0, 2, 1, 3)
    return folded.reshape(channels, height, breadth)


def attend(queries, key_rows, value_rows):
    scores = jnp.einsum("bqhe,bkhe->bhqk", queries, key_rows, preferred_element_type=jnp.float32)
    scores = scores / jnp.sqrt(jnp.float32(queries.shape[-1]))
    weights = jax.nn.softmax(scores, axis=-1).astype(jnp.bfloat16)
    mixed = jnp.einsum("bhqk,bkhe->bqhe", weights, value_rows, preferred_element_type=jnp.float32)
    return mixed.astype(jnp.bfloat16)


def convolve(padded, w_dec):
    channels = padded.shape[0]
    height = padded.shape[1] - 2
    breadth = padded.shape[2] - 2
    shifted = [
        padded[:, row_at : row_at + height, col_at : col_at + breadth]
        for row_at in range(3)
        for col_at in range(3)
    ]
    stacked = jnp.stack(shifted).reshape(9 * channels, height * breadth)
    summed = lax.dot_general(
        stacked, w_dec, (((0,), (0,)), ((), ())), preferred_element_type=jnp.float32
    )
    return jax.nn.silu(summed).astype(jnp.bfloat16).reshape(height, breadth, w_dec.shape[1])


def fetch_next(block):
    return from_behind(block, "width", -1)


def pass_right(block):
    return from_behind(block.astype(jnp.bfloat16), "width", 1).astype(block.dtype)


def shards(latent, starts, counts, step_index, cond_mod, w_patch, w_qkv, w_out, w_final, w_dec):
    guide_at = lax.axis_index("guide")
    place = lax.axis_index("width")
    channels, height, columns = latent.shape
    half_rows = height // 2
    fraction = (step_index[0].astype(jnp.float32) + 1.0) / STEPS
    sigma = 3.0 * fraction / (1.0 + 2.0 * fraction)
    modulation = cond_mod[0]
    own_cols = latent.astype(jnp.bfloat16)
    ahead = fetch_next(own_cols)
    further = fetch_next(ahead)
    three_blocks = jnp.concatenate([own_cols, ahead, further], axis=2)
    offset = starts[0] - place * columns
    window = lax.dynamic_slice_in_dim(three_blocks, offset, 2 * columns, 2)
    patches = patchify(window)
    token_count = patches.shape[0]
    hidden = jnp.dot(patches, w_patch, preferred_element_type=jnp.float32)
    modulated = (layer_norm(hidden) * (1.0 + modulation[1]) + modulation[0]).astype(jnp.bfloat16)
    partner = from_partner(modulated, "guide", 0)
    both_rows = jnp.where(
        guide_at == 0, jnp.stack([modulated, partner]), jnp.stack([partner, modulated])
    )
    both_rows = both_rows.reshape(2 * token_count, modulated.shape[1])
    head_share = HEADS // 2
    shard_rows = w_qkv.shape[0]
    weight_half = lax.dynamic_slice_in_dim(
        w_qkv.reshape(shard_rows, 3, HEADS, HEAD), guide_at * head_share, head_share, 2
    )
    weight_half = weight_half.reshape(shard_rows, 3 * head_share * HEAD)
    projected = jnp.dot(
        both_rows,
        lax.all_gather(weight_half, "width", axis=0, tiled=True),
        preferred_element_type=jnp.float32,
    )
    projected = projected.reshape(2, token_count, 3, head_share, HEAD)
    queries = head_norm(projected[:, :, 0]).astype(jnp.bfloat16)
    key_rows = head_norm(projected[:, :, 1]).astype(jnp.bfloat16)
    value_rows = projected[:, :, 2].astype(jnp.bfloat16)
    attended = attend(queries, key_rows, value_rows).reshape(2 * token_count, head_share * HEAD)
    out_rows = lax.dynamic_slice_in_dim(w_out, guide_at * head_share * HEAD, head_share * HEAD, 0)
    partial_value = jnp.dot(attended, out_rows, preferred_element_type=jnp.float32).reshape(
        2, token_count, w_out.shape[1]
    )
    mixed_out = lax.psum_scatter(
        partial_value.astype(jnp.bfloat16), "guide", scatter_dimension=0, tiled=True
    ).astype(jnp.float32)[0]
    residual = hidden + modulation[2] * mixed_out
    final_in = layer_norm(residual).astype(jnp.bfloat16)
    result = jnp.dot(final_in, w_final, preferred_element_type=jnp.float32)
    velocity_win = unpatchify(result, channels, height, 2 * columns)
    branch_pair = lax.all_to_all(
        velocity_win[None].astype(jnp.bfloat16), "guide", split_axis=2, concat_axis=0, tiled=True
    ).astype(jnp.float32)
    guided = branch_pair[1] + guidance * (branch_pair[0] - branch_pair[1])
    spread_out = jnp.zeros((channels, half_rows, 3 * columns), jnp.float32)
    spread_out = lax.dynamic_update_slice_in_dim(spread_out, guided, offset, 2)
    carried = pass_right(spread_out[:, :, 2 * columns :])
    arrived = pass_right(spread_out[:, :, columns : 2 * columns] + carried)
    summed = spread_out[:, :, :columns] + arrived
    velocity = summed / counts.astype(jnp.float32)[None, None, :]
    mine_rows = lax.dynamic_slice_in_dim(latent, guide_at * half_rows, half_rows, 1)
    denoised = mine_rows - sigma * velocity
    padded = extended(denoised.astype(jnp.bfloat16), (("guide", 1), ("width", 2)), 1)
    features = convolve(padded, w_dec)
    return (denoised, features)


def solution(mesh):
    return jax.shard_map(
        shards,
        mesh=mesh,
        in_specs=(
            P(None, None, ("groups", "width")),
            P(("groups", "width")),
            P(("groups", "width")),
            P("groups"),
            P("guide", None, None),
            P(),
            P("width", None),
            P(),
            P(),
            P(),
        ),
        out_specs=(P(None, "guide", ("groups", "width")), P("guide", ("groups", "width"), None)),
        check_vma=False,
    )
```

profile of v0, /device:TPU:0, one launch (start us, length us, event | category | flops | bytes accessed | tf_op | source)
XLA Modules:
  0.0 284.3 jit_solution(5866533222557531510)
XLA Ops:
  7.3 3.7 %copy.37 = bf16[304,3840]{0,1:T(8,128)(2,1)S(1)} copy(bf16[304,3840]{1,0:T(8,128)(2,1)} %param.16) | data formatting | bytes 4669440 | tf_op args[6]
  10.9 1.3 constant_dynamic-slice_fusion
  12.2 2.5 copy.38
  14.8 6.1 %collective-permute-start = (bf16[16,8,128]{2,1,0:T(8,128)(2,1)S(1)}, bf16[16,8,128]{2,1,0:T(8,128)(2,1)S(1)}, u32[]{:S(2)}, u32[]{:S(2)}) collective-permute-start(bf16[16,8,128]{2,1,0:T(8,128)(2,1)S(1)} %convert_element_type.86), channel_id=1, source_target_pairs={{0,14},{2,0},{4,2},{6,4},{8,6},{10,8},{12,10},{14,12},{1,15},{3,1}... | collective-permute-start | bytes 98312 | tf_op jit(solution)/shard_map/ppermute | solution.py:17
  20.9 1.6 collective-permute-done
  22.5 5.0 %collective-permute-start.1 = (bf16[16,8,128]{2,1,0:T(8,128)(2,1)S(1)}, bf16[16,8,128]{2,1,0:T(8,128)(2,1)S(1)}, u32[]{:S(2)}, u32[]{:S(2)}) collective-permute-start(bf16[16,8,128]{2,1,0:T(8,128)(2,1)S(1)} %collective-permute-done), channel_id=1, source_target_pairs={{0,14},{2,0},{4,2},{6,4},{8,6},{10,8},{12,10},{14,12},{1,15},{3,1}... | collective-permute-start | bytes 98312 | tf_op jit(solution)/shard_map/ppermute | solution.py:17
  28.3 1.4 collective-permute-done.1
  29.7 0.1 fusion.33
  29.8 0.3 copy.35
  30.1 0.4 copy.36
  30.5 0.9 fusion.52
  31.4 0.6 multiply_reduce_fusion.2
  32.1 1.0 add_convert_fusion
  33.1 0.6 copy-done.2
  33.6 4.9 %fusion.59 = bf16[1,512,2432]{2,1,0:T(8,128)(2,1)} fusion(f32[2432]{0:T(1024)S(1)} %get-tuple-element.5, f32[2432]{0:T(1024)S(1)} %get-tuple-element.6, f32[512]{0:T(512)S(1)} %add_rsqrt_fusion.3, f32[512,2432]{1,0:T(8,128)} %copy-done.2, f32[512]{0:T(512)S(1)} %broadcast_multiply_fusion.1), kind=kLoop, calls=%fused_computation.109 | loop fusion | flops 6225920 | bytes 7494656 | tf_op jit(solution)/shard_map/stack | solution.py:116
  38.5 115.2 %all-gather.2.cloned.1.call-done = bf16[2432,1920]{1,0:T(8,128)(2,1)} async-done(((bf16[304,1920]{1,0:T(8,128)(2,1)}), bf16[2432,1920]{1,0:T(8,128)(2,1)}) %all-gather.2.cloned.1.call-update) | async-done | bytes 9338896 | tf_op jit(solution)/shard_map/all_gather | solution.py:127
  153.7 13.3 %copy.39 = bf16[1920,2432]{1,0:T(8,128)(2,1)} copy(bf16[1920,2432]{0,1:T(8,128)(2,1)} %bitcast.153) | data formatting | bytes 18677760 | tf_op jit(solution)/shard_map/dot_general | solution.py:125
  166.9 23.0 %fusion.7 = f32[2,512,3,10,64]{1,4,3,2,0:T(8,128)S(1)} fusion(bf16[3,10,64,2432,1]{3,2,1,0,4:T(8,128)(2,1)} %bitcast.154, bf16[1,512,2432]{2,1,0:T(8,128)(2,1)} %bitcast.5, bf16[1,512,2432]{2,1,0:T(8,128)(2,1)} %fusion.59, pred[]{:T(512)S(6)} %eq.3), kind=kOutput, calls=%fused_computation.10 | convolution fusion | flops 9585426432 | bytes 22183936 | tf_op jit(solution)/shard_map/dot_general | solution.py:125
  189.9 3.1 %copy-done.4 = f32[2,512,3,10,64]{1,4,3,2,0:T(8,128)} copy-done((f32[2,512,3,10,64]{1,4,3,2,0:T(8,128)}, f32[2,512,3,10,64]{1,4,3,2,0:T(8,128)S(1)}, u32[]{:S(2)}) %copy-start.4) | copy-done | bytes 7864344
  193.1 0.8 multiply_reduce_fusion.3
  193.9 13.0 %fusion.53 = (f32[2,10,512]{2,1,0:T(8,128)S(1)}, f32[2,10,512,512]{2,3,1,0:T(8,128)}) fusion(f32[2,512,3,10,64]{1,4,3,2,0:T(8,128)} %copy-done.4, f32[2,512,10]{1,2,0:T(8,128)S(1)} %get-tuple-element.20, f32[2,512,10]{1,2,0:T(8,128)S(1)} %get-tuple-element.19), kind=kOutput, calls=%fused_computation.108 | convolution fusion | flops 689439232 | bytes 26337280 | tf_op jit(solution)/shard_map/sub | solution.py:67
  206.8 9.8 %fusion.23 = bf16[2,10,64,512]{3,2,1,0:T(8,128)(2,1)S(1)} fusion(f32[2,10,512,512]{2,3,1,0:T(8,128)} %get-tuple-element.18, f32[2,10,512]{2,1,0:T(8,128)S(1)} %get-tuple-element.17, f32[2,512,3,10,64]{1,4,3,2,0:T(8,128)} %copy-done.4), kind=kOutput, calls=%fused_computation.36 | convolution fusion | flops 682229760 | bytes 23633920 | tf_op jit(solution)/shard_map/bhqk,bkhe->bqhe/dot_general | solution.py:68
  216.7 6.0 %convolution_convert_fusion = bf16[2,512,2432]{2,1,0:T(8,128)(2,1)} fusion(bf16[2,512,640]{1,2,0:T(8,128)(2,1)S(1)} %bitcast.164, bf16[1280,2432]{1,0:T(8,128)(2,1)S(1)} %bitcast.163, s32[]{:T(128)S(6)} %select_n.28), kind=kOutput, calls=%fused_computation.7 | convolution fusion | flops 3190161408 | bytes 9404420 | tf_op jit(solution)/shard_map/dot_general | solution.py:136
  222.8 11.1 %reduce-scatter.2.cloned.1.call-done = bf16[1,512,2432]{2,1,0:T(8,128)(2,1)} async-done(((bf16[2,512,2432]{2,1,0:T(8,128)(2,1)}), bf16[1,512,2432]{2,1,0:T(8,128)(2,1)}) %reduce-scatter.2.cloned.1.call-update) | async-done | bytes 2490384 | tf_op jit(solution)/shard_map/reduce_scatter | solution.py:139
  233.9 4.1 %fusion.27 = f32[512]{0:T(512)S(1)} fusion(f32[512,2432]{1,0:T(8,128)} %copy-done.2, bf16[1,512,2432]{2,1,0:T(8,128)(2,1)} %reduce-scatter.2.cloned.1.call-done, f32[2432]{0:T(1024)S(1)} %get-tuple-element.4), kind=kLoop, calls=%fused_computation.38 | loop fusion | flops 4980224 | bytes 7482880 | tf_op jit(solution)/shard_map/reduce_sum | solution.py:44
  238.0 3.7 %multiply_reduce_fusion.1 = f32[512]{0:T(512)S(1)} fusion(f32[512]{0:T(512)S(1)} %broadcast_multiply_fusion, f32[512,2432]{1,0:T(8,128)} %copy-done.2, bf16[1,512,2432]{2,1,0:T(8,128)(2,1)S(1)} %copy-done.3, f32[2432]{0:T(1024)S(1)} %get-tuple-element.4), kind=kLoop, calls=%fused_computation.19 | loop fusion | flops 7470592 | bytes 7484928 | tf_op jit(solution)/shard_map/reduce_sum | solution.py:45
  241.8 1.3 fusion.28
  243.1 0.4 copy.42
  243.5 0.2 copy.43
  243.7 3.8 %all_to_all.4 = bf16[1,16,8,256]{3,1,0,2:T(8,128)(2,1)S(1)} all-to-all(bf16[1,16,8,256]{3,1,0,2:T(8,128)(2,1)S(1)} %copy.43), channel_id=1, replica_groups=mesh['groups'=2,'width'=8,'guide'=2] {'guide'}, dimensions={2} | all-to-all | bytes 131072 | tf_op jit(solution)/shard_map/all_to_all | solution.py:146
  247.6 2.6 dynamic_update_slice.3
  250.2 1.9 collective-permute-start.3
  252.1 4.6 %collective-permute-done.3 = bf16[16,4,128]{2,1,0:T(4,128)(2,1)S(1)} collective-permute-done((bf16[16,4,128]{2,1,0:T(4,128)(2,1)S(1)}, bf16[16,4,128]{2,1,0:T(4,128)(2,1)S(1)}, u32[]{:S(2)}, u32[]{:S(2)}) %collective-permute-start.3) | collective-permute-done | bytes 16416 | tf_op jit(solution)/shard_map/ppermute | solution.py:17
  257.5 5.7 %collective-permute-done.4 = bf16[16,4,128]{2,1,0:T(4,128)(2,1)S(1)} collective-permute-done((bf16[16,4,128]{2,1,0:T(4,128)(2,1)S(1)}, bf16[16,4,128]{2,1,0:T(4,128)(2,1)S(1)}, u32[]{:S(2)}, u32[]{:S(2)}) %collective-permute-start.4) | collective-permute-done | bytes 16416 | tf_op jit(solution)/shard_map/ppermute | solution.py:17
  263.2 0.6 fusion.49
  263.8 1.3 collective-permute-start.5
  265.1 1.3 collective-permute-start.6
  266.5 1.8 collective-permute-done.6
  268.3 1.3 collective-permute-start.7
  269.6 1.3 collective-permute-start.8
  270.9 0.3 collective-permute-done.7
  271.3 4.1 %collective-permute-done.8 = bf16[16,6,1]{2,1,0:T(8,128)(2,1)S(1)} collective-permute-done((bf16[16,6,1]{2,1,0:T(8,128)(2,1)S(1)}, bf16[16,6,1]{2,1,0:T(8,128)(2,1)S(1)}, u32[]{:S(2)}, u32[]{:S(2)}) %collective-permute-start.8) | collective-permute-done | bytes 224 | tf_op jit(solution)/shard_map/ppermute | solution.py:38
  275.4 0.1 constant_dynamic-update-slice_fusion.6
  275.6 0.1 constant_dynamic-update-slice_fusion.5
  275.7 0.1 constant_dynamic-update-slice_fusion.3
  275.8 0.1 constant_dynamic-update-slice_fusion.2
  276.0 0.1 constant_dynamic-update-slice_fusion
  276.1 1.3 multiply_convert_fusion.6
  (58 shorter events, 0.8 us)
Async XLA Ops:
  7.2 23.3 %copy-start = (bf16[64,2432]{1,0:T(8,128)(2,1)S(1)}, bf16[64,2432]{1,0:T(8,128)(2,1)}, u32[]{:S(2)}) copy-start(bf16[64,2432]{1,0:T(8,128)(2,1)} %param.15) | copy-start | bytes 933892
  7.2 146.5 %all-gather.2.cloned.1.call-start = ((), (), s32[]{:S(2)}) async-start(), calls=%async_computation.2 | async-start | bytes 10506240 | tf_op jit(solution)/shard_map/all_gather | solution.py:127
  7.2 7.6 %copy-start.6 = (f32[16,8,128]{2,1,0:T(8,128)S(1)}, f32[16,8,128]{2,1,0:T(8,128)}, u32[]{:S(2)}) copy-start(f32[16,8,128]{2,1,0:T(8,128)} %param.10) | copy-start | bytes 196612
  7.2 20.3 %copy-start.7 = (f32[1,3,2432]{2,0,1:T(1,128)S(1)}, f32[1,3,2432]{2,0,1:T(1,128)}, u32[]{:S(2)}) copy-start(f32[1,3,2432]{2,0,1:T(1,128)} %param.14) | copy-start | bytes 87556
  14.8 219.1 %reduce-scatter.2.cloned.1.call-start = ((), (), s32[]{:S(2)}) async-start(), calls=%async_computation.3 | async-start | bytes 7471104 | tf_op jit(solution)/shard_map/reduce_scatter | solution.py:139
  14.8 7.7 %collective-permute-start = (bf16[16,8,128]{2,1,0:T(8,128)(2,1)S(1)}, bf16[16,8,128]{2,1,0:T(8,128)(2,1)S(1)}, u32[]{:S(2)}, u32[]{:S(2)}) collective-permute-start(bf16[16,8,128]{2,1,0:T(8,128)(2,1)S(1)} %convert_element_type.86), channel_id=1, source_target_pairs={{0,14},{2,0},{4,2},{6,4},{8,6},{10,8},{12,10},{14,12},{1,15},{3,1}... | collective-permute-start | bytes 98312 | tf_op jit(solution)/shard_map/ppermute | solution.py:17
  22.5 7.2 %collective-permute-start.1 = (bf16[16,8,128]{2,1,0:T(8,128)(2,1)S(1)}, bf16[16,8,128]{2,1,0:T(8,128)(2,1)S(1)}, u32[]{:S(2)}, u32[]{:S(2)}) collective-permute-start(bf16[16,8,128]{2,1,0:T(8,128)(2,1)S(1)} %collective-permute-done), channel_id=1, source_target_pairs={{0,14},{2,0},{4,2},{6,4},{8,6},{10,8},{12,10},{14,12},{1,15},{3,1}... | collective-permute-start | bytes 98312 | tf_op jit(solution)/shard_map/ppermute | solution.py:17
  31.4 2.2 copy-start.2
  33.6 133.3 %collective-permute-start.2 = (bf16[512,2432]{1,0:T(8,128)(2,1)S(1)}, bf16[512,2432]{1,0:T(8,128)(2,1)}, u32[]{:S(2)}, u32[]{:S(2)}) collective-permute-start(bf16[512,2432]{1,0:T(8,128)(2,1)S(1)} %add_convert_fusion), channel_id=1, source_target_pairs={{0,1},{1,0},{2,3},{3,2},{4,5},{5,4},{6,7},{7,6},{8,9},{9,8},{10,11... | collective-permute-start | bytes 7471112 | tf_op jit(solution)/shard_map/ppermute | solution.py:27
  189.9 3.1 %copy-start.4 = (f32[2,512,3,10,64]{1,4,3,2,0:T(8,128)}, f32[2,512,3,10,64]{1,4,3,2,0:T(8,128)S(1)}, u32[]{:S(2)}) copy-start(f32[2,512,3,10,64]{1,4,3,2,0:T(8,128)S(1)} %fusion.7) | copy-start | bytes 23592964
  193.9 22.8 %slice-start.2 = ((s8[6225920]{0:T(1024)(128)(4,1)}), s8[2031616]{0:T(1024)(128)(4,1)S(1)}, s32[]{:S(2)}) async-start(s8[6225920]{0:T(1024)(128)(4,1)} %bitcast.162), calls=%async_computation.6 | async-start | bytes 4063232
  206.8 9.9 %slice-start.3 = ((s8[6225920]{0:T(1024)(128)(4,1)}), s8[4194304]{0:T(1024)(128)(4,1)S(1)}, s32[]{:S(2)}) async-start(s8[6225920]{0:T(1024)(128)(4,1)} %bitcast.162), calls=%async_computation.7 | async-start | bytes 8388608
  222.7 19.0 %slice-start = ((s8[4980736]{0:T(1024)(128)(4,1)}), s8[786432]{0:T(1024)(128)(4,1)S(1)}, s32[]{:S(2)}) async-start(s8[4980736]{0:T(1024)(128)(4,1)} %bitcast.151), calls=%async_computation.4 | async-start | bytes 1572864
  233.9 4.1 %copy-start.3 = (bf16[1,512,2432]{2,1,0:T(8,128)(2,1)S(1)}, bf16[1,512,2432]{2,1,0:T(8,128)(2,1)}, u32[]{:S(2)}) copy-start(bf16[1,512,2432]{2,1,0:T(8,128)(2,1)} %reduce-scatter.2.cloned.1.call-done) | copy-start | bytes 7471108
  233.9 7.8 %slice-start.1 = ((s8[4980736]{0:T(1024)(128)(4,1)}), s8[4194304]{0:T(1024)(128)(4,1)S(1)}, s32[]{:S(2)}) async-start(s8[4980736]{0:T(1024)(128)(4,1)} %bitcast.151), calls=%async_computation.5 | async-start | bytes 8388608
  238.0 3.8 %copy-start.5 = (bf16[2432,64]{0,1:T(8,128)(2,1)S(1)}, bf16[2432,64]{0,1:T(8,128)(2,1)}, u32[]{:S(2)}) copy-start(bf16[2432,64]{0,1:T(8,128)(2,1)} %param.18) | copy-start | bytes 933892
  241.7 15.7 %copy-start.9 = (s32[128]{0:T(128)S(1)}, s32[128]{0:T(128)}, u32[]{:S(2)}) copy-start(s32[128]{0:T(128)} %param.12) | copy-start | bytes 1540
  241.8 34.4 %copy-start.8 = (bf16[144,512]{1,0:T(8,128)(2,1)S(1)}, bf16[144,512]{1,0:T(8,128)(2,1)}, u32[]{:S(2)}) copy-start(bf16[144,512]{1,0:T(8,128)(2,1)} %param.19) | copy-start | bytes 442372
  241.8 35.7 %copy-start.1 = (bf16[64,2432]{1,0:T(8,128)(2,1)S(1)}, bf16[64,2432]{1,0:T(8,128)(2,1)}, u32[]{:S(2)}) copy-start(bf16[64,2432]{1,0:T(8,128)(2,1)} %param.15) | copy-start | bytes 933892
  250.2 6.5 %collective-permute-start.3 = (bf16[16,4,128]{2,1,0:T(4,128)(2,1)S(1)}, bf16[16,4,128]{2,1,0:T(4,128)(2,1)S(1)}, u32[]{:S(2)}, u32[]{:S(2)}) collective-permute-start(bf16[16,4,128]{2,1,0:T(4,128)(2,1)S(1)} %slice.166), channel_id=1, source_target_pairs={{0,2},{2,4},{4,6},{6,8},{8,10},{10,12},{12,14},{14,0},{1,3},{3,5},... | collective-permute-start | bytes 49160 | tf_op jit(solution)/shard_map/ppermute | solution.py:17
  256.7 6.5 %collective-permute-start.4 = (bf16[16,4,128]{2,1,0:T(4,128)(2,1)S(1)}, bf16[16,4,128]{2,1,0:T(4,128)(2,1)S(1)}, u32[]{:S(2)}, u32[]{:S(2)}) collective-permute-start(bf16[16,4,128]{2,1,0:T(4,128)(2,1)S(1)} %fusion.40), channel_id=1, source_target_pairs={{0,2},{2,4},{4,6},{6,8},{8,10},{10,12},{12,14},{14,0},{1,3},{3,5},... | collective-permute-start | bytes 49160 | tf_op jit(solution)/shard_map/ppermute | solution.py:17
  263.8 2.6 collective-permute-start.5
  265.1 3.1 %collective-permute-start.6 = (bf16[16,1,128]{2,1,0:T(2,128)(2,1)S(1)}, bf16[16,1,128]{2,1,0:T(2,128)(2,1)S(1)}, u32[]{:S(2)}, u32[]{:S(2)}) collective-permute-start(bf16[16,1,128]{2,1,0:T(2,128)(2,1)S(1)} %get-tuple-element.14), channel_id=1, source_target_pairs={{1,0},{3,2},{5,4},{7,6},{9,8},{11,10},{13,12},{15,14},{17,16},{19,... | collective-permute-start | bytes 12296 | tf_op jit(solution)/shard_map/ppermute | solution.py:38
  268.3 2.9 %collective-permute-start.7 = (bf16[16,6,1]{2,1,0:T(8,128)(2,1)S(1)}, bf16[16,6,1]{2,1,0:T(8,128)(2,1)S(1)}, u32[]{:S(2)}, u32[]{:S(2)}) collective-permute-start(bf16[16,6,1]{2,1,0:T(8,128)(2,1)S(1)} %get-tuple-element.12), channel_id=1, source_target_pairs={{0,2},{2,4},{4,6},{6,8},{8,10},{10,12},{12,14},{1,3},{3,5},{5,7},{... | collective-permute-start | bytes 584 | tf_op jit(solution)/shard_map/ppermute | solution.py:35
  269.6 5.8 %collective-permute-start.8 = (bf16[16,6,1]{2,1,0:T(8,128)(2,1)S(1)}, bf16[16,6,1]{2,1,0:T(8,128)(2,1)S(1)}, u32[]{:S(2)}, u32[]{:S(2)}) collective-permute-start(bf16[16,6,1]{2,1,0:T(8,128)(2,1)S(1)} %get-tuple-element.11), channel_id=1, source_target_pairs={{2,0},{4,2},{6,4},{8,6},{10,8},{12,10},{14,12},{3,1},{5,3},{7,5},{... | collective-permute-start | bytes 584 | tf_op jit(solution)/shard_map/ppermute | solution.py:38
Sparse Core Ops, SparseCore 0:
  14.9 138.7 all-gather.1
  222.9 10.9 reduce-scatter.1
where the time goes:
time: 285 us; the launch traced here: 284 us
  waiting for transfers between devices  146 us (51%)
  matrix products  55.3 us (19%)
  local copies, waits for them, and re-layouts  28.5 us (10%)
  starting transfers between devices  18.3 us (6%)
  other arithmetic  16.8 us (6%)
  between operations  15.8 us (6%)
  blocking collectives  3.79 us (1%)
    all_gather x1, waiting for transfers between devices, shards(): lax.all_gather(weight_half, 'width', axis=0, tiled=True)  115 us
    dot_general x1, matrix products, shards(): jnp.dot(both_rows, lax.all_gather(weight_half, 'width', axis=0, tiled=Tru...  23 us
    ppermute x4, waiting for transfers between devices, from_behind(): return lax.ppermute(x, axis, [(i, (i + by) % peers) for i in range(peers)])  13.3 us
    dot_general x1, local copies, waits for them, and re-layouts, shards(): jnp.dot(both_rows, lax.all_gather(weight_half, 'width', axis=0, tiled=Tru...  13.3 us
    ppermute x4, starting transfers between devices, from_behind(): return lax.ppermute(x, axis, [(i, (i + by) % peers) for i in range(peers)])  13.1 us
    sub x1, matrix products, attend(): weights = jax.nn.softmax(scores, axis=-1).astype(jnp.bfloat16)  13 us
    reduce_scatter x1, waiting for transfers between devices, shards(): lax.psum_scatter(partial_value.astype(jnp.bfloat16), 'guide', scatter_dim...  11.1 us
    dot_general x1, matrix products, attend(): jnp.einsum('bhqk,bkhe->bqhe', weights, value_rows, preferred_element_type...  9.84 us
  transfers between devices with their start and end apart: 11, of which 9 were waited for; matrix products, arithmetic and copies ran while one was open for 8% of the time, Pallas kernels for 0%

commit v1 on v0

v1 whole, which is shorter than its diff:
```python
import functools

import jax
import jax.numpy as jnp
from jax import lax
from jax.experimental import pallas as pl
from jax.experimental.pallas import tpu as pltpu
from jax.sharding import PartitionSpec as P

HEADS = 20
HEAD = 64
STEPS = 28
LANES = 128
ROWS = 72

guidance = 4.0
epsilon = 1e-06

bf16 = jnp.bfloat16
f32 = jnp.float32
PARTS = (0, 2, 1)
LOG2E = 1.4426950408889634


def dot(a, b, dims=((1,), (0,))):
    return lax.dot_general(a, b, (dims, ((), ())), preferred_element_type=f32)


def call(body, outs, scratch=(), anys=(), smem=(), count=0, limit=56):
    def spec(i):
        if i in anys:
            return pl.BlockSpec(memory_space=pl.ANY)
        if i in smem:
            return pl.BlockSpec(memory_space=pltpu.SMEM)
        return pl.BlockSpec(memory_space=pltpu.VMEM)

    return pl.pallas_call(
        body,
        out_shape=tuple(jax.ShapeDtypeStruct(s, t) for s, t in outs),
        in_specs=[spec(i) for i in range(count)],
        out_specs=tuple(pl.BlockSpec(memory_space=pltpu.VMEM) for _ in outs),
        scratch_shapes=list(scratch),
        compiler_params=pltpu.CompilerParams(vmem_limit_bytes=limit << 20),
    )


def iota(shape, dim):
    return lax.broadcasted_iota(jnp.int32, shape, dim)


def split(values):
    high = values.astype(bf16)
    return high, (values - high.astype(f32)).astype(bf16)


def partial_kernel(place_ref, a_ref, w_ref, out_ref, w_buf, sems, *, width, slots, local_pairs, features):
    group = place_ref[0]
    span = local_pairs * LANES
    copies = []
    for part in range(3):
        start = pl.multiple_of(part * features + group * span, LANES)
        copies.append(
            pltpu.make_async_copy(w_ref.at[:, pl.ds(start, span)], w_buf.at[part], sems.at[part])
        )
    for one in copies:
        one.start()
    for one in copies:
        one.wait()
    a = a_ref[...]
    for owner in range(width):
        for slot in range(slots):
            tile = owner * slots + slot
            if tile < 3 * local_pairs:
                pair, sub = divmod(tile, 3)
                both = dot(a, w_buf[PARTS[sub], :, pair * LANES : (pair + 1) * LANES])
                value = (both[:ROWS] + both[ROWS:]).astype(bf16)
            else:
                value = jnp.zeros((ROWS, LANES), bf16)
            out_ref[owner, :, slot * LANES : (slot + 1) * LANES] = value


def sum_kernel(parts_ref, out_ref, *, width):
    total = parts_ref[0].astype(f32)
    for i in range(1, width):
        total = total + parts_ref[i].astype(f32)
    out_ref[...] = total.astype(bf16)


def window_kernel(
    place_ref, own_ref, right_ref, left_ref, further_ref, w_ref,
    x_ref, xt_ref, var_ref, varrow_ref, lat_ref, count_ref,
    rows_buf, xt_buf, hid_buf,
):
    channels, height, columns = own_ref.shape[0] - 1, own_ref.shape[1], own_ref.shape[2]
    offset = place_ref[1]
    guide = place_ref[2]
    near = height // 2 + 1
    lane = iota((channels, LANES), 1)
    for r in range(height):
        at = slice(r * channels, (r + 1) * channels)
        rows_buf[at, :columns] = own_ref[:channels, r, :].astype(bf16)
        rows_buf[at, columns : 2 * columns] = right_ref[:channels, r, :].astype(bf16)
        rows_buf[at, 2 * columns :] = further_ref[:, r, :]
    col = iota((3 * columns, 2 * columns), 0)
    spot = iota((3 * columns, 2 * columns), 1)
    b = (spot >= columns).astype(jnp.int32)
    pick = jnp.where(col == offset + 2 * (spot - b * columns) + b, 1.0, 0.0).astype(bf16)
    placed = dot(rows_buf[...], pick).astype(bf16)
    tokens = height // 2 * columns
    for p in range(height // 2):
        for a in range(2):
            for b in range(2):
                f = (a * 2 + b) * channels
                xt_buf[f : f + channels, p * columns : (p + 1) * columns] = placed[
                    (2 * p + a) * channels : (2 * p + a + 1) * channels, b * columns : (b + 1) * columns
                ].astype(f32)
    feats = 4 * channels
    xt = xt_buf[:feats, :]
    xpad = jnp.concatenate([xt, jnp.zeros((LANES - feats, tokens), f32)], axis=0)
    xrow = xpad.T
    model = w_ref.shape[1]
    block = 64
    x_bf = xrow[:, :feats].astype(bf16)
    hid_buf[...] = dot(x_bf, w_ref[...])

    def stats(i, carry):
        at = pl.ds(pl.multiple_of(i * block, block), block)
        h = hid_buf[at, :]
        mean = jnp.sum(h, axis=1, keepdims=True) * (1.0 / model)
        c = h - mean
        v = jnp.sum(c * c, axis=1, keepdims=True) * (1.0 / model)
        var_ref[at, :] = jnp.broadcast_to(v, (block, LANES))
        return carry

    lax.fori_loop(0, tokens // block, stats, 0)
    var = var_ref[...]
    std_hi, std_lo = split(jnp.sqrt(var + epsilon))
    spots = iota((tokens, LANES), 1)
    x_ref[...] = jnp.where(
        spots == feats, std_hi.astype(f32), jnp.where(spots == feats + 1, std_lo.astype(f32), xrow)
    ).astype(bf16)
    var_t = var.T[:8]
    varrow_ref[...] = var_t
    hi_t, lo_t = split(jnp.sqrt(var_t + epsilon))
    down = iota((8, tokens), 0)
    tail = jnp.where(down == 0, hi_t.astype(f32), jnp.where(down == 1, lo_t.astype(f32), 0.0))
    xt_ref[...] = jnp.concatenate([xt, tail], axis=0).astype(bf16)
    first = guide * (near - 2)
    for i in range(near):
        r = pl.ds(first + i, 1)
        lat_ref[i, :, :columns] = own_ref[:channels, r, :].reshape(channels, columns)
        before = pltpu.roll(left_ref[:channels, r, :].reshape(channels, columns), 1, 1)
        after = pltpu.roll(right_ref[:channels, r, :].reshape(channels, columns), 1, 1)
        lat_ref[i, :, columns:] = jnp.where(lane == 0, before, jnp.where(lane == 1, after, 0.0))
    lane8 = iota((height, LANES), 1)
    count_ref[:, :columns] = own_ref[channels]
    before = pltpu.roll(left_ref[channels], 1, 1)
    after = pltpu.roll(right_ref[channels], 1, 1)
    count_ref[:, columns:] = jnp.where(lane8 == 0, before, jnp.where(lane8 == 1, after, 1.0))


def attend_pairs(m_ref, x_ref, xt_ref, var_ref, varrow_ref, att_ref, slots, pairs):
    tokens = x_ref.shape[0]
    x = x_ref[:, :ROWS]
    xt = xt_ref[...]
    var = var_ref[...]
    eps_col = epsilon * (var + epsilon)
    rstd = lax.rsqrt(var + epsilon)
    eps_row = epsilon * (varrow_ref[:1, :] + epsilon)
    low = iota((tokens, LANES), 1) < HEAD
    scale = LOG2E * HEAD**-0.5

    def tile(t):
        slot = t % slots
        return m_ref[t // slots, :, slot * LANES : (slot + 1) * LANES]

    for pair in range(pairs):
        mq, mv, mk = (tile(3 * pair + sub) for sub in range(3))
        both = dot(x, jnp.concatenate([mq, mv], axis=1))
        uq = both[:, :LANES]
        uv = both[:, LANES:] * rstd
        uk = dot(mk, xt, ((0,), (0,)))
        sq = uq * uq
        sum_low = jnp.sum(jnp.where(low, sq, 0.0), axis=1, keepdims=True)
        sum_high = jnp.sum(jnp.where(low, 0.0, sq), axis=1, keepdims=True)
        q = uq * lax.rsqrt(jnp.where(low, sum_low, sum_high) * (1.0 / HEAD) + eps_col)
        keys = []
        for half in range(2):
            k = uk[half * HEAD : (half + 1) * HEAD]
            mean = jnp.sum(k * k, axis=0, keepdims=True) * (1.0 / HEAD)
            keys.append((k * lax.rsqrt(mean + eps_row)).astype(bf16))
        kt = jnp.concatenate(keys, axis=0)
        outs = []
        for half in range(2):
            mine = low if half == 0 else jnp.logical_not(low)
            qh = jnp.where(mine, q, 0.0).astype(bf16)
            vh = jnp.where(mine, uv, 1.0).astype(bf16)
            weights = jnp.exp2(dot(qh, kt) * scale).astype(bf16)
            outs.append(dot(weights, vh))
        top = jnp.where(low, outs[0], outs[1])
        sums = pltpu.roll(jnp.where(low, outs[1], outs[0]), HEAD, 1)
        att_ref[:, pair * LANES : (pair + 1) * LANES] = (top / sums).astype(bf16)


def first_kernel(m_ref, x_ref, xt_ref, var_ref, varrow_ref, att_ref, *, slots, pairs):
    attend_pairs(m_ref, x_ref, xt_ref, var_ref, varrow_ref, att_ref, slots, pairs)


def second_kernel(
    place_ref, m_ref, x_ref, xt_ref, var_ref, varrow_ref, att_ref, wp_ref, gate_ref, wf_ref, wo_ref,
    mine_ref, send_ref,
    att_buf, wo_buf, res_buf, fin_buf, sem,
    *, slots, pairs, channels, height, columns, halves,
):
    load = pltpu.make_async_copy(wo_ref, wo_buf, sem.at[0])
    load.start()
    group = place_ref[0]
    guide = place_ref[2]
    attend_pairs(m_ref, x_ref, xt_ref, var_ref, varrow_ref, att_buf, slots, pairs) if halves == 2 else None
    load.wait()
    tokens = x_ref.shape[0]
    feats = wp_ref.shape[0]
    model = wp_ref.shape[1]
    span = pairs * LANES
    x = x_ref[:, :feats]
    first = pl.multiple_of(group * span, LANES) if halves == 2 else 0
    other = pl.multiple_of((1 - group) * span, LANES)
    start = 0
    while start < model:
        size = min(2 * LANES, model - start)
        cols = slice(start, start + size)
        mixed = dot(att_ref[...], wo_buf[pl.ds(first, span), cols])
        if halves == 2:
            mixed = mixed + dot(att_buf[...], wo_buf[pl.ds(other, span), cols])
        res_buf[:, cols] = dot(x, wp_ref[:, cols]) + gate_ref[:, cols] * mixed
        start += size
    block = 32

    def norm(i, carry):
        at = pl.ds(pl.multiple_of(i * block, block), block)
        h = res_buf[at, :]
        mean = jnp.sum(h, axis=1, keepdims=True) * (1.0 / model)
        c = h - mean
        v = jnp.sum(c * c, axis=1, keepdims=True) * (1.0 / model)
        fin_buf[at, :] = (c * lax.rsqrt(v + epsilon)).astype(bf16)
        return carry

    lax.fori_loop(0, tokens // block, norm, 0)
    result = dot(fin_buf[...], wf_ref[...])
    near = height // 2 + 1
    keep = guide * (near - 2)
    give = (1 - guide) * (near - 2)
    for p in range(height // 2):
        turned = result[p * columns : (p + 1) * columns].T
        for a in range(2):
            r = 2 * p + a
            for b in range(2):
                f = (a * 2 + b) * channels
                piece = turned[f : f + channels]

                @pl.when(jnp.logical_and(r >= keep, r < keep + near))
                def _():
                    mine_ref[r - keep, :, b * columns : (b + 1) * columns] = piece

                @pl.when(jnp.logical_and(r >= give, r < give + near))
                def _():
                    send_ref[r - give, :, b * columns : (b + 1) * columns] = piece.astype(bf16)


def spread_kernel(place_ref, mine_ref, theirs_ref, own_ref, one_ref, two_ref, back_ref):
    offset = place_ref[1]
    guide = place_ref[2]
    near, channels, wide = mine_ref.shape
    columns = wide // 2
    mine = mine_ref[...].reshape(near * channels, wide)
    theirs = theirs_ref[...].reshape(near * channels, wide).astype(f32)
    cond = jnp.where(guide == 0, mine, theirs)
    plain = jnp.where(guide == 0, theirs, mine)
    guided = plain + guidance * (cond - plain)
    high, low = split(guided)
    spot = iota((wide, 2 * columns), 0)
    lane = iota((wide, 2 * columns), 1)
    b = (spot >= columns).astype(jnp.int32)
    col = offset + 2 * (spot - b * columns) + b
    target = jnp.where(lane < columns, lane, jnp.where(lane == columns, -1, lane - 1))
    target = jnp.where(lane > columns + 1, -4 * wide, target)

    def place(distance):
        return jnp.where(col == target + distance * columns, 1.0, 0.0).astype(bf16)

    here = place(0)
    own_ref[...] = dot(high, here) + dot(low, here)
    one_ref[...] = dot(high, place(1)).astype(bf16)
    two_ref[...] = dot(high, place(2)).astype(bf16)
    back_ref[...] = dot(high, place(-1)[:, columns:]).astype(bf16)


def decode_kernel(
    place_ref, own_ref, one_ref, two_ref, back_ref, lat_ref, count_ref, w_ref, den_ref, feat_ref, pad_buf,
    *, width,
):
    guide = place_ref[2]
    place = place_ref[3]
    near, channels, wide = lat_ref.shape
    columns = wide // 2
    fraction = (jnp.full((1, wide), place_ref[4], jnp.int32).astype(f32) + 1.0) / STEPS
    sigma = 3.0 * fraction / (1.0 + 2.0 * fraction)
    total = own_ref[...] + one_ref[...].astype(f32) + two_ref[...].astype(f32)
    back = jnp.concatenate([jnp.zeros(back_ref.shape, f32), back_ref[...].astype(f32)], axis=1)
    velocity = (total + back) / count_ref[:1, :]
    clean = lat_ref[...].reshape(near * channels, wide) - sigma * velocity
    half = near - 1
    first = guide
    lane = iota((near * channels, columns), 1)
    main = clean[:, :columns]
    edges = clean[:, columns:]
    left = jnp.where(place == 0, 0.0, edges[:, 0:1])
    right = jnp.where(place == width - 1, 0.0, edges[:, 1:2])
    before = jnp.where(lane == 0, left, pltpu.roll(main, 1, 1))
    after = jnp.where(lane == columns - 1, right, pltpu.roll(main, columns - 1, 1))
    zero = jnp.zeros((channels, columns), f32)
    for b, value in enumerate((before, main, after)):
        pad_buf[b, 0] = zero
        pad_buf[b, near + 1] = zero
        for i in range(near):
            pad_buf[b, i + 1] = value[i * channels : (i + 1) * channels]
    for r in range(half):
        at = first + r
        den_ref[:, r, :] = pad_buf[1, at + 1]
        stacked = jnp.concatenate(
            [pad_buf[b, at + a] for a in range(3) for b in range(3)], axis=0
        ).astype(bf16)
        summed = dot(stacked, w_ref[...], ((0,), (0,)))
        feat_ref[r] = (summed / (1.0 + jnp.exp(-summed))).astype(bf16)


def shift(x, by):
    peers = lax.axis_size("width")
    return lax.ppermute(x, "width", [(i, (i + by) % peers) for i in range(peers)])


def swap(x, axis):
    return lax.ppermute(x, axis, [(0, 1), (1, 0)])


def shards(latent, starts, counts, step_index, cond_mod, w_patch, w_qkv, w_out, w_final, w_dec):
    guide = lax.axis_index("guide")
    place = lax.axis_index("width")
    group = lax.axis_index("groups")
    width = lax.axis_size("width")
    channels, height, columns = latent.shape
    model = w_patch.shape[1]
    feats = w_patch.shape[0]
    features = HEADS * HEAD
    pairs = features // LANES
    halves = 2 if lax.axis_size("groups") == 2 and pairs % 2 == 0 else 1
    local_pairs = pairs // halves
    slots = -(-3 * local_pairs // width)
    if halves == 1:
        group = group * 0
    rows = w_qkv.shape[0]
    modulation = cond_mod[0]
    offset = starts[0] - place * columns
    scalars = jnp.stack([group, offset, guide, place, step_index[0]]).astype(jnp.int32)

    pack = jnp.concatenate(
        [latent, jnp.broadcast_to(counts.astype(f32)[None, None, :], (1, height, columns))], axis=0
    )
    right = shift(pack, -1)
    further = shift(latent.astype(bf16), -2)
    left = shift(pack, 1)

    wide = w_patch.astype(f32)
    centered = wide - jnp.mean(wide, axis=1, keepdims=True)
    mine = lax.dynamic_slice_in_dim(centered, place * rows, rows, 1)
    own_mod = lax.dynamic_slice_in_dim(modulation, place * rows, rows, 1)
    shift_rows = jnp.concatenate([own_mod[0:1]] * 2 + [jnp.zeros((ROWS - feats - 2, rows), f32)])
    stacked = jnp.concatenate([mine * (1.0 + own_mod[1:2]), shift_rows])
    a = jnp.concatenate(split(stacked), axis=0)

    (parts,) = call(
        functools.partial(
            partial_kernel, width=width, slots=slots, local_pairs=local_pairs, features=features
        ),
        [((width, ROWS, slots * LANES), bf16)],
        scratch=[
            pltpu.VMEM((3, rows, local_pairs * LANES), bf16),
            pltpu.SemaphoreType.DMA((3,)),
        ],
        anys=(2,), smem=(0,), count=3,
    )(scalars, a, w_qkv)
    parts = lax.all_to_all(parts, "width", 0, 0, tiled=True)
    (chunk,) = call(
        functools.partial(sum_kernel, width=width), [((ROWS, slots * LANES), bf16)], count=1
    )(parts)
    near = height // 2 + 1
    tokens = height // 2 * columns
    x, xt, var, varrow, lat, count = call(
        window_kernel,
        [
            ((tokens, LANES), bf16), ((ROWS, tokens), bf16), ((tokens, LANES), f32),
            ((8, tokens), f32), ((near, channels, 2 * columns), f32), ((height, 2 * columns), f32),
        ],
        scratch=[
            pltpu.VMEM((height * channels, 3 * columns), bf16),
            pltpu.VMEM((feats, tokens), f32),
            pltpu.VMEM((tokens, model), f32),
        ],
        smem=(0,), count=6,
    )(scalars, pack, right, left, further, w_patch)
    half = lax.all_to_all(
        jnp.broadcast_to(chunk[None], (width,) + chunk.shape), "width", 0, 0, tiled=True
    )
    other = swap(half, "groups") if halves == 2 else half
    (att,) = call(
        functools.partial(first_kernel, slots=slots, pairs=local_pairs),
        [((tokens, local_pairs * LANES), bf16)],
        count=5,
    )(half, x, xt, var, varrow)
    mine_v, send_v = call(
        functools.partial(
            second_kernel, slots=slots, pairs=local_pairs, channels=channels, height=height,
            columns=columns, halves=halves,
        ),
        [((near, channels, 2 * columns), f32), ((near, channels, 2 * columns), bf16)],
        scratch=[
            pltpu.VMEM((tokens, local_pairs * LANES), bf16),
            pltpu.VMEM(w_out.shape, bf16),
            pltpu.VMEM((tokens, model), f32),
            pltpu.VMEM((tokens, model), bf16),
            pltpu.SemaphoreType.DMA((1,)),
        ],
        anys=(10,), smem=(0,), count=11,
    )(scalars, other, x, xt, var, varrow, att, w_patch, modulation[2:3], w_final, w_out)
    theirs = swap(send_v, "guide")
    flat = near * channels
    own, one, two, back = call(
        spread_kernel,
        [
            ((flat, 2 * columns), f32), ((flat, 2 * columns), bf16),
            ((flat, 2 * columns), bf16), ((flat, columns), bf16),
        ],
        smem=(0,), count=3,
    )(scalars, mine_v, theirs)
    one = shift(one, 1)
    two = shift(two, 2)
    back = shift(back, -1)
    return call(
        functools.partial(decode_kernel, width=width),
        [((channels, height // 2, columns), f32), ((height // 2, columns, w_dec.shape[1]), bf16)],
        scratch=[pltpu.VMEM((3, near + 2, channels, columns), f32)],
        smem=(0,), count=8,
    )(scalars, own, one, two, back, lat, count, w_dec)


def solution(mesh):
    return jax.shard_map(
        shards,
        mesh=mesh,
        in_specs=(
            P(None, None, ("groups", "width")),
            P(("groups", "width")),
            P(("groups", "width")),
            P("groups"),
            P("guide", None, None),
            P(),
            P("width", None),
            P(),
            P(),
            P(),
        ),
        out_specs=(P(None, "guide", ("groups", "width")), P("guide", ("groups", "width"), None)),
        check_vma=False,
    )
```

time: 285 us -> 97.8 us (0.34)
  waiting for transfers between devices: 146 us -> 7.58 us
  matrix products: 55.3 us -> 0 us
  Pallas kernels: 0 us -> 41.3 us
  local copies, waits for them, and re-layouts: 28.5 us -> 7.76 us
  blocking collectives: 3.79 us -> 17.8 us
  between operations: 15.8 us -> 2.13 us
  other arithmetic: 16.8 us -> 3.9 us
    all_gather x1 -> x0, waiting for transfers between devices: 115 us -> none  [shards(): lax.all_gather(weight_half, 'width', axis=0, tiled=True)]
    dot_general x6 -> x0, matrix products: 42.3 us -> none  [the longest x1 23 us: shards(): jnp.dot(both_rows, lax.all_gather(weight_half, 'width', axis=0, tiled=Tru...]
    pallas_call x0 -> x7, Pallas kernels: none -> 41.3 us  [the longest x1 20.2 us: shards(): call(functools.partial(second_kernel, slots=slots, pairs=local_pairs, cha...]
    ppermute x9 -> x8, waiting for transfers between devices: 19.4 us -> 3.44 us  [the longest x6 2.02 us: shift(): lax.ppermute(x, 'width', [(i, (i + by) % peers) for i in range(peers)])]
    all_to_all x1, blocking collectives: 3.79 us -> 17.8 us  [shards(): parts = lax.all_to_all(parts, 'width', 0, 0, tiled=True)]
    dot_general x1 -> x0, local copies, waits for them, and re-layouts: 13.3 us -> none  [shards(): jnp.dot(both_rows, lax.all_gather(weight_half, 'width', axis=0, tiled=Tru...]
    sub x1 -> x0, matrix products: 13 us -> none  [attend(): weights = jax.nn.softmax(scores, axis=-1).astype(jnp.bfloat16)]
    reduce_scatter x1 -> x0, waiting for transfers between devices: 11.1 us -> none  [shards(): lax.psum_scatter(partial_value.astype(jnp.bfloat16), 'guide', scatter_dim...]
  transfers between devices with their start and end apart: 11 -> 9, of which waited for: 9 -> 4; matrix products, arithmetic and copies ran while one was open for 8% -> 2% of each run, Pallas kernels for 0% -> 12%
where the time goes in v1:
time: 97.8 us; the launch traced here: 97 us
  Pallas kernels  41.3 us (42%)
  blocking collectives  17.8 us (18%)
  starting transfers between devices  16.6 us (17%)
  local copies, waits for them, and re-layouts  7.76 us (8%)
  waiting for transfers between devices  7.58 us (8%)
  other arithmetic  3.9 us (4%)
  between operations  2.13 us (2%)
    pallas_call x1, Pallas kernels, shards(): call(functools.partial(second_kernel, slots=slots, pairs=local_pairs, cha...  20.2 us
    all_to_all x1, blocking collectives, shards(): parts = lax.all_to_all(parts, 'width', 0, 0, tiled=True)  17.8 us
    ppermute x6, starting transfers between devices, shift(): lax.ppermute(x, 'width', [(i, (i + by) % peers) for i in range(peers)])  11.6 us
    pallas_call x1, Pallas kernels, shards(): call(functools.partial(first_kernel, slots=slots, pairs=local_pairs), [((...  6.32 us
    pallas_call x1, Pallas kernels, shards(): call(window_kernel, [((tokens, LANES), bf16), ((ROWS, tokens), bf16), ((t...  5.36 us
    unnamed x27, local copies, waits for them, and re-layouts  4.28 us
    all_to_all x1, waiting for transfers between devices, shards(): lax.all_to_all(jnp.broadcast_to(chunk[None], (width,) + chunk.shape), 'wi...  4.14 us
    pallas_call x1, Pallas kernels, shards(): call(functools.partial(partial_kernel, width=width, slots=slots, local_pa...  3.59 us
  transfers between devices with their start and end apart: 9, of which 4 were waited for; matrix products, arithmetic and copies ran while one was open for 2% of the time, Pallas kernels for 12%

profile of v1, /device:TPU:0, one launch (start us, length us, event | category | flops | bytes accessed | tf_op | source)
XLA Modules:
  0.0 97.0 jit_solution(1806611809329929522)
XLA Ops:
  0.6 0.0 copy-start.12
  0.7 1.1 %convert_element_type.18 = f32[64,2432]{1,0:T(8,128)S(1)} convert(bf16[64,2432]{1,0:T(8,128)(2,1)} %wp_ref.1) | non-fusion elementwise | flops 155648 | bytes 933888 | tf_op jit(solution)/shard_map/convert_element_type | solution.py:373
  1.7 1.1 %convert_reduce_fusion = f32[64]{0:T(128)S(1)} fusion(bf16[64,2432]{1,0:T(8,128)(2,1)} %wp_ref.1), kind=kLoop, calls=%fused_computation | loop fusion | flops 311232 | bytes 311552 | tf_op jit(solution)/shard_map/reduce_sum | solution.py:374
  2.9 0.1 pad.7.clone
  2.9 0.8 fusion.2
  3.7 0.1 fusion
  3.8 0.1 fusion.1
  3.9 0.1 subtract_convert_fusion
  5.3 0.7 pad_maximum_fusion.a_ref
  6.0 0.6 stack.19.place_ref
  6.6 3.6 %shard_map.113 = bf16[8,72,256]{2,1,0:T(8,128)(2,1)} custom-call(s32[5]{0:T(128)} %stack.19.place_ref, bf16[144,304]{1,0:T(8,128)(2,1)} %pad_maximum_fusion.a_ref, bf16[304,3840]{1,0:T(8,128)(2,1)} %w_ref.3), custom_call_target="tpu_custom_call" | custom-call | tf_op jit(solution)/shard_map/pallas_call | solution.py:381
  10.2 17.8 %all_to_all.10.parts_ref = bf16[8,72,256]{2,1,0:T(8,128)(2,1)} all-to-all(bf16[8,72,256]{2,1,0:T(8,128)(2,1)} %shard_map.113), channel_id=1, replica_groups=mesh['groups'=2,'width'=8,'guide'=2] {'width'}, dimensions={0} | all-to-all | bytes 589824 | tf_op jit(solution)/shard_map/all_to_all | solution.py:392
  27.9 1.6 %shard_map.114 = bf16[72,256]{1,0:T(8,128)(2,1)} custom-call(bf16[8,72,256]{2,1,0:T(8,128)(2,1)} %all_to_all.10.parts_ref), custom_call_target="tpu_custom_call" | custom-call | tf_op jit(solution)/shard_map/pallas_call | solution.py:393
  29.6 1.5 %broadcast_in_dim.7 = bf16[8,72,256]{2,1,0:T(8,128)(2,1)} broadcast(bf16[72,256]{1,0:T(8,128)(2,1)} %shard_map.114), dimensions={1,2} | broadcast | bytes 331776 | tf_op jit(solution)/shard_map/broadcast_in_dim | solution.py:412
  31.1 3.4 %all-to-all-start.1 = ((bf16[8,72,256]{2,1,0:T(8,128)(2,1)}), bf16[8,72,256]{2,1,0:T(8,128)(2,1)S(1)}, u32[]{:S(2)}, u32[]{:S(2)}) async-start(bf16[8,72,256]{2,1,0:T(8,128)(2,1)} %broadcast_in_dim.7), calls=%async_computation.1 | async-start | bytes 589824 | tf_op jit(solution)/shard_map/all_to_all | solution.py:411
  34.5 4.7 %collective-permute-start.1 = (f32[17,8,128]{2,1,0:T(8,128)S(1)}, f32[17,8,128]{2,1,0:T(8,128)S(1)}, u32[]{:S(2)}, u32[]{:S(2)}) collective-permute-start(f32[17,8,128]{2,1,0:T(8,128)S(1)} %pad_maximum_fusion.1.own_ref), channel_id=1, source_target_pairs={{0,14},{2,0},{4,2},{6,4},{8,6},{10,8},{12,10},{14,12},{1,15},{3,1}... | collective-permute-start | bytes 208904 | tf_op jit(solution)/shard_map/ppermute | solution.py:339
  39.2 0.0 collective-permute-start.2
  39.3 1.1 %collective-permute-start.3 = (bf16[16,8,128]{2,1,0:T(8,128)(2,1)S(1)}, bf16[16,8,128]{2,1,0:T(8,128)(2,1)S(1)}, u32[]{:S(2)}, u32[]{:S(2)}) collective-permute-start(bf16[16,8,128]{2,1,0:T(8,128)(2,1)S(1)} %convert_element_type.23), channel_id=1, source_target_pairs={{0,12},{2,14},{4,0},{6,2},{8,4},{10,6},{12,8},{14,10},{1,13},{3,15... | collective-permute-start | bytes 98312 | tf_op jit(solution)/shard_map/ppermute | solution.py:339
  40.4 4.1 %all-to-all-done.1.m_ref = bf16[8,72,256]{2,1,0:T(8,128)(2,1)S(1)} async-done(((bf16[8,72,256]{2,1,0:T(8,128)(2,1)}), bf16[8,72,256]{2,1,0:T(8,128)(2,1)S(1)}, u32[]{:S(2)}, u32[]{:S(2)}) %all-to-all-start.1) | async-done | bytes 294944 | tf_op jit(solution)/shard_map/all_to_all | solution.py:411
  44.5 1.5 %collective-permute-start = (bf16[8,72,256]{2,1,0:T(8,128)(2,1)S(1)}, bf16[8,72,256]{2,1,0:T(8,128)(2,1)S(1)}, u32[]{:S(2)}, u32[]{:S(2)}) collective-permute-start(bf16[8,72,256]{2,1,0:T(8,128)(2,1)S(1)} %all-to-all-done.1.m_ref), channel_id=1, source_target_pairs={{0,16},{16,0},{1,17},{17,1},{2,18},{18,2},{3,19},{19,3},{4,20},{20... | collective-permute-start | bytes 884744 | tf_op jit(solution)/shard_map/ppermute | solution.py:343
  46.0 1.3 %slice_bitcast_fusion.gate_ref = f32[1,2432]{1,0:T(1,128)} fusion(f32[1,3,2432]{2,0,1:T(1,128)} %param.14), kind=kLoop, calls=%fused_computation.8 | loop fusion | bytes 19456 | tf_op jit(solution)/shard_map/slice | solution.py:434
  47.3 1.1 %copy.12.wf_ref = bf16[2432,64]{1,0:T(8,128)(2,1)} copy(bf16[2432,64]{0,1:T(8,128)(2,1)S(1)} %copy-done.1) | data formatting | bytes 622592 | tf_op args[8]
  48.4 0.0 collective-permute-done.3.further_ref
  48.4 0.0 collective-permute-done.1.right_ref
  48.4 0.0 copy-start.5
  48.4 0.0 collective-permute-done.2.left_ref
  48.4 0.6 copy-done.10
  49.0 0.0 copy-done.5
  49.0 0.6 copy-done.6
  49.7 5.4 %shard_map.115 = (bf16[512,128]{1,0:T(8,128)(2,1)}, bf16[72,512]{1,0:T(8,128)(2,1)}, f32[512,128]{1,0:T(8,128)}, f32[8,512]{1,0:T(8,128)}, f32[5,16,256]{2,1,0:T(8,128)}, /*index=5*/f32[8,256]{1,0:T(8,128)}) custom-call(s32[5]{0:T(128)} %stack.19.place_ref, f32[17,8,128]{2,1,0:T(8,128)} %copy-done.3, f32[17,8,128]{2,1,0:T(8,128)} %copy-done.5, ...), custom_call_target="tpu_custom_call" | custom-call | tf_op jit(solution)/shard_map/pallas_call | solution.py:398
  55.0 6.3 %shard_map.116.att_ref = bf16[512,640]{1,0:T(8,128)(2,1)} custom-call(bf16[8,72,256]{2,1,0:T(8,128)(2,1)} %copy-done, bf16[512,128]{1,0:T(8,128)(2,1)} %get-tuple-element.14.x_ref, bf16[72,512]{1,0:T(8,128)(2,1)} %get-tuple-element.15.xt_ref, f32[512,128]{1,0:T(8,128)} %get-tuple-element.16.var_ref, f32[8,512]{1,0:T(8,128)} %get-tuple-element.17.varrow_ref), custom_call_target="tpu_custom_call" | custom-call | tf_op jit(solution)/shard_map/pallas_call | solution.py:415
  61.3 0.0 collective-permute-done.m_ref
  61.3 0.7 copy-done.2
  62.0 20.2 %shard_map.117 = (f32[5,16,256]{2,1,0:T(8,128)}, bf16[5,16,256]{2,1,0:T(8,128)(2,1)}) custom-call(s32[5]{0:T(128)} %stack.19.place_ref, bf16[8,72,256]{2,1,0:T(8,128)(2,1)} %copy-done.2, bf16[512,128]{1,0:T(8,128)(2,1)} %get-tuple-element.14.x_ref, bf16[72,512]{1,0:T(8,128)(2,1)} %get-tuple-element.15.xt_ref, f32[512,128]{1,0:T(8,128)} %get-tuple-element.16.var_ref, ...), custom_call_target="tpu_custom_call" | custom-call | tf_op jit(solution)/shard_map/pallas_call | solution.py:420
  82.2 0.1 collective-permute-start.4
  82.3 1.4 %collective-permute-done.4.theirs_ref = bf16[5,16,256]{2,1,0:T(8,128)(2,1)S(1)} collective-permute-done((bf16[5,16,256]{2,1,0:T(8,128)(2,1)}, bf16[5,16,256]{2,1,0:T(8,128)(2,1)S(1)}, u32[]{:S(2)}, u32[]{:S(2)}) %collective-permute-start.4) | collective-permute-done | bytes 40992 | tf_op jit(solution)/shard_map/ppermute | solution.py:343
  83.7 0.6 copy-done.9
  84.3 1.8 %shard_map.118 = (f32[80,256]{1,0:T(8,128)}, bf16[80,256]{1,0:T(8,128)(2,1)}, bf16[80,256]{1,0:T(8,128)(2,1)}, bf16[80,128]{1,0:T(8,128)(2,1)}) custom-call(s32[5]{0:T(128)} %stack.19.place_ref, f32[5,16,256]{2,1,0:T(8,128)} %get-tuple-element.18.mine_ref, bf16[5,16,256]{2,1,0:T(8,128)(2,1)} %copy-done.9), custom_call_target="tpu_custom_call" | custom-call | tf_op jit(solution)/shard_map/pallas_call | solution.py:437
  86.1 1.5 %collective-permute-start.5 = (bf16[80,256]{1,0:T(8,128)(2,1)}, bf16[80,256]{1,0:T(8,128)(2,1)S(1)}, u32[]{:S(2)}, u32[]{:S(2)}) collective-permute-start(bf16[80,256]{1,0:T(8,128)(2,1)} %get-tuple-element.21), channel_id=1, source_target_pairs={{0,2},{2,4},{4,6},{6,8},{8,10},{10,12},{12,14},{14,0},{1,3},{3,5},... | collective-permute-start | bytes 122888 | tf_op jit(solution)/shard_map/ppermute | solution.py:339
  87.6 0.0 collective-permute-start.6
  87.6 4.3 %collective-permute-start.7 = (bf16[80,128]{1,0:T(8,128)(2,1)}, bf16[80,128]{1,0:T(8,128)(2,1)S(1)}, u32[]{:S(2)}, u32[]{:S(2)}) collective-permute-start(bf16[80,128]{1,0:T(8,128)(2,1)} %get-tuple-element.23), channel_id=1, source_target_pairs={{0,14},{2,0},{4,2},{6,4},{8,6},{10,8},{12,10},{14,12},{1,15},{3,1}... | collective-permute-start | bytes 61448 | tf_op jit(solution)/shard_map/ppermute | solution.py:339
  91.9 1.7 %collective-permute-done.7.back_ref = bf16[80,128]{1,0:T(8,128)(2,1)S(1)} collective-permute-done((bf16[80,128]{1,0:T(8,128)(2,1)}, bf16[80,128]{1,0:T(8,128)(2,1)S(1)}, u32[]{:S(2)}, u32[]{:S(2)}) %collective-permute-start.7) | collective-permute-done | bytes 20512 | tf_op jit(solution)/shard_map/ppermute | solution.py:339
  93.6 0.0 collective-permute-done.5.one_ref
  93.6 0.3 collective-permute-done.6.two_ref
  93.9 0.3 copy-done.11
  94.2 0.0 copy-done.7
  94.2 0.3 copy-done.8
  94.6 2.5 %shard_map.119 = (f32[16,4,128]{2,1,0:T(4,128)}, bf16[4,128,512]{2,1,0:T(8,128)(2,1)}) custom-call(s32[5]{0:T(128)} %stack.19.place_ref, f32[80,256]{1,0:T(8,128)} %get-tuple-element.20.own_ref, bf16[80,256]{1,0:T(8,128)(2,1)} %copy-done.7, bf16[80,256]{1,0:T(8,128)(2,1)} %copy-done.8, bf16[80,128]{1,0:T(8,128)(2,1)} %copy-done.11, ...), custom_call_target="tpu_custom_call" | custom-call | tf_op jit(solution)/shard_map/pallas_call | solution.py:448
  (22 shorter events, 0.1 us)
Async XLA Ops:
  0.6 33.9 %copy-start.12 = (s32[128]{0:T(128)S(1)}, s32[128]{0:T(128)}, u32[]{:S(2)}) copy-start(s32[128]{0:T(128)} %param.12) | copy-start | bytes 1540
  0.6 33.9 %copy-start.4 = (f32[16,8,128]{2,1,0:T(8,128)S(1)}, f32[16,8,128]{2,1,0:T(8,128)}, u32[]{:S(2)}) copy-start(f32[16,8,128]{2,1,0:T(8,128)} %param.10) | copy-start | bytes 196612
  0.6 46.6 %copy-start.1 = (bf16[2432,64]{0,1:T(8,128)(2,1)S(1)}, bf16[2432,64]{0,1:T(8,128)(2,1)}, u32[]{:S(2)}) copy-start(bf16[2432,64]{0,1:T(8,128)(2,1)} %param.18) | copy-start | bytes 933892
  31.1 13.5 %all-to-all-start.1 = ((bf16[8,72,256]{2,1,0:T(8,128)(2,1)}), bf16[8,72,256]{2,1,0:T(8,128)(2,1)S(1)}, u32[]{:S(2)}, u32[]{:S(2)}) async-start(bf16[8,72,256]{2,1,0:T(8,128)(2,1)} %broadcast_in_dim.7), calls=%async_computation.1 | async-start | bytes 589824 | tf_op jit(solution)/shard_map/all_to_all | solution.py:411
  34.5 13.9 %copy-start.3 = (f32[17,8,128]{2,1,0:T(8,128)}, f32[17,8,128]{2,1,0:T(8,128)S(1)}, u32[]{:S(2)}) copy-start(f32[17,8,128]{2,1,0:T(8,128)S(1)} %pad_maximum_fusion.1.own_ref) | copy-start | bytes 208900
  34.5 13.8 %collective-permute-start.1 = (f32[17,8,128]{2,1,0:T(8,128)S(1)}, f32[17,8,128]{2,1,0:T(8,128)S(1)}, u32[]{:S(2)}, u32[]{:S(2)}) collective-permute-start(f32[17,8,128]{2,1,0:T(8,128)S(1)} %pad_maximum_fusion.1.own_ref), channel_id=1, source_target_pairs={{0,14},{2,0},{4,2},{6,4},{8,6},{10,8},{12,10},{14,12},{1,15},{3,1}... | collective-permute-start | bytes 208904 | tf_op jit(solution)/shard_map/ppermute | solution.py:339
  39.2 9.2 %collective-permute-start.2 = (f32[17,8,128]{2,1,0:T(8,128)S(1)}, f32[17,8,128]{2,1,0:T(8,128)S(1)}, u32[]{:S(2)}, u32[]{:S(2)}) collective-permute-start(f32[17,8,128]{2,1,0:T(8,128)S(1)} %pad_maximum_fusion.1.own_ref), channel_id=1, source_target_pairs={{0,2},{2,4},{4,6},{6,8},{8,10},{10,12},{12,14},{14,0},{1,3},{3,5},... | collective-permute-start | bytes 208904 | tf_op jit(solution)/shard_map/ppermute | solution.py:339
  39.3 9.1 %collective-permute-start.3 = (bf16[16,8,128]{2,1,0:T(8,128)(2,1)S(1)}, bf16[16,8,128]{2,1,0:T(8,128)(2,1)S(1)}, u32[]{:S(2)}, u32[]{:S(2)}) collective-permute-start(bf16[16,8,128]{2,1,0:T(8,128)(2,1)S(1)} %convert_element_type.23), channel_id=1, source_target_pairs={{0,12},{2,14},{4,0},{6,2},{8,4},{10,6},{12,8},{14,10},{1,13},{3,15... | collective-permute-start | bytes 98312 | tf_op jit(solution)/shard_map/ppermute | solution.py:339
  44.5 10.5 %copy-start = (bf16[8,72,256]{2,1,0:T(8,128)(2,1)}, bf16[8,72,256]{2,1,0:T(8,128)(2,1)S(1)}, u32[]{:S(2)}) copy-start(bf16[8,72,256]{2,1,0:T(8,128)(2,1)S(1)} %all-to-all-done.1.m_ref) | copy-start | bytes 884740
  44.5 16.8 %collective-permute-start = (bf16[8,72,256]{2,1,0:T(8,128)(2,1)S(1)}, bf16[8,72,256]{2,1,0:T(8,128)(2,1)S(1)}, u32[]{:S(2)}, u32[]{:S(2)}) collective-permute-start(bf16[8,72,256]{2,1,0:T(8,128)(2,1)S(1)} %all-to-all-done.1.m_ref), channel_id=1, source_target_pairs={{0,16},{16,0},{1,17},{17,1},{2,18},{18,2},{3,19},{19,3},{4,20},{20... | collective-permute-start | bytes 884744 | tf_op jit(solution)/shard_map/ppermute | solution.py:343
  48.4 0.6 copy-start.10
  48.4 0.6 copy-start.5
  49.0 0.6 copy-start.6
  61.3 0.7 copy-start.2
  82.2 1.5 %collective-permute-start.4 = (bf16[5,16,256]{2,1,0:T(8,128)(2,1)}, bf16[5,16,256]{2,1,0:T(8,128)(2,1)S(1)}, u32[]{:S(2)}, u32[]{:S(2)}) collective-permute-start(bf16[5,16,256]{2,1,0:T(8,128)(2,1)} %get-tuple-element.19), channel_id=1, source_target_pairs={{0,1},{1,0},{2,3},{3,2},{4,5},{5,4},{6,7},{7,6},{8,9},{9,8},{10,11... | collective-permute-start | bytes 122888 | tf_op jit(solution)/shard_map/ppermute | solution.py:343
  83.7 0.6 copy-start.9
  86.1 7.5 %collective-permute-start.5 = (bf16[80,256]{1,0:T(8,128)(2,1)}, bf16[80,256]{1,0:T(8,128)(2,1)S(1)}, u32[]{:S(2)}, u32[]{:S(2)}) collective-permute-start(bf16[80,256]{1,0:T(8,128)(2,1)} %get-tuple-element.21), channel_id=1, source_target_pairs={{0,2},{2,4},{4,6},{6,8},{8,10},{10,12},{12,14},{14,0},{1,3},{3,5},... | collective-permute-start | bytes 122888 | tf_op jit(solution)/shard_map/ppermute | solution.py:339
  87.6 6.3 %collective-permute-start.6 = (bf16[80,256]{1,0:T(8,128)(2,1)}, bf16[80,256]{1,0:T(8,128)(2,1)S(1)}, u32[]{:S(2)}, u32[]{:S(2)}) collective-permute-start(bf16[80,256]{1,0:T(8,128)(2,1)} %get-tuple-element.22), channel_id=1, source_target_pairs={{0,4},{2,6},{4,8},{6,10},{8,12},{10,14},{12,0},{14,2},{1,5},{3,7},... | collective-permute-start | bytes 122888 | tf_op jit(solution)/shard_map/ppermute | solution.py:339
  87.6 6.0 %collective-permute-start.7 = (bf16[80,128]{1,0:T(8,128)(2,1)}, bf16[80,128]{1,0:T(8,128)(2,1)S(1)}, u32[]{:S(2)}, u32[]{:S(2)}) collective-permute-start(bf16[80,128]{1,0:T(8,128)(2,1)} %get-tuple-element.23), channel_id=1, source_target_pairs={{0,14},{2,0},{4,2},{6,4},{8,6},{10,8},{12,10},{14,12},{1,15},{3,1}... | collective-permute-start | bytes 61448 | tf_op jit(solution)/shard_map/ppermute | solution.py:339
  93.6 0.6 copy-start.11
  93.6 0.6 copy-start.7
  93.9 0.6 copy-start.8

commit v2 on v1

--- a/solution.py
+++ b/solution.py
@@ -26,7 +26,7 @@
     return lax.dot_general(a, b, (dims, ((), ())), preferred_element_type=f32)
 
 
-def call(body, outs, scratch=(), anys=(), smem=(), count=0, limit=56):
+def call(body, outs, scratch=(), anys=(), smem=(), count=0, limit=56, flops=0):
     def spec(i):
         if i in anys:
             return pl.BlockSpec(memory_space=pl.ANY)
@@ -41,6 +41,7 @@
         out_specs=tuple(pl.BlockSpec(memory_space=pltpu.VMEM) for _ in outs),
         scratch_shapes=list(scratch),
         compiler_params=pltpu.CompilerParams(vmem_limit_bytes=limit << 20),
+        cost_estimate=pl.CostEstimate(flops=int(flops), bytes_accessed=1 << 20, transcendentals=0),
     )
 
 
@@ -53,7 +54,9 @@
     return high, (values - high.astype(f32)).astype(bf16)
 
 
-def partial_kernel(place_ref, a_ref, w_ref, out_ref, w_buf, sems, *, width, slots, local_pairs, features):
+def partial_kernel(
+    place_ref, mod_ref, wp_ref, w_ref, out_ref, w_buf, sems, *, width, slots, local_pairs, features
+):
     group = place_ref[0]
     span = local_pairs * LANES
     copies = []
@@ -64,9 +67,22 @@
         )
     for one in copies:
         one.start()
+    feats, model = wp_ref.shape
+    rows = w_buf.shape[1]
+    window = min(model, -(-(rows + LANES - 1) // LANES) * LANES)
+    begin = place_ref[3] * rows
+    low = jnp.minimum(begin // LANES * LANES, model - window)
+    cols = pl.ds(pl.multiple_of(low, LANES), window)
+    mean = jnp.sum(wp_ref[...].astype(f32), axis=1, keepdims=True) * (1.0 / model)
+    centered = wp_ref[:, cols].astype(f32) - mean
+    scaled = centered * (1.0 + mod_ref[0, 1:2, cols])
+    down = iota((ROWS - feats, window), 0)
+    tail = jnp.where(down < 2, jnp.broadcast_to(mod_ref[0, 0:1, cols], down.shape), 0.0)
+    stacked = jnp.concatenate([scaled, tail], axis=0)
+    stacked = pltpu.roll(stacked, (window - (begin - low)) % window, 1)
+    a = jnp.concatenate(split(stacked), axis=0)[:, :rows]
     for one in copies:
         one.wait()
-    a = a_ref[...]
     for owner in range(width):
         for slot in range(slots):
             tile = owner * slots + slot
@@ -159,8 +175,10 @@
     count_ref[:, columns:] = jnp.where(lane8 == 0, before, jnp.where(lane8 == 1, after, 1.0))
 
 
-def attend_pairs(m_ref, x_ref, xt_ref, var_ref, varrow_ref, att_ref, slots, pairs):
+def attend_pairs(place_ref, near_ref, far_ref, x_ref, xt_ref, var_ref, varrow_ref, put, slots, pairs, fold):
     tokens = x_ref.shape[0]
+    key = place_ref[5]
+    side = place_ref[3] % fold
     x = x_ref[:, :ROWS]
     xt = xt_ref[...]
     var = var_ref[...]
@@ -171,8 +189,10 @@
     scale = LOG2E * HEAD**-0.5
 
     def tile(t):
-        slot = t % slots
-        return m_ref[t // slots, :, slot * LANES : (slot + 1) * LANES]
+        owner, slot = divmod(t, slots)
+        z, y = divmod(owner, fold)
+        at = (z ^ key, slice(None), slice(slot * LANES, (slot + 1) * LANES))
+        return jnp.where(side == y, near_ref[at], far_ref[at])
 
     for pair in range(pairs):
         mq, mv, mk = (tile(3 * pair + sub) for sub in range(3))
@@ -199,54 +219,67 @@
             outs.append(dot(weights, vh))
         top = jnp.where(low, outs[0], outs[1])
         sums = pltpu.roll(jnp.where(low, outs[1], outs[0]), HEAD, 1)
-        att_ref[:, pair * LANES : (pair + 1) * LANES] = (top / sums).astype(bf16)
-
-
-def first_kernel(m_ref, x_ref, xt_ref, var_ref, varrow_ref, att_ref, *, slots, pairs):
-    attend_pairs(m_ref, x_ref, xt_ref, var_ref, varrow_ref, att_ref, slots, pairs)
+        put(pair, (top / sums).astype(bf16))
+
+
+def first_kernel(
+    place_ref, near_ref, far_ref, x_ref, xt_ref, var_ref, varrow_ref, att_ref, *, slots, pairs, fold
+):
+    def put(pair, value):
+        att_ref[:, pair * LANES : (pair + 1) * LANES] = value
+
+    attend_pairs(place_ref, near_ref, far_ref, x_ref, xt_ref, var_ref, varrow_ref, put, slots, pairs, fold)
 
 
 def second_kernel(
-    place_ref, m_ref, x_ref, xt_ref, var_ref, varrow_ref, att_ref, wp_ref, gate_ref, wf_ref, wo_ref,
+    place_ref, near_ref, far_ref, x_ref, xt_ref, var_ref, varrow_ref, att_ref, wp_ref, mod_ref, wf_ref, wo_ref,
     mine_ref, send_ref,
-    att_buf, wo_buf, res_buf, fin_buf, sem,
-    *, slots, pairs, channels, height, columns, halves,
+    att_buf, wo_buf, res_buf, fin_buf, sum_buf, sem,
+    *, slots, pairs, channels, height, columns, halves, fold,
 ):
     load = pltpu.make_async_copy(wo_ref, wo_buf, sem.at[0])
     load.start()
     group = place_ref[0]
     guide = place_ref[2]
-    attend_pairs(m_ref, x_ref, xt_ref, var_ref, varrow_ref, att_buf, slots, pairs) if halves == 2 else None
+    span = pairs * LANES
+    first = pl.multiple_of(group * span, LANES) if halves == 2 else 0
+    att_buf[:, pl.ds(first, span)] = att_ref[...]
+    if halves == 2:
+        other = (1 - group) * span
+
+        def put(pair, value):
+            at = pl.multiple_of(other + pair * LANES, LANES)
+            att_buf[:, pl.ds(at, LANES)] = value
+
+        attend_pairs(place_ref, near_ref, far_ref, x_ref, xt_ref, var_ref, varrow_ref, put, slots, pairs, fold)
     load.wait()
     tokens = x_ref.shape[0]
-    feats = wp_ref.shape[0]
-    model = wp_ref.shape[1]
-    span = pairs * LANES
+    feats, model = wp_ref.shape
     x = x_ref[:, :feats]
-    first = pl.multiple_of(group * span, LANES) if halves == 2 else 0
-    other = pl.multiple_of((1 - group) * span, LANES)
-    start = 0
-    while start < model:
-        size = min(2 * LANES, model - start)
-        cols = slice(start, start + size)
-        mixed = dot(att_ref[...], wo_buf[pl.ds(first, span), cols])
-        if halves == 2:
-            mixed = mixed + dot(att_buf[...], wo_buf[pl.ds(other, span), cols])
-        res_buf[:, cols] = dot(x, wp_ref[:, cols]) + gate_ref[:, cols] * mixed
-        start += size
-    block = 32
-
-    def norm(i, carry):
-        at = pl.ds(pl.multiple_of(i * block, block), block)
-        h = res_buf[at, :]
-        mean = jnp.sum(h, axis=1, keepdims=True) * (1.0 / model)
-        c = h - mean
-        v = jnp.sum(c * c, axis=1, keepdims=True) * (1.0 / model)
-        fin_buf[at, :] = (c * lax.rsqrt(v + epsilon)).astype(bf16)
-        return carry
-
-    lax.fori_loop(0, tokens // block, norm, 0)
-    result = dot(fin_buf[...], wf_ref[...])
+    tiles = [(at, min(2 * LANES, model - at)) for at in range(0, model, 2 * LANES)]
+    sum_buf[...] = jnp.zeros(sum_buf.shape, f32)
+
+    def folded(value):
+        total = value[:, :LANES]
+        for at in range(LANES, value.shape[1], LANES):
+            total = total + value[:, at : at + LANES]
+        return total
+
+    for at, size in tiles:
+        cols = slice(at, at + size)
+        mixed = dot(att_buf[...], wo_buf[:, cols])
+        value = dot(x, wp_ref[:, cols]) + mod_ref[0, 2:3, cols] * mixed
+        res_buf[:, cols] = value
+        sum_buf[...] = sum_buf[...] + folded(value)
+    mean = jnp.sum(sum_buf[...], axis=1, keepdims=True) * (1.0 / model)
+    sum_buf[...] = jnp.zeros(sum_buf.shape, f32)
+    for at, size in tiles:
+        cols = slice(at, at + size)
+        value = res_buf[:, cols] - mean
+        fin_buf[:, cols] = value.astype(bf16)
+        sum_buf[...] = sum_buf[...] + folded(value * value)
+    spread = jnp.sum(sum_buf[...], axis=1, keepdims=True) * (1.0 / model)
+    result = dot(fin_buf[...], wf_ref[...], ((1,), (1,))) * lax.rsqrt(spread + epsilon)
     near = height // 2 + 1
     keep = guide * (near - 2)
     give = (1 - guide) * (near - 2)
@@ -343,6 +376,26 @@
     return lax.ppermute(x, axis, [(0, 1), (1, 0)])
 
 
+def gather_major(chunk, fold, direct):
+    width = lax.axis_size("width")
+    if not direct:
+        every = lax.all_gather(chunk, "width")
+        every = every.reshape((width // fold, fold) + chunk.shape)
+        return lax.dynamic_index_in_dim(every, lax.axis_index("width") % fold, 1, False)
+    pieces = [chunk]
+    for d in range(1, width // fold):
+        route = [(i, (i // fold ^ d) * fold + i % fold) for i in range(width)]
+        pieces.append(lax.ppermute(chunk, "width", route))
+    return jnp.stack(pieces)
+
+
+def swap_minor(stack, fold):
+    if fold == 1:
+        return stack
+    width = lax.axis_size("width")
+    return lax.ppermute(stack, "width", [(i, i ^ 1) for i in range(width)])
+
+
 def shards(latent, starts, counts, step_index, cond_mod, w_patch, w_qkv, w_out, w_final, w_dec):
     guide = lax.axis_index("guide")
     place = lax.axis_index("width")
@@ -359,9 +412,12 @@
     if halves == 1:
         group = group * 0
     rows = w_qkv.shape[0]
-    modulation = cond_mod[0]
+    fold = 2 if width % 2 == 0 else 1
+    depth = width // fold
+    direct = depth <= 8 and depth & (depth - 1) == 0
     offset = starts[0] - place * columns
-    scalars = jnp.stack([group, offset, guide, place, step_index[0]]).astype(jnp.int32)
+    key = place // fold if direct else 0
+    scalars = jnp.stack([group, offset, guide, place, step_index[0], key]).astype(jnp.int32)
 
     pack = jnp.concatenate(
         [latent, jnp.broadcast_to(counts.astype(f32)[None, None, :], (1, height, columns))], axis=0
@@ -369,14 +425,6 @@
     right = shift(pack, -1)
     further = shift(latent.astype(bf16), -2)
     left = shift(pack, 1)
-
-    wide = w_patch.astype(f32)
-    centered = wide - jnp.mean(wide, axis=1, keepdims=True)
-    mine = lax.dynamic_slice_in_dim(centered, place * rows, rows, 1)
-    own_mod = lax.dynamic_slice_in_dim(modulation, place * rows, rows, 1)
-    shift_rows = jnp.concatenate([own_mod[0:1]] * 2 + [jnp.zeros((ROWS - feats - 2, rows), f32)])
-    stacked = jnp.concatenate([mine * (1.0 + own_mod[1:2]), shift_rows])
-    a = jnp.concatenate(split(stacked), axis=0)
 
     (parts,) = call(
         functools.partial(
@@ -387,8 +435,8 @@
             pltpu.VMEM((3, rows, local_pairs * LANES), bf16),
             pltpu.SemaphoreType.DMA((3,)),
         ],
-        anys=(2,), smem=(0,), count=3,
-    )(scalars, a, w_qkv)
+        anys=(3,), smem=(0,), count=4,
+    )(scalars, cond_mod, w_patch, w_qkv)
     parts = lax.all_to_all(parts, "width", 0, 0, tiled=True)
     (chunk,) = call(
         functools.partial(sum_kernel, width=width), [((ROWS, slots * LANES), bf16)], count=1
@@ -406,32 +454,35 @@
             pltpu.VMEM((feats, tokens), f32),
             pltpu.VMEM((tokens, model), f32),
         ],
-        smem=(0,), count=6,
+        smem=(0,), count=6, flops=5e9,
     )(scalars, pack, right, left, further, w_patch)
-    half = lax.all_to_all(
-        jnp.broadcast_to(chunk[None], (width,) + chunk.shape), "width", 0, 0, tiled=True
-    )
-    other = swap(half, "groups") if halves == 2 else half
+    stack = gather_major(chunk, fold, direct)
+    side = swap_minor(stack, fold)
+    if halves == 2:
+        stack_x, side_x = swap(stack, "groups"), swap(side, "groups")
+    else:
+        stack_x, side_x = stack, side
     (att,) = call(
-        functools.partial(first_kernel, slots=slots, pairs=local_pairs),
+        functools.partial(first_kernel, slots=slots, pairs=local_pairs, fold=fold),
         [((tokens, local_pairs * LANES), bf16)],
-        count=5,
-    )(half, x, xt, var, varrow)
+        smem=(0,), count=7, flops=6e9,
+    )(scalars, stack, side, x, xt, var, varrow)
     mine_v, send_v = call(
         functools.partial(
             second_kernel, slots=slots, pairs=local_pairs, channels=channels, height=height,
-            columns=columns, halves=halves,
+            columns=columns, halves=halves, fold=fold,
         ),
         [((near, channels, 2 * columns), f32), ((near, channels, 2 * columns), bf16)],
         scratch=[
-            pltpu.VMEM((tokens, local_pairs * LANES), bf16),
+            pltpu.VMEM((tokens, features), bf16),
             pltpu.VMEM(w_out.shape, bf16),
             pltpu.VMEM((tokens, model), f32),
             pltpu.VMEM((tokens, model), bf16),
+            pltpu.VMEM((tokens, LANES), f32),
             pltpu.SemaphoreType.DMA((1,)),
         ],
-        anys=(10,), smem=(0,), count=11,
-    )(scalars, other, x, xt, var, varrow, att, w_patch, modulation[2:3], w_final, w_out)
+        anys=(11,), smem=(0,), count=12, flops=12e9,
+    )(scalars, stack_x, side_x, x, xt, var, varrow, att, w_patch, cond_mod, w_final.T, w_out)
     theirs = swap(send_v, "guide")
     flat = near * channels
     own, one, two, back = call(

time: 97.8 us -> 88.5 us (0.905)
  blocking collectives: 17.8 us -> 0 us
  starting transfers between devices: 16.6 us -> 26.3 us
  waiting for transfers between devices: 7.58 us -> 12.8 us
  Pallas kernels: 41.3 us -> 37.6 us
  local copies, waits for them, and re-layouts: 7.76 us -> 5.95 us
    all_to_all x1 -> x0, blocking collectives: 17.8 us -> none  [shards(): parts = lax.all_to_all(parts, 'width', 0, 0, tiled=True)]
    ppermute x0 -> x4, starting transfers between devices: none -> 8.91 us  [the longest x1 4.52 us: swap_minor(): return lax.ppermute(stack, 'width', [(i, i ^ 1) for i in range(width)])]
    all_to_all x1, waiting for transfers between devices: 4.14 us -> 8.95 us  [shards(): parts = lax.all_to_all(parts, 'width', 0, 0, tiled=True)]
    pallas_call x1, Pallas kernels: 20.2 us -> 16.2 us  [shards(): call(functools.partial(second_kernel, slots=slots, pairs=local_pairs, cha...]
    all_to_all x1, starting transfers between devices: 3.42 us -> 7.32 us  [shards(): parts = lax.all_to_all(parts, 'width', 0, 0, tiled=True)]
    ppermute x6, starting transfers between devices: 11.6 us -> 7.89 us  [shift(): lax.ppermute(x, 'width', [(i, (i + by) % peers) for i in range(peers)])]
    broadcast_in_dim x2 -> x0, local copies, waits for them, and re-layouts: 1.5 us -> none  [the longest x1 1.5 us: shards(): jnp.broadcast_to(chunk[None], (width,) + chunk.shape)]
    slice x1 -> x0, local copies, waits for them, and re-layouts: 1.3 us -> none  [shards(): modulation[2:3]]
  transfers between devices with their start and end apart: 9 -> 14, of which waited for: 4 -> 5; matrix products, arithmetic and copies ran while one was open for 2% -> 4% of each run, Pallas kernels for 12% -> 13%
where the time goes in v2:
time: 88.5 us; the launch traced here: 87.7 us
  Pallas kernels  37.6 us (42%)
  starting transfers between devices  26.3 us (30%)
  waiting for transfers between devices  12.8 us (14%)
  local copies, waits for them, and re-layouts  5.95 us (7%)
  other arithmetic  3.14 us (4%)
  between operations  2.02 us (2%)
    pallas_call x1, Pallas kernels, shards(): call(functools.partial(second_kernel, slots=slots, pairs=local_pairs, cha...  16.2 us
    all_to_all x1, waiting for transfers between devices, shards(): parts = lax.all_to_all(parts, 'width', 0, 0, tiled=True)  8.95 us
    ppermute x6, starting transfers between devices, shift(): lax.ppermute(x, 'width', [(i, (i + by) % peers) for i in range(peers)])  7.89 us
    all_to_all x1, starting transfers between devices, shards(): parts = lax.all_to_all(parts, 'width', 0, 0, tiled=True)  7.32 us
    pallas_call x1, Pallas kernels, shards(): call(functools.partial(first_kernel, slots=slots, pairs=local_pairs, fold...  6.39 us
    unnamed x27, local copies, waits for them, and re-layouts  5.33 us
    pallas_call x1, Pallas kernels, shards(): call(window_kernel, [((tokens, LANES), bf16), ((ROWS, tokens), bf16), ((t...  5.33 us
    ppermute x1, starting transfers between devices, swap_minor(): return lax.ppermute(stack, 'width', [(i, i ^ 1) for i in range(width)])  4.52 us
  transfers between devices with their start and end apart: 14, of which 5 were waited for; matrix products, arithmetic and copies ran while one was open for 4% of the time, Pallas kernels for 13%

profile of v2, /device:TPU:0, one launch (start us, length us, event | category | flops | bytes accessed | tf_op | source)
XLA Modules:
  0.0 87.7 jit_solution(12042171562361630727)
XLA Ops:
  1.9 1.4 %copy.12.mod_ref = f32[1,3,2432]{2,1,0:T(4,128)} copy(f32[1,3,2432]{2,0,1:T(1,128)} %param.14) | data formatting | bytes 58368 | tf_op args[4]
  3.3 0.6 stack.38.place_ref
  3.9 3.7 %shard_map.113 = bf16[8,72,256]{2,1,0:T(8,128)(2,1)} custom-call(s32[6]{0:T(128)} %stack.38.place_ref, f32[1,3,2432]{2,1,0:T(4,128)} %copy.12.mod_ref, bf16[64,2432]{1,0:T(8,128)(2,1)} %wp_ref.3, bf16[304,3840]{1,0:T(8,128)(2,1)} %w_ref.3), custom_call_target="tpu_custom_call" | custom-call | bytes 1048576 | tf_op jit(solution)/shard_map/pallas_call | solution.py:429
  7.7 7.3 %all-to-all-start = ((bf16[8,72,256]{2,1,0:T(8,128)(2,1)}), bf16[8,72,256]{2,1,0:T(8,128)(2,1)S(1)}, u32[]{:S(2)}, u32[]{:S(2)}) async-start(bf16[8,72,256]{2,1,0:T(8,128)(2,1)} %shard_map.113), calls=%async_computation | async-start | bytes 589824 | tf_op jit(solution)/shard_map/all_to_all | solution.py:440
  15.0 0.7 convert_element_type.6
  15.6 9.0 %all-to-all-done.parts_ref = bf16[8,72,256]{2,1,0:T(8,128)(2,1)S(1)} async-done(((bf16[8,72,256]{2,1,0:T(8,128)(2,1)}), bf16[8,72,256]{2,1,0:T(8,128)(2,1)S(1)}, u32[]{:S(2)}, u32[]{:S(2)}) %all-to-all-start) | async-done | bytes 294944 | tf_op jit(solution)/shard_map/all_to_all | solution.py:440
  24.6 0.7 copy-done
  25.3 1.6 %shard_map.114 = bf16[72,256]{1,0:T(8,128)(2,1)} custom-call(bf16[8,72,256]{2,1,0:T(8,128)(2,1)} %copy-done), custom_call_target="tpu_custom_call" | custom-call | bytes 1048576 | tf_op jit(solution)/shard_map/pallas_call | solution.py:441
  26.9 1.0 %collective-permute-start = (bf16[72,256]{1,0:T(8,128)(2,1)}, bf16[72,256]{1,0:T(8,128)(2,1)S(1)}, u32[]{:S(2)}, u32[]{:S(2)}) collective-permute-start(bf16[72,256]{1,0:T(8,128)(2,1)} %shard_map.114), channel_id=1, source_target_pairs={{0,4},{2,6},{4,0},{6,2},{8,12},{10,14},{12,8},{14,10},{1,5},{3,7},... | collective-permute-start | bytes 110600 | tf_op jit(solution)/shard_map/ppermute | solution.py:388
  27.9 0.7 collective-permute-start.1
  28.6 2.7 %collective-permute-start.2 = (bf16[72,256]{1,0:T(8,128)(2,1)}, bf16[72,256]{1,0:T(8,128)(2,1)S(1)}, u32[]{:S(2)}, u32[]{:S(2)}) collective-permute-start(bf16[72,256]{1,0:T(8,128)(2,1)} %shard_map.114), channel_id=1, source_target_pairs={{0,12},{2,14},{4,8},{6,10},{8,4},{10,6},{12,0},{14,2},{1,13},{3,15... | collective-permute-start | bytes 110600 | tf_op jit(solution)/shard_map/ppermute | solution.py:388
  31.3 0.8 pad_maximum_fusion.1.own_ref
  32.2 2.3 %collective-permute-start.6 = (f32[17,8,128]{2,1,0:T(8,128)S(1)}, f32[17,8,128]{2,1,0:T(8,128)S(1)}, u32[]{:S(2)}, u32[]{:S(2)}) collective-permute-start(f32[17,8,128]{2,1,0:T(8,128)S(1)} %pad_maximum_fusion.1.own_ref), channel_id=1, source_target_pairs={{0,14},{2,0},{4,2},{6,4},{8,6},{10,8},{12,10},{14,12},{1,15},{3,1}... | collective-permute-start | bytes 208904 | tf_op jit(solution)/shard_map/ppermute | solution.py:372
  34.5 0.8 convert_element_type.7
  35.3 0.0 collective-permute-done
  35.3 0.8 collective-permute-start.8
  36.2 0.0 collective-permute-done.1
  36.2 0.0 collective-permute-done.2
  36.2 0.8 pad_maximum_fusion.near_ref
  37.0 4.5 %collective-permute-start.4 = (bf16[4,72,256]{2,1,0:T(8,128)(2,1)S(1)}, bf16[4,72,256]{2,1,0:T(8,128)(2,1)S(1)}, u32[]{:S(2)}, u32[]{:S(2)}) collective-permute-start(bf16[4,72,256]{2,1,0:T(8,128)(2,1)S(1)} %pad_maximum_fusion.near_ref), channel_id=1, source_target_pairs={{0,2},{2,0},{4,6},{6,4},{8,10},{10,8},{12,14},{14,12},{1,3},{3,1},... | collective-permute-start | bytes 442376 | tf_op jit(solution)/shard_map/ppermute | solution.py:396
  41.5 0.0 collective-permute-done.6.right_ref
  41.5 0.1 collective-permute-done.7.left_ref
  41.6 0.5 copy-done.12
  42.1 0.0 copy-done.10
  42.1 0.6 copy-done.11
  42.8 5.3 %shard_map.115 = (bf16[512,128]{1,0:T(8,128)(2,1)}, bf16[72,512]{1,0:T(8,128)(2,1)}, f32[512,128]{1,0:T(8,128)}, f32[8,512]{1,0:T(8,128)}, f32[5,16,256]{2,1,0:T(8,128)}, /*index=5*/f32[8,256]{1,0:T(8,128)}) custom-call(s32[6]{0:T(128)} %stack.38.place_ref, f32[17,8,128]{2,1,0:T(8,128)} %copy-done.2, f32[17,8,128]{2,1,0:T(8,128)} %copy-done.10, ...), custom_call_target="tpu_custom_call" | custom-call | flops 5000000000 | bytes 1048576 | tf_op jit(solution)/shard_map/pallas_call | solution.py:446
  48.1 1.6 %collective-permute-start.3 = (bf16[4,72,256]{2,1,0:T(8,128)(2,1)S(1)}, bf16[4,72,256]{2,1,0:T(8,128)(2,1)S(1)}, u32[]{:S(2)}, u32[]{:S(2)}) collective-permute-start(bf16[4,72,256]{2,1,0:T(8,128)(2,1)S(1)} %pad_maximum_fusion.near_ref), channel_id=1, source_target_pairs={{0,16},{16,0},{1,17},{17,1},{2,18},{18,2},{3,19},{19,3},{4,20},{20... | collective-permute-start | bytes 442376 | tf_op jit(solution)/shard_map/ppermute | solution.py:376
  49.7 0.0 collective-permute-done.4.far_ref
  49.7 0.5 collective-permute-start.5
  50.2 0.1 copy-done.7
  50.3 6.4 %shard_map.116.att_ref = bf16[512,640]{1,0:T(8,128)(2,1)} custom-call(s32[6]{0:T(128)} %stack.38.place_ref, bf16[4,72,256]{2,1,0:T(8,128)(2,1)} %copy-done.1, bf16[4,72,256]{2,1,0:T(8,128)(2,1)} %copy-done.7, bf16[512,128]{1,0:T(8,128)(2,1)} %get-tuple-element.14.x_ref, bf16[72,512]{1,0:T(8,128)(2,1)} %get-tuple-element.15.xt_ref, ...), custom_call_target="tpu_custom_call" | custom-call | flops 6000000000 | bytes 1048576 | tf_op jit(solution)/shard_map/pallas_call | solution.py:465
  56.7 0.0 collective-permute-done.3.near_ref
  56.7 0.0 collective-permute-done.5.far_ref
  56.7 0.6 copy-done.8
  57.4 0.1 copy-done.9
  57.4 16.2 %shard_map.117 = (f32[5,16,256]{2,1,0:T(8,128)}, bf16[5,16,256]{2,1,0:T(8,128)(2,1)}) custom-call(s32[6]{0:T(128)} %stack.38.place_ref, bf16[4,72,256]{2,1,0:T(8,128)(2,1)} %copy-done.8, bf16[4,72,256]{2,1,0:T(8,128)(2,1)} %copy-done.9, bf16[512,128]{1,0:T(8,128)(2,1)} %get-tuple-element.14.x_ref, bf16[72,512]{1,0:T(8,128)(2,1)} %get-tuple-element.15.xt_ref, ...), custom_call_target="tpu_custom_call" | custom-call | flops 12000000000 | bytes 1048576 | tf_op jit(solution)/shard_map/pallas_call | solution.py:470
  73.7 0.1 collective-permute-start.9
  73.8 1.4 %collective-permute-done.9.theirs_ref = bf16[5,16,256]{2,1,0:T(8,128)(2,1)S(1)} collective-permute-done((bf16[5,16,256]{2,1,0:T(8,128)(2,1)}, bf16[5,16,256]{2,1,0:T(8,128)(2,1)S(1)}, u32[]{:S(2)}, u32[]{:S(2)}) %collective-permute-start.9) | collective-permute-done | bytes 40992 | tf_op jit(solution)/shard_map/ppermute | solution.py:376
  75.2 0.6 copy-done.5
  75.8 1.8 %shard_map.118 = (f32[80,256]{1,0:T(8,128)}, bf16[80,256]{1,0:T(8,128)(2,1)}, bf16[80,256]{1,0:T(8,128)(2,1)}, bf16[80,128]{1,0:T(8,128)(2,1)}) custom-call(s32[6]{0:T(128)} %stack.38.place_ref, f32[5,16,256]{2,1,0:T(8,128)} %get-tuple-element.18.mine_ref, bf16[5,16,256]{2,1,0:T(8,128)(2,1)} %copy-done.5), custom_call_target="tpu_custom_call" | custom-call | bytes 1048576 | tf_op jit(solution)/shard_map/pallas_call | solution.py:488
  77.6 0.7 collective-permute-start.10
  78.3 4.0 %collective-permute-start.12 = (bf16[80,128]{1,0:T(8,128)(2,1)}, bf16[80,128]{1,0:T(8,128)(2,1)S(1)}, u32[]{:S(2)}, u32[]{:S(2)}) collective-permute-start(bf16[80,128]{1,0:T(8,128)(2,1)} %get-tuple-element.23), channel_id=1, source_target_pairs={{0,14},{2,0},{4,2},{6,4},{8,6},{10,8},{12,10},{14,12},{1,15},{3,1}... | collective-permute-start | bytes 61448 | tf_op jit(solution)/shard_map/ppermute | solution.py:372
  82.3 1.7 %collective-permute-done.12.back_ref = bf16[80,128]{1,0:T(8,128)(2,1)S(1)} collective-permute-done((bf16[80,128]{1,0:T(8,128)(2,1)}, bf16[80,128]{1,0:T(8,128)(2,1)S(1)}, u32[]{:S(2)}, u32[]{:S(2)}) %collective-permute-start.12) | collective-permute-done | bytes 20512 | tf_op jit(solution)/shard_map/ppermute | solution.py:372
  84.0 0.6 collective-permute-done.10.one_ref
  84.6 0.0 collective-permute-done.11.two_ref
  84.6 0.5 copy-done.3
  85.2 0.1 copy-done.4
  85.2 2.5 %shard_map.119 = (f32[16,4,128]{2,1,0:T(4,128)}, bf16[4,128,512]{2,1,0:T(8,128)(2,1)}) custom-call(s32[6]{0:T(128)} %stack.38.place_ref, f32[80,256]{1,0:T(8,128)} %get-tuple-element.20.own_ref, bf16[80,256]{1,0:T(8,128)(2,1)} %copy-done.3, bf16[80,256]{1,0:T(8,128)(2,1)} %copy-done.4, bf16[80,128]{1,0:T(8,128)(2,1)} %copy-done.6, ...), custom_call_target="tpu_custom_call" | custom-call | bytes 1048576 | tf_op jit(solution)/shard_map/pallas_call | solution.py:499
  (20 shorter events, 0.0 us)
Async XLA Ops:
  7.7 16.9 %all-to-all-start = ((bf16[8,72,256]{2,1,0:T(8,128)(2,1)}), bf16[8,72,256]{2,1,0:T(8,128)(2,1)S(1)}, u32[]{:S(2)}, u32[]{:S(2)}) async-start(bf16[8,72,256]{2,1,0:T(8,128)(2,1)} %shard_map.113), calls=%async_computation | async-start | bytes 589824 | tf_op jit(solution)/shard_map/all_to_all | solution.py:440
  24.6 0.7 copy-start
  26.9 8.4 %collective-permute-start = (bf16[72,256]{1,0:T(8,128)(2,1)}, bf16[72,256]{1,0:T(8,128)(2,1)S(1)}, u32[]{:S(2)}, u32[]{:S(2)}) collective-permute-start(bf16[72,256]{1,0:T(8,128)(2,1)} %shard_map.114), channel_id=1, source_target_pairs={{0,4},{2,6},{4,0},{6,2},{8,12},{10,14},{12,8},{14,10},{1,5},{3,7},... | collective-permute-start | bytes 110600 | tf_op jit(solution)/shard_map/ppermute | solution.py:388
  27.9 8.2 %collective-permute-start.1 = (bf16[72,256]{1,0:T(8,128)(2,1)}, bf16[72,256]{1,0:T(8,128)(2,1)S(1)}, u32[]{:S(2)}, u32[]{:S(2)}) collective-permute-start(bf16[72,256]{1,0:T(8,128)(2,1)} %shard_map.114), channel_id=1, source_target_pairs={{0,8},{2,10},{4,12},{6,14},{8,0},{10,2},{12,4},{14,6},{1,9},{3,11}... | collective-permute-start | bytes 110600 | tf_op jit(solution)/shard_map/ppermute | solution.py:388
  28.6 7.6 %collective-permute-start.2 = (bf16[72,256]{1,0:T(8,128)(2,1)}, bf16[72,256]{1,0:T(8,128)(2,1)S(1)}, u32[]{:S(2)}, u32[]{:S(2)}) collective-permute-start(bf16[72,256]{1,0:T(8,128)(2,1)} %shard_map.114), channel_id=1, source_target_pairs={{0,12},{2,14},{4,8},{6,10},{8,4},{10,6},{12,0},{14,2},{1,13},{3,15... | collective-permute-start | bytes 110600 | tf_op jit(solution)/shard_map/ppermute | solution.py:388
  32.2 9.5 %copy-start.2 = (f32[17,8,128]{2,1,0:T(8,128)}, f32[17,8,128]{2,1,0:T(8,128)S(1)}, u32[]{:S(2)}) copy-start(f32[17,8,128]{2,1,0:T(8,128)S(1)} %pad_maximum_fusion.1.own_ref) | copy-start | bytes 208900
  32.2 9.4 %collective-permute-start.6 = (f32[17,8,128]{2,1,0:T(8,128)S(1)}, f32[17,8,128]{2,1,0:T(8,128)S(1)}, u32[]{:S(2)}, u32[]{:S(2)}) collective-permute-start(f32[17,8,128]{2,1,0:T(8,128)S(1)} %pad_maximum_fusion.1.own_ref), channel_id=1, source_target_pairs={{0,14},{2,0},{4,2},{6,4},{8,6},{10,8},{12,10},{14,12},{1,15},{3,1}... | collective-permute-start | bytes 208904 | tf_op jit(solution)/shard_map/ppermute | solution.py:372
  34.5 7.1 %collective-permute-start.7 = (f32[17,8,128]{2,1,0:T(8,128)S(1)}, f32[17,8,128]{2,1,0:T(8,128)S(1)}, u32[]{:S(2)}, u32[]{:S(2)}) collective-permute-start(f32[17,8,128]{2,1,0:T(8,128)S(1)} %pad_maximum_fusion.1.own_ref), channel_id=1, source_target_pairs={{0,2},{2,4},{4,6},{6,8},{8,10},{10,12},{12,14},{14,0},{1,3},{3,5},... | collective-permute-start | bytes 208904 | tf_op jit(solution)/shard_map/ppermute | solution.py:372
  35.3 6.2 %collective-permute-start.8 = (bf16[16,8,128]{2,1,0:T(8,128)(2,1)S(1)}, bf16[16,8,128]{2,1,0:T(8,128)(2,1)S(1)}, u32[]{:S(2)}, u32[]{:S(2)}) collective-permute-start(bf16[16,8,128]{2,1,0:T(8,128)(2,1)S(1)} %convert_element_type.7), channel_id=1, source_target_pairs={{0,12},{2,14},{4,0},{6,2},{8,4},{10,6},{12,8},{14,10},{1,13},{3,15... | collective-permute-start | bytes 98312 | tf_op jit(solution)/shard_map/ppermute | solution.py:372
  37.0 11.1 %copy-start.1 = (bf16[4,72,256]{2,1,0:T(8,128)(2,1)}, bf16[4,72,256]{2,1,0:T(8,128)(2,1)S(1)}, u32[]{:S(2)}) copy-start(bf16[4,72,256]{2,1,0:T(8,128)(2,1)S(1)} %pad_maximum_fusion.near_ref) | copy-start | bytes 442372
  37.0 12.7 %collective-permute-start.4 = (bf16[4,72,256]{2,1,0:T(8,128)(2,1)S(1)}, bf16[4,72,256]{2,1,0:T(8,128)(2,1)S(1)}, u32[]{:S(2)}, u32[]{:S(2)}) collective-permute-start(bf16[4,72,256]{2,1,0:T(8,128)(2,1)S(1)} %pad_maximum_fusion.near_ref), channel_id=1, source_target_pairs={{0,2},{2,0},{4,6},{6,4},{8,10},{10,8},{12,14},{14,12},{1,3},{3,1},... | collective-permute-start | bytes 442376 | tf_op jit(solution)/shard_map/ppermute | solution.py:396
  41.5 0.6 copy-start.12
  41.5 0.6 copy-start.10
  42.1 0.6 copy-start.11
  48.1 8.6 %collective-permute-start.3 = (bf16[4,72,256]{2,1,0:T(8,128)(2,1)S(1)}, bf16[4,72,256]{2,1,0:T(8,128)(2,1)S(1)}, u32[]{:S(2)}, u32[]{:S(2)}) collective-permute-start(bf16[4,72,256]{2,1,0:T(8,128)(2,1)S(1)} %pad_maximum_fusion.near_ref), channel_id=1, source_target_pairs={{0,16},{16,0},{1,17},{17,1},{2,18},{18,2},{3,19},{19,3},{4,20},{20... | collective-permute-start | bytes 442376 | tf_op jit(solution)/shard_map/ppermute | solution.py:376
  49.7 0.7 copy-start.7
  49.7 7.1 %collective-permute-start.5 = (bf16[4,72,256]{2,1,0:T(8,128)(2,1)S(1)}, bf16[4,72,256]{2,1,0:T(8,128)(2,1)S(1)}, u32[]{:S(2)}, u32[]{:S(2)}) collective-permute-start(bf16[4,72,256]{2,1,0:T(8,128)(2,1)S(1)} %collective-permute-done.4.far_ref), channel_id=1, source_target_pairs={{0,16},{16,0},{1,17},{17,1},{2,18},{18,2},{3,19},{19,3},{4,20},{20... | collective-permute-start | bytes 442376 | tf_op jit(solution)/shard_map/ppermute | solution.py:376
  56.7 0.7 copy-start.8
  56.7 0.7 copy-start.9
  73.7 1.5 %collective-permute-start.9 = (bf16[5,16,256]{2,1,0:T(8,128)(2,1)}, bf16[5,16,256]{2,1,0:T(8,128)(2,1)S(1)}, u32[]{:S(2)}, u32[]{:S(2)}) collective-permute-start(bf16[5,16,256]{2,1,0:T(8,128)(2,1)} %get-tuple-element.19), channel_id=1, source_target_pairs={{0,1},{1,0},{2,3},{3,2},{4,5},{5,4},{6,7},{7,6},{8,9},{9,8},{10,11... | collective-permute-start | bytes 122888 | tf_op jit(solution)/shard_map/ppermute | solution.py:376
  75.2 0.6 copy-start.5
  77.6 7.0 %collective-permute-start.10 = (bf16[80,256]{1,0:T(8,128)(2,1)}, bf16[80,256]{1,0:T(8,128)(2,1)S(1)}, u32[]{:S(2)}, u32[]{:S(2)}) collective-permute-start(bf16[80,256]{1,0:T(8,128)(2,1)} %get-tuple-element.21), channel_id=1, source_target_pairs={{0,2},{2,4},{4,6},{6,8},{8,10},{10,12},{12,14},{14,0},{1,3},{3,5},... | collective-permute-start | bytes 122888 | tf_op jit(solution)/shard_map/ppermute | solution.py:372
  78.3 6.3 %collective-permute-start.11 = (bf16[80,256]{1,0:T(8,128)(2,1)}, bf16[80,256]{1,0:T(8,128)(2,1)S(1)}, u32[]{:S(2)}, u32[]{:S(2)}) collective-permute-start(bf16[80,256]{1,0:T(8,128)(2,1)} %get-tuple-element.22), channel_id=1, source_target_pairs={{0,4},{2,6},{4,8},{6,10},{8,12},{10,14},{12,0},{14,2},{1,5},{3,7},... | collective-permute-start | bytes 122888 | tf_op jit(solution)/shard_map/ppermute | solution.py:372
  78.3 5.7 %collective-permute-start.12 = (bf16[80,128]{1,0:T(8,128)(2,1)}, bf16[80,128]{1,0:T(8,128)(2,1)S(1)}, u32[]{:S(2)}, u32[]{:S(2)}) collective-permute-start(bf16[80,128]{1,0:T(8,128)(2,1)} %get-tuple-element.23), channel_id=1, source_target_pairs={{0,14},{2,0},{4,2},{6,4},{8,6},{10,8},{12,10},{14,12},{1,15},{3,1}... | collective-permute-start | bytes 61448 | tf_op jit(solution)/shard_map/ppermute | solution.py:372
  84.0 0.6 copy-start.6
  84.6 0.6 copy-start.3
  84.6 0.6 copy-start.4

commit v3 on v2

--- a/solution.py
+++ b/solution.py
@@ -26,10 +26,10 @@
     return lax.dot_general(a, b, (dims, ((), ())), preferred_element_type=f32)
 
 
-def call(body, outs, scratch=(), anys=(), smem=(), count=0, limit=56, flops=0):
+def call(body, outs, scratch=(), anys=(), smem=(), count=0, limit=16, flops=0):
     def spec(i):
         if i in anys:
-            return pl.BlockSpec(memory_space=pl.ANY)
+            return pl.BlockSpec(memory_space=pltpu.HBM)
         if i in smem:
             return pl.BlockSpec(memory_space=pltpu.SMEM)
         return pl.BlockSpec(memory_space=pltpu.VMEM)
@@ -75,9 +75,9 @@
     cols = pl.ds(pl.multiple_of(low, LANES), window)
     mean = jnp.sum(wp_ref[...].astype(f32), axis=1, keepdims=True) * (1.0 / model)
     centered = wp_ref[:, cols].astype(f32) - mean
-    scaled = centered * (1.0 + mod_ref[0, 1:2, cols])
+    scaled = centered * (1.0 + mod_ref[1, :, cols])
     down = iota((ROWS - feats, window), 0)
-    tail = jnp.where(down < 2, jnp.broadcast_to(mod_ref[0, 0:1, cols], down.shape), 0.0)
+    tail = jnp.where(down < 2, jnp.broadcast_to(mod_ref[0, :, cols], down.shape), 0.0)
     stacked = jnp.concatenate([scaled, tail], axis=0)
     stacked = pltpu.roll(stacked, (window - (begin - low)) % window, 1)
     a = jnp.concatenate(split(stacked), axis=0)[:, :rows]
@@ -234,11 +234,9 @@
 def second_kernel(
     place_ref, near_ref, far_ref, x_ref, xt_ref, var_ref, varrow_ref, att_ref, wp_ref, mod_ref, wf_ref, wo_ref,
     mine_ref, send_ref,
-    att_buf, wo_buf, res_buf, fin_buf, sum_buf, sem,
+    att_buf, res_buf, fin_buf, sum_buf,
     *, slots, pairs, channels, height, columns, halves, fold,
 ):
-    load = pltpu.make_async_copy(wo_ref, wo_buf, sem.at[0])
-    load.start()
     group = place_ref[0]
     guide = place_ref[2]
     span = pairs * LANES
@@ -252,7 +250,6 @@
             att_buf[:, pl.ds(at, LANES)] = value
 
         attend_pairs(place_ref, near_ref, far_ref, x_ref, xt_ref, var_ref, varrow_ref, put, slots, pairs, fold)
-    load.wait()
     tokens = x_ref.shape[0]
     feats, model = wp_ref.shape
     x = x_ref[:, :feats]
@@ -267,8 +264,8 @@
 
     for at, size in tiles:
         cols = slice(at, at + size)
-        mixed = dot(att_buf[...], wo_buf[:, cols])
-        value = dot(x, wp_ref[:, cols]) + mod_ref[0, 2:3, cols] * mixed
+        mixed = dot(att_buf[...], wo_ref[:, cols])
+        value = dot(x, wp_ref[:, cols]) + mod_ref[2, :, cols] * mixed
         res_buf[:, cols] = value
         sum_buf[...] = sum_buf[...] + folded(value)
     mean = jnp.sum(sum_buf[...], axis=1, keepdims=True) * (1.0 / model)
@@ -415,16 +412,10 @@
     fold = 2 if width % 2 == 0 else 1
     depth = width // fold
     direct = depth <= 8 and depth & (depth - 1) == 0
+    changes = jnp.swapaxes(cond_mod, 0, 1)
     offset = starts[0] - place * columns
     key = place // fold if direct else 0
     scalars = jnp.stack([group, offset, guide, place, step_index[0], key]).astype(jnp.int32)
-
-    pack = jnp.concatenate(
-        [latent, jnp.broadcast_to(counts.astype(f32)[None, None, :], (1, height, columns))], axis=0
-    )
-    right = shift(pack, -1)
-    further = shift(latent.astype(bf16), -2)
-    left = shift(pack, 1)
 
     (parts,) = call(
         functools.partial(
@@ -435,12 +426,17 @@
             pltpu.VMEM((3, rows, local_pairs * LANES), bf16),
             pltpu.SemaphoreType.DMA((3,)),
         ],
-        anys=(3,), smem=(0,), count=4,
-    )(scalars, cond_mod, w_patch, w_qkv)
+        anys=(3,), smem=(0,), count=4, limit=8,
+    )(scalars, changes, w_patch, pltpu.with_memory_space_constraint(w_qkv, pltpu.HBM))
+    latent_now, counts_now, parts = lax.optimization_barrier((latent, counts, parts))
+    pack = jnp.concatenate(
+        [latent_now, jnp.broadcast_to(counts_now.astype(f32)[None, None, :], (1, height, columns))], axis=0
+    )
+    right = shift(pack, -1)
+    further = shift(latent_now.astype(bf16), -2)
+    left = shift(pack, 1)
+
     parts = lax.all_to_all(parts, "width", 0, 0, tiled=True)
-    (chunk,) = call(
-        functools.partial(sum_kernel, width=width), [((ROWS, slots * LANES), bf16)], count=1
-    )(parts)
     near = height // 2 + 1
     tokens = height // 2 * columns
     x, xt, var, varrow, lat, count = call(
@@ -456,6 +452,10 @@
         ],
         smem=(0,), count=6, flops=5e9,
     )(scalars, pack, right, left, further, w_patch)
+    parts, x = lax.optimization_barrier((parts, x))
+    (chunk,) = call(
+        functools.partial(sum_kernel, width=width), [((ROWS, slots * LANES), bf16)], count=1, limit=4
+    )(parts)
     stack = gather_major(chunk, fold, direct)
     side = swap_minor(stack, fold)
     if halves == 2:
@@ -475,14 +475,12 @@
         [((near, channels, 2 * columns), f32), ((near, channels, 2 * columns), bf16)],
         scratch=[
             pltpu.VMEM((tokens, features), bf16),
-            pltpu.VMEM(w_out.shape, bf16),
             pltpu.VMEM((tokens, model), f32),
             pltpu.VMEM((tokens, model), bf16),
             pltpu.VMEM((tokens, LANES), f32),
-            pltpu.SemaphoreType.DMA((1,)),
         ],
-        anys=(11,), smem=(0,), count=12, flops=12e9,
-    )(scalars, stack_x, side_x, x, xt, var, varrow, att, w_patch, cond_mod, w_final.T, w_out)
+        smem=(0,), count=12, flops=12e9, limit=22,
+    )(scalars, stack_x, side_x, x, xt, var, varrow, att, w_patch, changes, w_final.T, w_out)
     theirs = swap(send_v, "guide")
     flat = near * channels
     own, one, two, back = call(

time: 88.5 us -> 77.7 us (0.88)
  Pallas kernels: 37.6 us -> 27.1 us
  starting transfers between devices: 26.3 us -> 32.8 us
  local copies, waits for them, and re-layouts: 5.95 us -> 2.8 us
  waiting for transfers between devices: 12.8 us -> 10.1 us
    all_to_all x1, waiting for transfers between devices: 8.95 us -> 0.01 us  [shards(): parts = lax.all_to_all(parts, 'width', 0, 0, tiled=True)]
    ppermute x6, starting transfers between devices: 7.89 us -> 16.7 us  [shift(): lax.ppermute(x, 'width', [(i, (i + by) % peers) for i in range(peers)])]
    pallas_call x1, Pallas kernels: 16.2 us -> 11.9 us  [shards(): call(functools.partial(second_kernel, slots=slots, pairs=local_pairs, cha...]
    ppermute x3, waiting for transfers between devices: 0.01 us -> 3.59 us  [gather_major(): pieces.append(lax.ppermute(chunk, 'width', route))]
    ppermute x1, starting transfers between devices: 4.52 us -> 1.53 us  [swap_minor(): return lax.ppermute(stack, 'width', [(i, i ^ 1) for i in range(width)])]
    unnamed x27 -> x18, local copies, waits for them, and re-layouts: 5.33 us -> 2.72 us
    ppermute x1, waiting for transfers between devices: 0.01 us -> 2.19 us  [swap_minor(): return lax.ppermute(stack, 'width', [(i, i ^ 1) for i in range(width)])]
    pallas_call x1, Pallas kernels: 1.62 us -> 0.04 us  [shards(): call(functools.partial(sum_kernel, width=width), [((ROWS, slots * LANES),...]
  transfers between devices with their start and end apart: 14 -> 14, of which waited for: 5 -> 7; matrix products, arithmetic and copies ran while one was open for 4% -> 1% of each run, Pallas kernels for 13% -> 12%
where the time goes in v3:
time: 77.7 us; the launch traced here: 77.2 us
  starting transfers between devices  32.8 us (42%)
  Pallas kernels  27.1 us (35%)
  waiting for transfers between devices  10.1 us (13%)
  local copies, waits for them, and re-layouts  2.8 us (4%)
  other arithmetic  2.37 us (3%)
  between operations  2.09 us (3%)
    ppermute x6, starting transfers between devices, shift(): lax.ppermute(x, 'width', [(i, (i + by) % peers) for i in range(peers)])  16.7 us
    pallas_call x1, Pallas kernels, shards(): call(functools.partial(second_kernel, slots=slots, pairs=local_pairs, cha...  11.9 us
    all_to_all x1, starting transfers between devices, shards(): parts = lax.all_to_all(parts, 'width', 0, 0, tiled=True)  6 us
    ppermute x3, starting transfers between devices, gather_major(): pieces.append(lax.ppermute(chunk, 'width', route))  5.55 us
    pallas_call x1, Pallas kernels, shards(): call(functools.partial(first_kernel, slots=slots, pairs=local_pairs, fold...  4.9 us
    pallas_call x1, Pallas kernels, shards(): call(window_kernel, [((tokens, LANES), bf16), ((ROWS, tokens), bf16), ((t...  4.13 us
    ppermute x3, waiting for transfers between devices, gather_major(): pieces.append(lax.ppermute(chunk, 'width', route))  3.59 us
    pallas_call x1, Pallas kernels, shards(): call(functools.partial(partial_kernel, width=width, slots=slots, local_pa...  3.34 us
  transfers between devices with their start and end apart: 14, of which 7 were waited for; matrix products, arithmetic and copies ran while one was open for 1% of the time, Pallas kernels for 12%

profile of v3, /device:TPU:0, one launch (start us, length us, event | category | flops | bytes accessed | tf_op | source)
XLA Modules:
  0.0 77.2 jit_solution(7589353015086493686)
XLA Ops:
  1.9 0.1 stack.38.place_ref
  2.0 1.0 %copy-done = bf16[64,2432]{1,0:T(8,128)(2,1)S(1)} copy-done((bf16[64,2432]{1,0:T(8,128)(2,1)S(1)}, bf16[64,2432]{1,0:T(8,128)(2,1)}, u32[]{:S(2)}) %copy-start) | copy-done | bytes 311320
  3.0 0.7 copy-done.4
  3.7 3.3 %shard_map.113 = bf16[8,72,256]{2,1,0:T(8,128)(2,1)} custom-call(s32[6]{0:T(128)S(1)} %stack.38.place_ref, f32[3,1,2432]{2,1,0:T(1,128)S(1)} %bitcast.14, bf16[64,2432]{1,0:T(8,128)(2,1)S(1)} %copy-done, bf16[304,3840]{1,0:T(8,128)(2,1)} %w_ref.3), custom_call_target="tpu_custom_call" | custom-call | bytes 1048576 | tf_op jit(solution)/shard_map/pallas_call | solution.py:420
  7.1 0.7 convert_element_type.6
  7.8 0.8 %pad_maximum_fusion.1.own_ref = f32[17,8,128]{2,1,0:T(8,128)S(1)} fusion(f32[1,8,128]{2,1,0:T(8,128)S(1)} %broadcast_in_dim.2, f32[16,8,128]{2,1,0:T(8,128)} %param.10), kind=kLoop, calls=%fused_computation.1 | loop fusion | flops 17408 | bytes 139264 | tf_op jit(solution)/shard_map/concatenate | solution.py:432
  8.6 6.0 %collective-permute-start = (f32[17,8,128]{2,1,0:T(8,128)S(1)}, f32[17,8,128]{2,1,0:T(8,128)S(1)}, u32[]{:S(2)}, u32[]{:S(2)}) collective-permute-start(f32[17,8,128]{2,1,0:T(8,128)S(1)} %pad_maximum_fusion.1.own_ref), channel_id=1, source_target_pairs={{0,14},{2,0},{4,2},{6,4},{8,6},{10,8},{12,10},{14,12},{1,15},{3,1}... | collective-permute-start | bytes 208904 | tf_op jit(solution)/shard_map/ppermute | solution.py:369
  14.6 0.0 collective-permute-start.1
  14.6 6.0 %all-to-all-start = ((bf16[8,72,256]{2,1,0:T(8,128)(2,1)}), bf16[8,72,256]{2,1,0:T(8,128)(2,1)S(1)}, u32[]{:S(2)}, u32[]{:S(2)}) async-start(bf16[8,72,256]{2,1,0:T(8,128)(2,1)} %shard_map.113), calls=%async_computation | async-start | bytes 589824 | tf_op jit(solution)/shard_map/all_to_all | solution.py:439
  20.6 0.8 %convert_element_type.7 = bf16[16,8,128]{2,1,0:T(8,128)(2,1)S(1)} convert(f32[16,8,128]{2,1,0:T(8,128)} %param.10) | non-fusion elementwise | flops 16384 | bytes 98304 | tf_op jit(solution)/shard_map/convert_element_type | solution.py:436
  21.5 3.8 %collective-permute-start.2 = (bf16[16,8,128]{2,1,0:T(8,128)(2,1)S(1)}, bf16[16,8,128]{2,1,0:T(8,128)(2,1)S(1)}, u32[]{:S(2)}, u32[]{:S(2)}) collective-permute-start(bf16[16,8,128]{2,1,0:T(8,128)(2,1)S(1)} %convert_element_type.7), channel_id=1, source_target_pairs={{0,12},{2,14},{4,0},{6,2},{8,4},{10,6},{12,8},{14,10},{1,13},{3,15... | collective-permute-start | bytes 98312 | tf_op jit(solution)/shard_map/ppermute | solution.py:369
  25.3 1.6 %collective-permute-done.2.further_ref = bf16[16,8,128]{2,1,0:T(8,128)(2,1)S(1)} collective-permute-done((bf16[16,8,128]{2,1,0:T(8,128)(2,1)S(1)}, bf16[16,8,128]{2,1,0:T(8,128)(2,1)S(1)}, u32[]{:S(2)}, u32[]{:S(2)}) %collective-permute-start.2) | collective-permute-done | bytes 32800 | tf_op jit(solution)/shard_map/ppermute | solution.py:369
  26.9 0.0 collective-permute-done.right_ref
  26.9 0.0 collective-permute-done.1.left_ref
  26.9 1.0 %copy-done.1 = bf16[64,2432]{1,0:T(8,128)(2,1)S(1)} copy-done((bf16[64,2432]{1,0:T(8,128)(2,1)S(1)}, bf16[64,2432]{1,0:T(8,128)(2,1)}, u32[]{:S(2)}) %copy-start.1) | copy-done | bytes 311320
  27.9 4.1 %shard_map.114 = (bf16[512,128]{1,0:T(8,128)(2,1)S(1)}, bf16[72,512]{1,0:T(8,128)(2,1)S(1)}, f32[512,128]{1,0:T(8,128)S(1)}, f32[8,512]{1,0:T(8,128)S(1)}, f32[5...) custom-call(s32[6]{0:T(128)S(1)} %stack.38.place_ref, f32[17,8,128]{2,1,0:T(8,128)S(1)} %pad_maximum_fusion.1.own_ref, ...), custom_call_target="tpu_custom_call" | custom-call | flops 5000000000 | bytes 1048576 | tf_op jit(solution)/shard_map/pallas_call | solution.py:442
  32.0 0.0 all-to-all-done.parts_ref
  32.0 0.0 slice-start
  32.1 4.3 %collective-permute-start.5 = (bf16[72,256]{1,0:T(8,128)(2,1)S(1)}, bf16[72,256]{1,0:T(8,128)(2,1)S(1)}, u32[]{:S(2)}, u32[]{:S(2)}) collective-permute-start(bf16[72,256]{1,0:T(8,128)(2,1)S(1)} %shard_map.115), channel_id=1, source_target_pairs={{0,12},{2,14},{4,8},{6,10},{8,4},{10,6},{12,0},{14,2},{1,13},{3,15... | collective-permute-start | bytes 110600 | tf_op jit(solution)/shard_map/ppermute | solution.py:385
  36.4 0.0 collective-permute-start.3
  36.4 1.3 %collective-permute-start.4 = (bf16[72,256]{1,0:T(8,128)(2,1)S(1)}, bf16[72,256]{1,0:T(8,128)(2,1)S(1)}, u32[]{:S(2)}, u32[]{:S(2)}) collective-permute-start(bf16[72,256]{1,0:T(8,128)(2,1)S(1)} %shard_map.115), channel_id=1, source_target_pairs={{0,8},{2,10},{4,12},{6,14},{8,0},{10,2},{12,4},{14,6},{1,9},{3,11}... | collective-permute-start | bytes 110600 | tf_op jit(solution)/shard_map/ppermute | solution.py:385
  37.6 0.8 %collective-permute-done.5 = bf16[72,256]{1,0:T(8,128)(2,1)S(1)} collective-permute-done((bf16[72,256]{1,0:T(8,128)(2,1)S(1)}, bf16[72,256]{1,0:T(8,128)(2,1)S(1)}, u32[]{:S(2)}, u32[]{:S(2)}) %collective-permute-start.5) | collective-permute-done | bytes 36896 | tf_op jit(solution)/shard_map/ppermute | solution.py:385
  38.4 1.9 %collective-permute-done.3 = bf16[72,256]{1,0:T(8,128)(2,1)S(1)} collective-permute-done((bf16[72,256]{1,0:T(8,128)(2,1)S(1)}, bf16[72,256]{1,0:T(8,128)(2,1)S(1)}, u32[]{:S(2)}, u32[]{:S(2)}) %collective-permute-start.3) | collective-permute-done | bytes 36896 | tf_op jit(solution)/shard_map/ppermute | solution.py:385
  40.3 0.9 %collective-permute-done.4 = bf16[72,256]{1,0:T(8,128)(2,1)S(1)} collective-permute-done((bf16[72,256]{1,0:T(8,128)(2,1)S(1)}, bf16[72,256]{1,0:T(8,128)(2,1)S(1)}, u32[]{:S(2)}, u32[]{:S(2)}) %collective-permute-start.4) | collective-permute-done | bytes 36896 | tf_op jit(solution)/shard_map/ppermute | solution.py:385
  41.2 1.5 %collective-permute-start.7 = (bf16[4,72,256]{2,1,0:T(8,128)(2,1)S(1)}, bf16[4,72,256]{2,1,0:T(8,128)(2,1)S(1)}, u32[]{:S(2)}, u32[]{:S(2)}) collective-permute-start(bf16[4,72,256]{2,1,0:T(8,128)(2,1)S(1)} %pad_maximum_fusion.near_ref), channel_id=1, source_target_pairs={{0,2},{2,0},{4,6},{6,4},{8,10},{10,8},{12,14},{14,12},{1,3},{3,1},... | collective-permute-start | bytes 442376 | tf_op jit(solution)/shard_map/ppermute | solution.py:393
  42.8 1.5 %collective-permute-start.6 = (bf16[4,72,256]{2,1,0:T(8,128)(2,1)S(1)}, bf16[4,72,256]{2,1,0:T(8,128)(2,1)S(1)}, u32[]{:S(2)}, u32[]{:S(2)}) collective-permute-start(bf16[4,72,256]{2,1,0:T(8,128)(2,1)S(1)} %pad_maximum_fusion.near_ref), channel_id=1, source_target_pairs={{0,16},{16,0},{1,17},{17,1},{2,18},{18,2},{3,19},{19,3},{4,20},{20... | collective-permute-start | bytes 442376 | tf_op jit(solution)/shard_map/ppermute | solution.py:373
  44.3 2.2 %collective-permute-done.7.far_ref = bf16[4,72,256]{2,1,0:T(8,128)(2,1)S(1)} collective-permute-done((bf16[4,72,256]{2,1,0:T(8,128)(2,1)S(1)}, bf16[4,72,256]{2,1,0:T(8,128)(2,1)S(1)}, u32[]{:S(2)}, u32[]{:S(2)}) %collective-permute-start.7) | collective-permute-done | bytes 147488 | tf_op jit(solution)/shard_map/ppermute | solution.py:393
  46.4 1.5 %collective-permute-start.8 = (bf16[4,72,256]{2,1,0:T(8,128)(2,1)S(1)}, bf16[4,72,256]{2,1,0:T(8,128)(2,1)S(1)}, u32[]{:S(2)}, u32[]{:S(2)}) collective-permute-start(bf16[4,72,256]{2,1,0:T(8,128)(2,1)S(1)} %collective-permute-done.7.far_ref), channel_id=1, source_target_pairs={{0,16},{16,0},{1,17},{17,1},{2,18},{18,2},{3,19},{19,3},{4,20},{20... | collective-permute-start | bytes 442376 | tf_op jit(solution)/shard_map/ppermute | solution.py:373
  47.9 4.9 %shard_map.116.att_ref = bf16[512,640]{1,0:T(8,128)(2,1)S(1)} custom-call(s32[6]{0:T(128)S(1)} %stack.38.place_ref, bf16[4,72,256]{2,1,0:T(8,128)(2,1)S(1)} %pad_maximum_fusion.near_ref, bf16[4,72,256]{2,1,0:T(8,128)(2,1)S(1)} %collective-permute-done.7.far_ref, bf16[512,128]{1,0:T(8,128)(2,1)S(1)} %get-tuple-element.24.x_ref, ...), custom_call_target="tpu_custom_call" | custom-call | flops 6000000000 | bytes 1048576 | tf_op jit(solution)/shard_map/pallas_call | solution.py:465
  52.8 0.0 collective-permute-done.6.near_ref
  52.9 0.0 collective-permute-done.8.far_ref
  52.9 0.0 slice-done
  52.9 0.0 copy-done.2
  52.9 0.0 copy-done.5
  52.9 0.0 slice-done.1
  52.9 0.0 copy-done.6
  52.9 0.0 copy-start.3
  52.9 11.9 %shard_map.117 = (f32[5,16,256]{2,1,0:T(8,128)S(1)}, bf16[5,16,256]{2,1,0:T(8,128)(2,1)S(1)}) custom-call(s32[6]{0:T(128)S(1)} %stack.38.place_ref, bf16[4,72,256]{2,1,0:T(8,128)(2,1)S(1)} %collective-permute-done.6.near_ref, bf16[4,72,256]{2,1,0:T(8,128)(2,1)S(1)} %collective-permute-done.8.far_ref, bf16[512,128]{1,0:T(8,128)(2,1)S(1)} %get-tuple-element.24.x_ref, ...), custom_call_target="tpu_custom_call" | custom-call | flops 12000000000 | bytes 1048576 | tf_op jit(solution)/shard_map/pallas_call | solution.py:470
  64.9 0.1 collective-permute-start.9
  64.9 1.2 %collective-permute-done.9.theirs_ref = bf16[5,16,256]{2,1,0:T(8,128)(2,1)S(1)} collective-permute-done((bf16[5,16,256]{2,1,0:T(8,128)(2,1)S(1)}, bf16[5,16,256]{2,1,0:T(8,128)(2,1)S(1)}, u32[]{:S(2)}, u32[]{:S(2)}) %collective-permute-start.9) | collective-permute-done | bytes 40992 | tf_op jit(solution)/shard_map/ppermute | solution.py:373
  66.2 0.8 %shard_map.118 = (f32[80,256]{1,0:T(8,128)S(1)}, bf16[80,256]{1,0:T(8,128)(2,1)S(1)}, bf16[80,256]{1,0:T(8,128)(2,1)S(1)}, bf16[80,128]{1,0:T(8,128)(2,1)S(1)}) custom-call(s32[6]{0:T(128)S(1)} %stack.38.place_ref, f32[5,16,256]{2,1,0:T(8,128)S(1)} %get-tuple-element.28.mine_ref, bf16[5,16,256]{2,1,0:T(8,128)(2,1)S(1)} %collective-permute-done.9.theirs_ref), custom_call_target="tpu_custom_call" | custom-call | bytes 1048576 | tf_op jit(solution)/shard_map/pallas_call | solution.py:486
  67.0 1.5 %collective-permute-start.10 = (bf16[80,256]{1,0:T(8,128)(2,1)S(1)}, bf16[80,256]{1,0:T(8,128)(2,1)S(1)}, u32[]{:S(2)}, u32[]{:S(2)}) collective-permute-start(bf16[80,256]{1,0:T(8,128)(2,1)S(1)} %get-tuple-element.31), channel_id=1, source_target_pairs={{0,2},{2,4},{4,6},{6,8},{8,10},{10,12},{12,14},{14,0},{1,3},{3,5},... | collective-permute-start | bytes 122888 | tf_op jit(solution)/shard_map/ppermute | solution.py:369
  68.5 2.0 %collective-permute-start.11 = (bf16[80,256]{1,0:T(8,128)(2,1)S(1)}, bf16[80,256]{1,0:T(8,128)(2,1)S(1)}, u32[]{:S(2)}, u32[]{:S(2)}) collective-permute-start(bf16[80,256]{1,0:T(8,128)(2,1)S(1)} %get-tuple-element.32), channel_id=1, source_target_pairs={{0,4},{2,6},{4,8},{6,10},{8,12},{10,14},{12,0},{14,2},{1,5},{3,7},... | collective-permute-start | bytes 122888 | tf_op jit(solution)/shard_map/ppermute | solution.py:369
  70.5 3.3 %collective-permute-start.12 = (bf16[80,128]{1,0:T(8,128)(2,1)S(1)}, bf16[80,128]{1,0:T(8,128)(2,1)S(1)}, u32[]{:S(2)}, u32[]{:S(2)}) collective-permute-start(bf16[80,128]{1,0:T(8,128)(2,1)S(1)} %get-tuple-element.33), channel_id=1, source_target_pairs={{0,14},{2,0},{4,2},{6,4},{8,6},{10,8},{12,10},{14,12},{1,15},{3,1}... | collective-permute-start | bytes 61448 | tf_op jit(solution)/shard_map/ppermute | solution.py:369
  73.8 1.5 %collective-permute-done.12.back_ref = bf16[80,128]{1,0:T(8,128)(2,1)S(1)} collective-permute-done((bf16[80,128]{1,0:T(8,128)(2,1)S(1)}, bf16[80,128]{1,0:T(8,128)(2,1)S(1)}, u32[]{:S(2)}, u32[]{:S(2)}) %collective-permute-start.12) | collective-permute-done | bytes 20512 | tf_op jit(solution)/shard_map/ppermute | solution.py:369
  75.2 0.0 collective-permute-done.10.one_ref
  75.2 0.0 collective-permute-done.11.two_ref
  75.2 2.0 %shard_map.119 = (f32[16,4,128]{2,1,0:T(4,128)}, bf16[4,128,512]{2,1,0:T(8,128)(2,1)}) custom-call(s32[6]{0:T(128)S(1)} %stack.38.place_ref, f32[80,256]{1,0:T(8,128)S(1)} %get-tuple-element.30.own_ref, bf16[80,256]{1,0:T(8,128)(2,1)S(1)} %collective-permute-done.10.one_ref, bf16[80,256]{1,0:T(8,128)(2,1)S(1)} %collective-permute-done.11.two_ref, ...), custom_call_target="tpu_custom_call" | custom-call | bytes 1048576 | tf_op jit(solution)/shard_map/pallas_call | solution.py:497
  (12 shorter events, 0.1 us)
Async XLA Ops:
  2.0 1.0 %copy-start = (bf16[64,2432]{1,0:T(8,128)(2,1)S(1)}, bf16[64,2432]{1,0:T(8,128)(2,1)}, u32[]{:S(2)}) copy-start(bf16[64,2432]{1,0:T(8,128)(2,1)} %wp_ref.3) | copy-start | bytes 933892
  3.0 0.7 copy-start.4
  8.6 18.3 %collective-permute-start = (f32[17,8,128]{2,1,0:T(8,128)S(1)}, f32[17,8,128]{2,1,0:T(8,128)S(1)}, u32[]{:S(2)}, u32[]{:S(2)}) collective-permute-start(f32[17,8,128]{2,1,0:T(8,128)S(1)} %pad_maximum_fusion.1.own_ref), channel_id=1, source_target_pairs={{0,14},{2,0},{4,2},{6,4},{8,6},{10,8},{12,10},{14,12},{1,15},{3,1}... | collective-permute-start | bytes 208904 | tf_op jit(solution)/shard_map/ppermute | solution.py:369
  14.6 12.3 %collective-permute-start.1 = (f32[17,8,128]{2,1,0:T(8,128)S(1)}, f32[17,8,128]{2,1,0:T(8,128)S(1)}, u32[]{:S(2)}, u32[]{:S(2)}) collective-permute-start(f32[17,8,128]{2,1,0:T(8,128)S(1)} %pad_maximum_fusion.1.own_ref), channel_id=1, source_target_pairs={{0,2},{2,4},{4,6},{6,8},{8,10},{10,12},{12,14},{14,0},{1,3},{3,5},... | collective-permute-start | bytes 208904 | tf_op jit(solution)/shard_map/ppermute | solution.py:369
  14.6 17.4 %all-to-all-start = ((bf16[8,72,256]{2,1,0:T(8,128)(2,1)}), bf16[8,72,256]{2,1,0:T(8,128)(2,1)S(1)}, u32[]{:S(2)}, u32[]{:S(2)}) async-start(bf16[8,72,256]{2,1,0:T(8,128)(2,1)} %shard_map.113), calls=%async_computation | async-start | bytes 589824 | tf_op jit(solution)/shard_map/all_to_all | solution.py:439
  21.5 5.4 %collective-permute-start.2 = (bf16[16,8,128]{2,1,0:T(8,128)(2,1)S(1)}, bf16[16,8,128]{2,1,0:T(8,128)(2,1)S(1)}, u32[]{:S(2)}, u32[]{:S(2)}) collective-permute-start(bf16[16,8,128]{2,1,0:T(8,128)(2,1)S(1)} %convert_element_type.7), channel_id=1, source_target_pairs={{0,12},{2,14},{4,0},{6,2},{8,4},{10,6},{12,8},{14,10},{1,13},{3,15... | collective-permute-start | bytes 98312 | tf_op jit(solution)/shard_map/ppermute | solution.py:369
  26.9 1.0 %copy-start.1 = (bf16[64,2432]{1,0:T(8,128)(2,1)S(1)}, bf16[64,2432]{1,0:T(8,128)(2,1)}, u32[]{:S(2)}) copy-start(bf16[64,2432]{1,0:T(8,128)(2,1)} %wp_ref.3) | copy-start | bytes 933892
  32.0 20.9 %slice-start = ((s8[6225920]{0:T(1024)(128)(4,1)}), s8[4194304]{0:T(1024)(128)(4,1)S(1)}, s32[]{:S(2)}) async-start(s8[6225920]{0:T(1024)(128)(4,1)} %bitcast.16), calls=%async_computation.1 | async-start | bytes 8388608
  32.1 6.3 %collective-permute-start.5 = (bf16[72,256]{1,0:T(8,128)(2,1)S(1)}, bf16[72,256]{1,0:T(8,128)(2,1)S(1)}, u32[]{:S(2)}, u32[]{:S(2)}) collective-permute-start(bf16[72,256]{1,0:T(8,128)(2,1)S(1)} %shard_map.115), channel_id=1, source_target_pairs={{0,12},{2,14},{4,8},{6,10},{8,4},{10,6},{12,0},{14,2},{1,13},{3,15... | collective-permute-start | bytes 110600 | tf_op jit(solution)/shard_map/ppermute | solution.py:385
  36.4 4.0 %collective-permute-start.3 = (bf16[72,256]{1,0:T(8,128)(2,1)S(1)}, bf16[72,256]{1,0:T(8,128)(2,1)S(1)}, u32[]{:S(2)}, u32[]{:S(2)}) collective-permute-start(bf16[72,256]{1,0:T(8,128)(2,1)S(1)} %shard_map.115), channel_id=1, source_target_pairs={{0,4},{2,6},{4,0},{6,2},{8,12},{10,14},{12,8},{14,10},{1,5},{3,7},... | collective-permute-start | bytes 110600 | tf_op jit(solution)/shard_map/ppermute | solution.py:385
  36.4 4.9 %collective-permute-start.4 = (bf16[72,256]{1,0:T(8,128)(2,1)S(1)}, bf16[72,256]{1,0:T(8,128)(2,1)S(1)}, u32[]{:S(2)}, u32[]{:S(2)}) collective-permute-start(bf16[72,256]{1,0:T(8,128)(2,1)S(1)} %shard_map.115), channel_id=1, source_target_pairs={{0,8},{2,10},{4,12},{6,14},{8,0},{10,2},{12,4},{14,6},{1,9},{3,11}... | collective-permute-start | bytes 110600 | tf_op jit(solution)/shard_map/ppermute | solution.py:385
  41.2 5.2 %collective-permute-start.7 = (bf16[4,72,256]{2,1,0:T(8,128)(2,1)S(1)}, bf16[4,72,256]{2,1,0:T(8,128)(2,1)S(1)}, u32[]{:S(2)}, u32[]{:S(2)}) collective-permute-start(bf16[4,72,256]{2,1,0:T(8,128)(2,1)S(1)} %pad_maximum_fusion.near_ref), channel_id=1, source_target_pairs={{0,2},{2,0},{4,6},{6,4},{8,10},{10,8},{12,14},{14,12},{1,3},{3,1},... | collective-permute-start | bytes 442376 | tf_op jit(solution)/shard_map/ppermute | solution.py:393
  42.8 10.1 %collective-permute-start.6 = (bf16[4,72,256]{2,1,0:T(8,128)(2,1)S(1)}, bf16[4,72,256]{2,1,0:T(8,128)(2,1)S(1)}, u32[]{:S(2)}, u32[]{:S(2)}) collective-permute-start(bf16[4,72,256]{2,1,0:T(8,128)(2,1)S(1)} %pad_maximum_fusion.near_ref), channel_id=1, source_target_pairs={{0,16},{16,0},{1,17},{17,1},{2,18},{18,2},{3,19},{19,3},{4,20},{20... | collective-permute-start | bytes 442376 | tf_op jit(solution)/shard_map/ppermute | solution.py:373
  46.4 6.4 %collective-permute-start.8 = (bf16[4,72,256]{2,1,0:T(8,128)(2,1)S(1)}, bf16[4,72,256]{2,1,0:T(8,128)(2,1)S(1)}, u32[]{:S(2)}, u32[]{:S(2)}) collective-permute-start(bf16[4,72,256]{2,1,0:T(8,128)(2,1)S(1)} %collective-permute-done.7.far_ref), channel_id=1, source_target_pairs={{0,16},{16,0},{1,17},{17,1},{2,18},{18,2},{3,19},{19,3},{4,20},{20... | collective-permute-start | bytes 442376 | tf_op jit(solution)/shard_map/ppermute | solution.py:373
  47.9 4.9 %copy-start.2 = (bf16[64,2432]{1,0:T(8,128)(2,1)S(1)}, bf16[64,2432]{1,0:T(8,128)(2,1)}, u32[]{:S(2)}) copy-start(bf16[64,2432]{1,0:T(8,128)(2,1)} %wp_ref.3) | copy-start | bytes 933892
  47.9 5.0 %copy-start.5 = (f32[1,3,2432]{2,0,1:T(1,128)S(1)}, f32[1,3,2432]{2,0,1:T(1,128)}, u32[]{:S(2)}) copy-start(f32[1,3,2432]{2,0,1:T(1,128)} %param.14) | copy-start | bytes 87556
  47.9 5.0 %slice-start.1 = ((s8[6225920]{0:T(1024)(128)(4,1)}), s8[2031616]{0:T(1024)(128)(4,1)S(1)}, s32[]{:S(2)}) async-start(s8[6225920]{0:T(1024)(128)(4,1)} %bitcast.16), calls=%async_computation.2 | async-start | bytes 4063232
  47.9 5.0 %copy-start.6 = (bf16[2432,64]{0,1:T(8,128)(2,1)S(1)}, bf16[2432,64]{0,1:T(8,128)(2,1)}, u32[]{:S(2)}) copy-start(bf16[2432,64]{0,1:T(8,128)(2,1)} %param.18) | copy-start | bytes 933892
  52.9 22.3 %copy-start.3 = (bf16[144,512]{1,0:T(8,128)(2,1)S(1)}, bf16[144,512]{1,0:T(8,128)(2,1)}, u32[]{:S(2)}) copy-start(bf16[144,512]{1,0:T(8,128)(2,1)} %w_ref.5) | copy-start | bytes 442372
  64.9 1.3 %collective-permute-start.9 = (bf16[5,16,256]{2,1,0:T(8,128)(2,1)S(1)}, bf16[5,16,256]{2,1,0:T(8,128)(2,1)S(1)}, u32[]{:S(2)}, u32[]{:S(2)}) collective-permute-start(bf16[5,16,256]{2,1,0:T(8,128)(2,1)S(1)} %get-tuple-element.29), channel_id=1, source_target_pairs={{0,1},{1,0},{2,3},{3,2},{4,5},{5,4},{6,7},{7,6},{8,9},{9,8},{10,11... | collective-permute-start | bytes 122888 | tf_op jit(solution)/shard_map/ppermute | solution.py:373
  67.0 8.3 %collective-permute-start.10 = (bf16[80,256]{1,0:T(8,128)(2,1)S(1)}, bf16[80,256]{1,0:T(8,128)(2,1)S(1)}, u32[]{:S(2)}, u32[]{:S(2)}) collective-permute-start(bf16[80,256]{1,0:T(8,128)(2,1)S(1)} %get-tuple-element.31), channel_id=1, source_target_pairs={{0,2},{2,4},{4,6},{6,8},{8,10},{10,12},{12,14},{14,0},{1,3},{3,5},... | collective-permute-start | bytes 122888 | tf_op jit(solution)/shard_map/ppermute | solution.py:369
  68.5 6.8 %collective-permute-start.11 = (bf16[80,256]{1,0:T(8,128)(2,1)S(1)}, bf16[80,256]{1,0:T(8,128)(2,1)S(1)}, u32[]{:S(2)}, u32[]{:S(2)}) collective-permute-start(bf16[80,256]{1,0:T(8,128)(2,1)S(1)} %get-tuple-element.32), channel_id=1, source_target_pairs={{0,4},{2,6},{4,8},{6,10},{8,12},{10,14},{12,0},{14,2},{1,5},{3,7},... | collective-permute-start | bytes 122888 | tf_op jit(solution)/shard_map/ppermute | solution.py:369
  70.5 4.7 %collective-permute-start.12 = (bf16[80,128]{1,0:T(8,128)(2,1)S(1)}, bf16[80,128]{1,0:T(8,128)(2,1)S(1)}, u32[]{:S(2)}, u32[]{:S(2)}) collective-permute-start(bf16[80,128]{1,0:T(8,128)(2,1)S(1)} %get-tuple-element.33), channel_id=1, source_target_pairs={{0,14},{2,0},{4,2},{6,4},{8,6},{10,8},{12,10},{14,12},{1,15},{3,1}... | collective-permute-start | bytes 61448 | tf_op jit(solution)/shard_map/ppermute | solution.py:369

commit v4 on v3

--- a/solution.py
+++ b/solution.py
@@ -55,17 +55,21 @@
 
 
 def partial_kernel(
-    place_ref, mod_ref, wp_ref, w_ref, out_ref, w_buf, sems, *, width, slots, local_pairs, features
+    place_ref, mod_ref, wp_ref, w_ref, *refs, width, slots, local_pairs, features, fold, direct
 ):
+    *out_refs, w_buf, mod_buf, wp_buf, sems = refs
     group = place_ref[0]
     span = local_pairs * LANES
-    copies = []
+    loads = [
+        pltpu.make_async_copy(wp_ref, wp_buf, sems.at[0]),
+        pltpu.make_async_copy(mod_ref, mod_buf, sems.at[1]),
+    ]
     for part in range(3):
         start = pl.multiple_of(part * features + group * span, LANES)
-        copies.append(
-            pltpu.make_async_copy(w_ref.at[:, pl.ds(start, span)], w_buf.at[part], sems.at[part])
+        loads.append(
+            pltpu.make_async_copy(w_ref.at[:, pl.ds(start, span)], w_buf.at[part], sems.at[2 + part])
         )
-    for one in copies:
+    for one in loads:
         one.start()
     feats, model = wp_ref.shape
     rows = w_buf.shape[1]
@@ -73,26 +77,42 @@
     begin = place_ref[3] * rows
     low = jnp.minimum(begin // LANES * LANES, model - window)
     cols = pl.ds(pl.multiple_of(low, LANES), window)
-    mean = jnp.sum(wp_ref[...].astype(f32), axis=1, keepdims=True) * (1.0 / model)
-    centered = wp_ref[:, cols].astype(f32) - mean
-    scaled = centered * (1.0 + mod_ref[1, :, cols])
+    loads[0].wait()
+    loads[1].wait()
+    mean = jnp.sum(wp_buf[...].astype(f32), axis=1, keepdims=True) * (1.0 / model)
+    centered = wp_buf[:, cols].astype(f32) - mean
+    scaled = centered * (1.0 + mod_buf[1, :, cols])
     down = iota((ROWS - feats, window), 0)
-    tail = jnp.where(down < 2, jnp.broadcast_to(mod_ref[0, :, cols], down.shape), 0.0)
+    tail = jnp.where(down < 2, jnp.broadcast_to(mod_buf[0, :, cols], down.shape), 0.0)
     stacked = jnp.concatenate([scaled, tail], axis=0)
     stacked = pltpu.roll(stacked, (window - (begin - low)) % window, 1)
     a = jnp.concatenate(split(stacked), axis=0)[:, :rows]
-    for one in copies:
+    for one in loads[2:]:
         one.wait()
+    side = place_ref[3] % fold
     for owner in range(width):
+        pieces = []
         for slot in range(slots):
             tile = owner * slots + slot
             if tile < 3 * local_pairs:
                 pair, sub = divmod(tile, 3)
                 both = dot(a, w_buf[PARTS[sub], :, pair * LANES : (pair + 1) * LANES])
-                value = (both[:ROWS] + both[ROWS:]).astype(bf16)
+                pieces.append(both[:ROWS] + both[ROWS:])
             else:
-                value = jnp.zeros((ROWS, LANES), bf16)
-            out_ref[owner, :, slot * LANES : (slot + 1) * LANES] = value
+                pieces.append(jnp.zeros((ROWS, LANES), f32))
+        value = jnp.concatenate(pieces, axis=1)
+        if not direct:
+            out_refs[0][owner] = value.astype(bf16)
+            continue
+        z, y = divmod(owner, fold)
+
+        @pl.when(side == y)
+        def _():
+            out_refs[0][z] = value
+
+        @pl.when(side != y)
+        def _():
+            out_refs[1][z] = value.astype(bf16)
 
 
 def sum_kernel(parts_ref, out_ref, *, width):
@@ -102,21 +122,36 @@
     out_ref[...] = total.astype(bf16)
 
 
+def first_sum_kernel(place_ref, keep_ref, came_ref, own_ref, *send_refs):
+    key = place_ref[5]
+    own_ref[...] = keep_ref[key] + came_ref[key].astype(f32)
+    for d, ref in enumerate(send_refs):
+        at = key ^ (d + 1)
+        ref[...] = (keep_ref[at] + came_ref[at].astype(f32)).astype(bf16)
+
+
+def last_sum_kernel(*refs):
+    *parts, out_ref = refs
+    total = parts[0][...]
+    for ref in parts[1:]:
+        total = total + ref[...].astype(f32)
+    out_ref[...] = total.astype(bf16)
+
+
 def window_kernel(
-    place_ref, own_ref, right_ref, left_ref, further_ref, w_ref,
-    x_ref, xt_ref, var_ref, varrow_ref, lat_ref, count_ref,
-    rows_buf, xt_buf, hid_buf,
+    place_ref, own_ref, right_ref, further_ref, wp_ref,
+    x_ref, xt_ref, var_ref, varrow_ref,
+    rows_buf, xt_buf, hid_buf, w_ref, sem,
 ):
-    channels, height, columns = own_ref.shape[0] - 1, own_ref.shape[1], own_ref.shape[2]
+    load = pltpu.make_async_copy(wp_ref, w_ref, sem.at[0])
+    load.start()
+    channels, height, columns = own_ref.shape
     offset = place_ref[1]
-    guide = place_ref[2]
-    near = height // 2 + 1
-    lane = iota((channels, LANES), 1)
     for r in range(height):
         at = slice(r * channels, (r + 1) * channels)
-        rows_buf[at, :columns] = own_ref[:channels, r, :].astype(bf16)
-        rows_buf[at, columns : 2 * columns] = right_ref[:channels, r, :].astype(bf16)
-        rows_buf[at, 2 * columns :] = further_ref[:, r, :]
+        rows_buf[at, :columns] = own_ref[:, r, :].astype(bf16)
+        rows_buf[at, columns : 2 * columns] = right_ref[:, r, :].astype(bf16)
+        rows_buf[at, 2 * columns :] = further_ref[:, r, :].astype(bf16)
     col = iota((3 * columns, 2 * columns), 0)
     spot = iota((3 * columns, 2 * columns), 1)
     b = (spot >= columns).astype(jnp.int32)
@@ -137,6 +172,7 @@
     model = w_ref.shape[1]
     block = 64
     x_bf = xrow[:, :feats].astype(bf16)
+    load.wait()
     hid_buf[...] = dot(x_bf, w_ref[...])
 
     def stats(i, carry):
@@ -161,18 +197,6 @@
     down = iota((8, tokens), 0)
     tail = jnp.where(down == 0, hi_t.astype(f32), jnp.where(down == 1, lo_t.astype(f32), 0.0))
     xt_ref[...] = jnp.concatenate([xt, tail], axis=0).astype(bf16)
-    first = guide * (near - 2)
-    for i in range(near):
-        r = pl.ds(first + i, 1)
-        lat_ref[i, :, :columns] = own_ref[:channels, r, :].reshape(channels, columns)
-        before = pltpu.roll(left_ref[:channels, r, :].reshape(channels, columns), 1, 1)
-        after = pltpu.roll(right_ref[:channels, r, :].reshape(channels, columns), 1, 1)
-        lat_ref[i, :, columns:] = jnp.where(lane == 0, before, jnp.where(lane == 1, after, 0.0))
-    lane8 = iota((height, LANES), 1)
-    count_ref[:, :columns] = own_ref[channels]
-    before = pltpu.roll(left_ref[channels], 1, 1)
-    after = pltpu.roll(right_ref[channels], 1, 1)
-    count_ref[:, columns:] = jnp.where(lane8 == 0, before, jnp.where(lane8 == 1, after, 1.0))
 
 
 def attend_pairs(place_ref, near_ref, far_ref, x_ref, xt_ref, var_ref, varrow_ref, put, slots, pairs, fold):
@@ -297,13 +321,15 @@
                     send_ref[r - give, :, b * columns : (b + 1) * columns] = piece.astype(bf16)
 
 
-def spread_kernel(place_ref, mine_ref, theirs_ref, own_ref, one_ref, two_ref, back_ref):
+def spread_kernel(place_ref, mine_ref, theirs_ref, lat_ref, own_ref, one_ref, two_ref, back_ref):
     offset = place_ref[1]
     guide = place_ref[2]
     near, channels, wide = mine_ref.shape
     columns = wide // 2
-    mine = mine_ref[...].reshape(near * channels, wide)
-    theirs = theirs_ref[...].reshape(near * channels, wide).astype(f32)
+    flat = near * channels
+    first = guide * (near - 2)
+    mine = mine_ref[...].reshape(flat, wide)
+    theirs = theirs_ref[...].reshape(flat, wide).astype(f32)
     cond = jnp.where(guide == 0, mine, theirs)
     plain = jnp.where(guide == 0, theirs, mine)
     guided = plain + guidance * (cond - plain)
@@ -314,15 +340,42 @@
     col = offset + 2 * (spot - b * columns) + b
     target = jnp.where(lane < columns, lane, jnp.where(lane == columns, -1, lane - 1))
     target = jnp.where(lane > columns + 1, -4 * wide, target)
+    edge = iota((flat, columns), 1)
 
     def place(distance):
         return jnp.where(col == target + distance * columns, 1.0, 0.0).astype(bf16)
 
+    def flagged(values, distance):
+        for at, column in ((2, distance * columns - 1), (3, (distance + 1) * columns)):
+            covered = jnp.logical_and(column >= offset, column < offset + wide)
+            values = jnp.where(edge == at, jnp.where(covered, 1.0, 0.0), values)
+        return values
+
+    latent = jnp.concatenate(
+        [lat_ref[:, pl.ds(first + i, 1), :].reshape(channels, columns) for i in range(near)], axis=0
+    )
+    top = latent.astype(bf16).astype(f32)
+    middle = (latent - top).astype(bf16).astype(f32)
+    bottom = latent - top - middle
+
+    def border(values, column):
+        for at, part in enumerate((top, middle, bottom)):
+            moved = pltpu.roll(part, (4 + at - column) % columns, 1)
+            values = jnp.where(edge == 4 + at, moved, values)
+        return values
+
     here = place(0)
-    own_ref[...] = dot(high, here) + dot(low, here)
-    one_ref[...] = dot(high, place(1)).astype(bf16)
-    two_ref[...] = dot(high, place(2)).astype(bf16)
-    back_ref[...] = dot(high, place(-1)[:, columns:]).astype(bf16)
+    own = dot(high, here) + dot(low, here)
+    own_ref[:, :columns] = own[:, :columns]
+    own_ref[:, columns:] = flagged(own[:, columns:], 0)
+    one = dot(high, place(1))
+    one_ref[:, :columns] = one[:, :columns].astype(bf16)
+    one_ref[:, columns:] = border(flagged(one[:, columns:], 1), columns - 1).astype(bf16)
+    two = dot(high, place(2))
+    two_ref[:, :columns] = two[:, :columns].astype(bf16)
+    two_ref[:, columns:] = flagged(two[:, columns:], 2).astype(bf16)
+    back = dot(high, place(-1)[:, columns:])
+    back_ref[...] = border(flagged(back, -1), 0).astype(bf16)
 
 
 def decode_kernel(
@@ -331,21 +384,28 @@
 ):
     guide = place_ref[2]
     place = place_ref[3]
-    near, channels, wide = lat_ref.shape
-    columns = wide // 2
-    fraction = (jnp.full((1, wide), place_ref[4], jnp.int32).astype(f32) + 1.0) / STEPS
+    channels, height, columns = lat_ref.shape
+    half = height // 2
+    near = half + 1
+    flat = near * channels
+    first = guide * (near - 2)
+    fraction = (jnp.full((1, columns), place_ref[4], jnp.int32).astype(f32) + 1.0) / STEPS
     sigma = 3.0 * fraction / (1.0 + 2.0 * fraction)
-    total = own_ref[...] + one_ref[...].astype(f32) + two_ref[...].astype(f32)
-    back = jnp.concatenate([jnp.zeros(back_ref.shape, f32), back_ref[...].astype(f32)], axis=1)
-    velocity = (total + back) / count_ref[:1, :]
-    clean = lat_ref[...].reshape(near * channels, wide) - sigma * velocity
-    half = near - 1
-    first = guide
-    lane = iota((near * channels, columns), 1)
-    main = clean[:, :columns]
-    edges = clean[:, columns:]
-    left = jnp.where(place == 0, 0.0, edges[:, 0:1])
-    right = jnp.where(place == width - 1, 0.0, edges[:, 1:2])
+    one = one_ref[...].astype(f32)
+    back = back_ref[...].astype(f32)
+    total = own_ref[...] + one + two_ref[...].astype(f32)
+    latent = jnp.concatenate(
+        [lat_ref[:, pl.ds(first + i, 1), :].reshape(channels, columns) for i in range(near)], axis=0
+    )
+    main = latent - sigma * (total[:, :columns] / count_ref[...].astype(f32))
+    edges = total[:, columns:] + back
+    left = one[:, columns + 4 : columns + 5] + one[:, columns + 5 : columns + 6] + one[:, columns + 6 : columns + 7]
+    right = back[:, 4:5] + back[:, 5:6] + back[:, 6:7]
+    left = left - sigma[:, :1] * (edges[:, 0:1] / edges[:, 2:3])
+    right = right - sigma[:, :1] * (edges[:, 1:2] / edges[:, 3:4])
+    left = jnp.where(place == 0, 0.0, left)
+    right = jnp.where(place == width - 1, 0.0, right)
+    lane = iota((flat, columns), 1)
     before = jnp.where(lane == 0, left, pltpu.roll(main, 1, 1))
     after = jnp.where(lane == columns - 1, right, pltpu.roll(main, columns - 1, 1))
     zero = jnp.zeros((channels, columns), f32)
@@ -355,7 +415,7 @@
         for i in range(near):
             pad_buf[b, i + 1] = value[i * channels : (i + 1) * channels]
     for r in range(half):
-        at = first + r
+        at = guide + r
         den_ref[:, r, :] = pad_buf[1, at + 1]
         stacked = jnp.concatenate(
             [pad_buf[b, at + a] for a in range(3) for b in range(3)], axis=0
@@ -371,6 +431,10 @@
 
 def swap(x, axis):
     return lax.ppermute(x, axis, [(0, 1), (1, 0)])
+
+
+def major_route(width, fold, d):
+    return [(i, (i // fold ^ d) * fold + i % fold) for i in range(width)]
 
 
 def gather_major(chunk, fold, direct):
@@ -381,8 +445,7 @@
         return lax.dynamic_index_in_dim(every, lax.axis_index("width") % fold, 1, False)
     pieces = [chunk]
     for d in range(1, width // fold):
-        route = [(i, (i // fold ^ d) * fold + i % fold) for i in range(width)]
-        pieces.append(lax.ppermute(chunk, "width", route))
+        pieces.append(lax.ppermute(chunk, "width", major_route(width, fold, d)))
     return jnp.stack(pieces)
 
 
@@ -411,51 +474,60 @@
     rows = w_qkv.shape[0]
     fold = 2 if width % 2 == 0 else 1
     depth = width // fold
-    direct = depth <= 8 and depth & (depth - 1) == 0
+    direct = fold == 2 and depth <= 8 and depth & (depth - 1) == 0
     changes = jnp.swapaxes(cond_mod, 0, 1)
     offset = starts[0] - place * columns
     key = place // fold if direct else 0
     scalars = jnp.stack([group, offset, guide, place, step_index[0], key]).astype(jnp.int32)
 
-    (parts,) = call(
+    right = shift(latent, -1)
+    further = shift(latent, -2)
+
+    slab = (ROWS, slots * LANES)
+    in_hbm = functools.partial(pltpu.with_memory_space_constraint, memory_space=pltpu.HBM)
+    parts = call(
         functools.partial(
-            partial_kernel, width=width, slots=slots, local_pairs=local_pairs, features=features
+            partial_kernel, width=width, slots=slots, local_pairs=local_pairs, features=features,
+            fold=fold, direct=direct,
         ),
-        [((width, ROWS, slots * LANES), bf16)],
+        [((depth,) + slab, f32), ((depth,) + slab, bf16)] if direct else [((width,) + slab, bf16)],
         scratch=[
             pltpu.VMEM((3, rows, local_pairs * LANES), bf16),
-            pltpu.SemaphoreType.DMA((3,)),
+            pltpu.VMEM(changes.shape, f32),
+            pltpu.VMEM(w_patch.shape, bf16),
+            pltpu.SemaphoreType.DMA((5,)),
         ],
-        anys=(3,), smem=(0,), count=4, limit=8,
-    )(scalars, changes, w_patch, pltpu.with_memory_space_constraint(w_qkv, pltpu.HBM))
-    latent_now, counts_now, parts = lax.optimization_barrier((latent, counts, parts))
-    pack = jnp.concatenate(
-        [latent_now, jnp.broadcast_to(counts_now.astype(f32)[None, None, :], (1, height, columns))], axis=0
-    )
-    right = shift(pack, -1)
-    further = shift(latent_now.astype(bf16), -2)
-    left = shift(pack, 1)
-
-    parts = lax.all_to_all(parts, "width", 0, 0, tiled=True)
+        anys=(1, 2, 3), smem=(0,), count=4, limit=8,
+    )(scalars, in_hbm(changes), in_hbm(w_patch), in_hbm(w_qkv))
     near = height // 2 + 1
     tokens = height // 2 * columns
-    x, xt, var, varrow, lat, count = call(
+    if direct:
+        came = swap_minor(parts[1], fold)
+    else:
+        came = lax.all_to_all(parts[0], "width", 0, 0, tiled=True)
+    x, xt, var, varrow = call(
         window_kernel,
-        [
-            ((tokens, LANES), bf16), ((ROWS, tokens), bf16), ((tokens, LANES), f32),
-            ((8, tokens), f32), ((near, channels, 2 * columns), f32), ((height, 2 * columns), f32),
-        ],
+        [((tokens, LANES), bf16), ((ROWS, tokens), bf16), ((tokens, LANES), f32), ((8, tokens), f32)],
         scratch=[
             pltpu.VMEM((height * channels, 3 * columns), bf16),
             pltpu.VMEM((feats, tokens), f32),
             pltpu.VMEM((tokens, model), f32),
+            pltpu.VMEM(w_patch.shape, bf16),
+            pltpu.SemaphoreType.DMA((1,)),
         ],
-        smem=(0,), count=6, flops=5e9,
-    )(scalars, pack, right, left, further, w_patch)
-    parts, x = lax.optimization_barrier((parts, x))
-    (chunk,) = call(
-        functools.partial(sum_kernel, width=width), [((ROWS, slots * LANES), bf16)], count=1, limit=4
-    )(parts)
+        anys=(4,), smem=(0,), count=5, flops=5e9,
+    )(scalars, latent, right, further, in_hbm(w_patch))
+    came, x = lax.optimization_barrier((came, x))
+    if direct:
+        own, *sends = call(
+            first_sum_kernel, [(slab, f32)] + [(slab, bf16)] * (depth - 1), smem=(0,), count=3, limit=4
+        )(scalars, parts[0], came)
+        got = [lax.ppermute(v, "width", major_route(width, fold, d + 1)) for d, v in enumerate(sends)]
+        (chunk,) = call(last_sum_kernel, [(slab, bf16)], count=depth, limit=4)(own, *got)
+    else:
+        (chunk,) = call(
+            functools.partial(sum_kernel, width=width), [(slab, bf16)], count=1, limit=4
+        )(came)
     stack = gather_major(chunk, fold, direct)
     side = swap_minor(stack, fold)
     if halves == 2:
@@ -489,8 +561,8 @@
             ((flat, 2 * columns), f32), ((flat, 2 * columns), bf16),
             ((flat, 2 * columns), bf16), ((flat, columns), bf16),
         ],
-        smem=(0,), count=3,
-    )(scalars, mine_v, theirs)
+        smem=(0,), count=4, limit=8,
+    )(scalars, mine_v, theirs, latent)
     one = shift(one, 1)
     two = shift(two, 2)
     back = shift(back, -1)
@@ -498,8 +570,8 @@
         functools.partial(decode_kernel, width=width),
         [((channels, height // 2, columns), f32), ((height // 2, columns, w_dec.shape[1]), bf16)],
         scratch=[pltpu.VMEM((3, near + 2, channels, columns), f32)],
-        smem=(0,), count=8,
-    )(scalars, own, one, two, back, lat, count, w_dec)
+        smem=(0,), count=8, limit=8,
+    )(scalars, own, one, two, back, latent, counts[None], w_dec)
 
 
 def solution(mesh):

time: 77.7 us -> 70.8 us (0.911)
  starting transfers between devices: 32.8 us -> 27.5 us
  other arithmetic: 2.37 us -> 0.02 us
  local copies, waits for them, and re-layouts: 2.8 us -> 0.96 us
  Pallas kernels: 27.1 us -> 28.8 us
  waiting for transfers between devices: 10.1 us -> 11.2 us
    all_to_all x1 -> x0, starting transfers between devices: 6 us -> none  [shards(): parts = lax.all_to_all(parts, 'width', 0, 0, tiled=True)]
    ppermute x3 -> x6, starting transfers between devices: 5.55 us -> 8.9 us  [the longest x3 4.45 us: gather_major(): pieces.append(lax.ppermute(chunk, 'width', major_route(width, fold, d)))]
    ppermute x6 -> x5, starting transfers between devices: 16.7 us -> 13.3 us  [shift(): lax.ppermute(x, 'width', [(i, (i + by) % peers) for i in range(peers)])]
    ppermute x3 -> x6, waiting for transfers between devices: 3.59 us -> 6.23 us  [the longest x3 3.28 us: gather_major(): pieces.append(lax.ppermute(chunk, 'width', major_route(width, fold, d)))]
    unnamed x18, local copies, waits for them, and re-layouts: 2.72 us -> 0.88 us
    ppermute x6 -> x5, waiting for transfers between devices: 3.09 us -> 1.49 us  [shift(): lax.ppermute(x, 'width', [(i, (i + by) % peers) for i in range(peers)])]
    convert_element_type x2 -> x0, other arithmetic: 1.5 us -> none  [the longest x1 0.84 us: shards(): further = shift(latent_now.astype(bf16), -2)]
    concatenate x1 -> x0, other arithmetic: 0.84 us -> none  [shards(): jnp.concatenate([latent_now, jnp.broadcast_to(counts_now.astype(f32)[None...]
  transfers between devices with their start and end apart: 14 -> 16, of which waited for: 7 -> 8; matrix products, arithmetic and copies ran while one was open for 1% -> 0% of each run, Pallas kernels for 12% -> 19%
where the time goes in v4:
time: 70.8 us; the launch traced here: 70.5 us
  Pallas kernels  28.8 us (41%)
  starting transfers between devices  27.5 us (39%)
  waiting for transfers between devices  11.2 us (16%)
  between operations  2.12 us (3%)
  local copies, waits for them, and re-layouts  0.96 us (1%)
    ppermute x5, starting transfers between devices, shift(): lax.ppermute(x, 'width', [(i, (i + by) % peers) for i in range(peers)])  13.3 us
    pallas_call x1, Pallas kernels, shards(): call(functools.partial(second_kernel, slots=slots, pairs=local_pairs, cha...  11.9 us
    pallas_call x1, Pallas kernels, shards(): call(functools.partial(first_kernel, slots=slots, pairs=local_pairs, fold...  4.9 us
    pallas_call x1, Pallas kernels, shards(): call(window_kernel, [((tokens, LANES), bf16), ((ROWS, tokens), bf16), ((t...  4.81 us
    ppermute x3, starting transfers between devices, gather_major(): pieces.append(lax.ppermute(chunk, 'width', major_route(width, fold, d)))  4.45 us
    ppermute x3, starting transfers between devices, shards(): lax.ppermute(v, 'width', major_route(width, fold, d + 1))  4.45 us
    pallas_call x1, Pallas kernels, shards(): call(functools.partial(partial_kernel, width=width, slots=slots, local_pa...  3.71 us
    ppermute x3, waiting for transfers between devices, gather_major(): pieces.append(lax.ppermute(chunk, 'width', major_route(width, fold, d)))  3.28 us
  transfers between devices with their start and end apart: 16, of which 8 were waited for; matrix products, arithmetic and copies ran while one was open for 0% of the time, Pallas kernels for 19%

profile of v4, /device:TPU:0, one launch (start us, length us, event | category | flops | bytes accessed | tf_op | source)
XLA Modules:
  0.0 70.5 jit_solution(16273629059209578716)
XLA Ops:
  0.6 6.1 %collective-permute-start.1 = (f32[16,8,128]{2,1,0:T(8,128)}, f32[16,8,128]{2,1,0:T(8,128)S(1)}, u32[]{:S(2)}, u32[]{:S(2)}) collective-permute-start(f32[16,8,128]{2,1,0:T(8,128)} %lat_ref.3), channel_id=1, source_target_pairs={{0,14},{2,0},{4,2},{6,4},{8,6},{10,8},{12,10},{14,12},{1,15},{3,1}... | collective-permute-start | bytes 196616 | tf_op jit(solution)/shard_map/ppermute | solution.py:429
  6.7 0.4 collective-permute-start.2
  8.5 0.1 stack.38.place_ref
  8.6 3.7 %shard_map.113 = (f32[4,72,256]{2,1,0:T(8,128)S(1)}, bf16[4,72,256]{2,1,0:T(8,128)(2,1)S(1)}) custom-call(s32[6]{0:T(128)S(1)} %stack.38.place_ref, f32[3,1,2432]{2,1,0:T(1,128)} %bitcast.15, bf16[64,2432]{1,0:T(8,128)(2,1)} %wp_ref.5, bf16[304,3840]{1,0:T(8,128)(2,1)} %w_ref.2), custom_call_target="tpu_custom_call" | custom-call | bytes 1048576 | tf_op jit(solution)/shard_map/pallas_call | solution.py:488
  12.3 0.7 collective-permute-start
  12.9 0.0 collective-permute-done.1.right_ref
  12.9 0.0 collective-permute-done.2.further_ref
  13.0 0.8 %copy-done.1 = f32[16,8,128]{2,1,0:T(8,128)S(1)} copy-done((f32[16,8,128]{2,1,0:T(8,128)S(1)}, f32[16,8,128]{2,1,0:T(8,128)}, u32[]{:S(2)}) %copy-start.1) | copy-done | bytes 65560
  13.8 4.8 %shard_map.114 = (bf16[512,128]{1,0:T(8,128)(2,1)S(1)}, bf16[72,512]{1,0:T(8,128)(2,1)S(1)}, f32[512,128]{1,0:T(8,128)S(1)}, f32[8,512]{1,0:T(8,128)S(1)}) custom-call(s32[6]{0:T(128)S(1)} %stack.38.place_ref, f32[16,8,128]{2,1,0:T(8,128)S(1)} %copy-done.1, f32[16,8,128]{2,1,0:T(8,128)S(1)} %collective-permute-done.1.right_ref, ...), custom_call_target="tpu_custom_call" | custom-call | flops 5000000000 | bytes 1048576 | tf_op jit(solution)/shard_map/pallas_call | solution.py:508
  18.6 0.0 collective-permute-done.came_ref
  18.6 0.6 shard_map.115
  19.2 1.1 %collective-permute-start.3 = (bf16[72,256]{1,0:T(8,128)(2,1)S(1)}, bf16[72,256]{1,0:T(8,128)(2,1)S(1)}, u32[]{:S(2)}, u32[]{:S(2)}) collective-permute-start(bf16[72,256]{1,0:T(8,128)(2,1)S(1)} %get-tuple-element.25), channel_id=1, source_target_pairs={{0,4},{2,6},{4,0},{6,2},{8,12},{10,14},{12,8},{14,10},{1,5},{3,7},... | collective-permute-start | bytes 110600 | tf_op jit(solution)/shard_map/ppermute | solution.py:525
  20.3 0.6 collective-permute-start.4
  20.8 2.8 %collective-permute-start.5 = (bf16[72,256]{1,0:T(8,128)(2,1)S(1)}, bf16[72,256]{1,0:T(8,128)(2,1)S(1)}, u32[]{:S(2)}, u32[]{:S(2)}) collective-permute-start(bf16[72,256]{1,0:T(8,128)(2,1)S(1)} %get-tuple-element.27), channel_id=1, source_target_pairs={{0,12},{2,14},{4,8},{6,10},{8,4},{10,6},{12,0},{14,2},{1,13},{3,15... | collective-permute-start | bytes 110600 | tf_op jit(solution)/shard_map/ppermute | solution.py:525
  23.7 0.0 collective-permute-done.3.refs_1_
  23.7 1.5 %collective-permute-done.4.refs_2_ = bf16[72,256]{1,0:T(8,128)(2,1)S(1)} collective-permute-done((bf16[72,256]{1,0:T(8,128)(2,1)S(1)}, bf16[72,256]{1,0:T(8,128)(2,1)S(1)}, u32[]{:S(2)}, u32[]{:S(2)}) %collective-permute-start.4) | collective-permute-done | bytes 36896 | tf_op jit(solution)/shard_map/ppermute | solution.py:525
  25.1 1.5 %collective-permute-done.5.refs_3_ = bf16[72,256]{1,0:T(8,128)(2,1)S(1)} collective-permute-done((bf16[72,256]{1,0:T(8,128)(2,1)S(1)}, bf16[72,256]{1,0:T(8,128)(2,1)S(1)}, u32[]{:S(2)}, u32[]{:S(2)}) %collective-permute-start.5) | collective-permute-done | bytes 36896 | tf_op jit(solution)/shard_map/ppermute | solution.py:525
  26.6 2.9 %collective-permute-start.8 = (bf16[72,256]{1,0:T(8,128)(2,1)S(1)}, bf16[72,256]{1,0:T(8,128)(2,1)S(1)}, u32[]{:S(2)}, u32[]{:S(2)}) collective-permute-start(bf16[72,256]{1,0:T(8,128)(2,1)S(1)} %shard_map.116), channel_id=1, source_target_pairs={{0,12},{2,14},{4,8},{6,10},{8,4},{10,6},{12,0},{14,2},{1,13},{3,15... | collective-permute-start | bytes 110600 | tf_op jit(solution)/shard_map/ppermute | solution.py:448
  29.5 0.0 collective-permute-start.6
  29.5 1.6 %collective-permute-start.7 = (bf16[72,256]{1,0:T(8,128)(2,1)S(1)}, bf16[72,256]{1,0:T(8,128)(2,1)S(1)}, u32[]{:S(2)}, u32[]{:S(2)}) collective-permute-start(bf16[72,256]{1,0:T(8,128)(2,1)S(1)} %shard_map.116), channel_id=1, source_target_pairs={{0,8},{2,10},{4,12},{6,14},{8,0},{10,2},{12,4},{14,6},{1,9},{3,11}... | collective-permute-start | bytes 110600 | tf_op jit(solution)/shard_map/ppermute | solution.py:448
  31.1 1.4 %collective-permute-done.8 = bf16[72,256]{1,0:T(8,128)(2,1)S(1)} collective-permute-done((bf16[72,256]{1,0:T(8,128)(2,1)S(1)}, bf16[72,256]{1,0:T(8,128)(2,1)S(1)}, u32[]{:S(2)}, u32[]{:S(2)}) %collective-permute-start.8) | collective-permute-done | bytes 36896 | tf_op jit(solution)/shard_map/ppermute | solution.py:448
  32.5 1.0 %collective-permute-done.6 = bf16[72,256]{1,0:T(8,128)(2,1)S(1)} collective-permute-done((bf16[72,256]{1,0:T(8,128)(2,1)S(1)}, bf16[72,256]{1,0:T(8,128)(2,1)S(1)}, u32[]{:S(2)}, u32[]{:S(2)}) %collective-permute-start.6) | collective-permute-done | bytes 36896 | tf_op jit(solution)/shard_map/ppermute | solution.py:448
  33.5 0.9 %collective-permute-done.7 = bf16[72,256]{1,0:T(8,128)(2,1)S(1)} collective-permute-done((bf16[72,256]{1,0:T(8,128)(2,1)S(1)}, bf16[72,256]{1,0:T(8,128)(2,1)S(1)}, u32[]{:S(2)}, u32[]{:S(2)}) %collective-permute-start.7) | collective-permute-done | bytes 36896 | tf_op jit(solution)/shard_map/ppermute | solution.py:448
  34.4 1.5 %collective-permute-start.10 = (bf16[4,72,256]{2,1,0:T(8,128)(2,1)S(1)}, bf16[4,72,256]{2,1,0:T(8,128)(2,1)S(1)}, u32[]{:S(2)}, u32[]{:S(2)}) collective-permute-start(bf16[4,72,256]{2,1,0:T(8,128)(2,1)S(1)} %pad_maximum_fusion.near_ref), channel_id=1, source_target_pairs={{0,2},{2,0},{4,6},{6,4},{8,10},{10,8},{12,14},{14,12},{1,3},{3,1},... | collective-permute-start | bytes 442376 | tf_op jit(solution)/shard_map/ppermute | solution.py:456
  35.9 1.5 %collective-permute-start.9 = (bf16[4,72,256]{2,1,0:T(8,128)(2,1)S(1)}, bf16[4,72,256]{2,1,0:T(8,128)(2,1)S(1)}, u32[]{:S(2)}, u32[]{:S(2)}) collective-permute-start(bf16[4,72,256]{2,1,0:T(8,128)(2,1)S(1)} %pad_maximum_fusion.near_ref), channel_id=1, source_target_pairs={{0,16},{16,0},{1,17},{17,1},{2,18},{18,2},{3,19},{19,3},{4,20},{20... | collective-permute-start | bytes 442376 | tf_op jit(solution)/shard_map/ppermute | solution.py:433
  37.4 2.2 %collective-permute-done.10.far_ref = bf16[4,72,256]{2,1,0:T(8,128)(2,1)S(1)} collective-permute-done((bf16[4,72,256]{2,1,0:T(8,128)(2,1)S(1)}, bf16[4,72,256]{2,1,0:T(8,128)(2,1)S(1)}, u32[]{:S(2)}, u32[]{:S(2)}) %collective-permute-start.10) | collective-permute-done | bytes 147488 | tf_op jit(solution)/shard_map/ppermute | solution.py:456
  39.6 1.5 %collective-permute-start.11 = (bf16[4,72,256]{2,1,0:T(8,128)(2,1)S(1)}, bf16[4,72,256]{2,1,0:T(8,128)(2,1)S(1)}, u32[]{:S(2)}, u32[]{:S(2)}) collective-permute-start(bf16[4,72,256]{2,1,0:T(8,128)(2,1)S(1)} %collective-permute-done.10.far_ref), channel_id=1, source_target_pairs={{0,16},{16,0},{1,17},{17,1},{2,18},{18,2},{3,19},{19,3},{4,20},{20... | collective-permute-start | bytes 442376 | tf_op jit(solution)/shard_map/ppermute | solution.py:433
  41.1 4.9 %shard_map.117.att_ref = bf16[512,640]{1,0:T(8,128)(2,1)S(1)} custom-call(s32[6]{0:T(128)S(1)} %stack.38.place_ref, bf16[4,72,256]{2,1,0:T(8,128)(2,1)S(1)} %pad_maximum_fusion.near_ref, bf16[4,72,256]{2,1,0:T(8,128)(2,1)S(1)} %collective-permute-done.10.far_ref, bf16[512,128]{1,0:T(8,128)(2,1)S(1)} %get-tuple-element.28.x_ref, ...), custom_call_target="tpu_custom_call" | custom-call | flops 6000000000 | bytes 1048576 | tf_op jit(solution)/shard_map/pallas_call | solution.py:537
  46.0 0.0 collective-permute-done.9.near_ref
  46.0 0.0 collective-permute-done.11.far_ref
  46.0 0.0 slice-done
  46.0 0.0 copy-done
  46.0 0.0 copy-done.4
  46.1 0.0 slice-done.1
  46.1 0.0 copy-start.2
  46.1 0.0 copy-start.3
  46.1 0.0 copy-start.5
  46.1 11.9 %shard_map.118 = (f32[5,16,256]{2,1,0:T(8,128)S(1)}, bf16[5,16,256]{2,1,0:T(8,128)(2,1)S(1)}) custom-call(s32[6]{0:T(128)S(1)} %stack.38.place_ref, bf16[4,72,256]{2,1,0:T(8,128)(2,1)S(1)} %collective-permute-done.9.near_ref, bf16[4,72,256]{2,1,0:T(8,128)(2,1)S(1)} %collective-permute-done.11.far_ref, bf16[512,128]{1,0:T(8,128)(2,1)S(1)} %get-tuple-element.28.x_ref, ...), custom_call_target="tpu_custom_call" | custom-call | flops 12000000000 | bytes 1048576 | tf_op jit(solution)/shard_map/pallas_call | solution.py:542
  58.0 0.1 collective-permute-start.12
  58.1 1.2 %collective-permute-done.12.theirs_ref = bf16[5,16,256]{2,1,0:T(8,128)(2,1)S(1)} collective-permute-done((bf16[5,16,256]{2,1,0:T(8,128)(2,1)S(1)}, bf16[5,16,256]{2,1,0:T(8,128)(2,1)S(1)}, u32[]{:S(2)}, u32[]{:S(2)}) %collective-permute-start.12) | collective-permute-done | bytes 40992 | tf_op jit(solution)/shard_map/ppermute | solution.py:433
  59.3 0.8 %shard_map.119 = (f32[80,256]{1,0:T(8,128)S(1)}, bf16[80,256]{1,0:T(8,128)(2,1)S(1)}, bf16[80,256]{1,0:T(8,128)(2,1)S(1)}, bf16[80,128]{1,0:T(8,128)(2,1)S(1)}) custom-call(s32[6]{0:T(128)S(1)} %stack.38.place_ref, f32[5,16,256]{2,1,0:T(8,128)S(1)} %get-tuple-element.32.mine_ref, bf16[5,16,256]{2,1,0:T(8,128)(2,1)S(1)} %collective-permute-done.12.theirs_ref, ...), custom_call_target="tpu_custom_call" | custom-call | bytes 1048576 | tf_op jit(solution)/shard_map/pallas_call | solution.py:558
  60.2 1.5 %collective-permute-start.13 = (bf16[80,256]{1,0:T(8,128)(2,1)S(1)}, bf16[80,256]{1,0:T(8,128)(2,1)S(1)}, u32[]{:S(2)}, u32[]{:S(2)}) collective-permute-start(bf16[80,256]{1,0:T(8,128)(2,1)S(1)} %get-tuple-element.35), channel_id=1, source_target_pairs={{0,2},{2,4},{4,6},{6,8},{8,10},{10,12},{12,14},{14,0},{1,3},{3,5},... | collective-permute-start | bytes 122888 | tf_op jit(solution)/shard_map/ppermute | solution.py:429
  61.6 2.0 %collective-permute-start.14 = (bf16[80,256]{1,0:T(8,128)(2,1)S(1)}, bf16[80,256]{1,0:T(8,128)(2,1)S(1)}, u32[]{:S(2)}, u32[]{:S(2)}) collective-permute-start(bf16[80,256]{1,0:T(8,128)(2,1)S(1)} %get-tuple-element.36), channel_id=1, source_target_pairs={{0,4},{2,6},{4,8},{6,10},{8,12},{10,14},{12,0},{14,2},{1,5},{3,7},... | collective-permute-start | bytes 122888 | tf_op jit(solution)/shard_map/ppermute | solution.py:429
  63.7 3.3 %collective-permute-start.15 = (bf16[80,128]{1,0:T(8,128)(2,1)S(1)}, bf16[80,128]{1,0:T(8,128)(2,1)S(1)}, u32[]{:S(2)}, u32[]{:S(2)}) collective-permute-start(bf16[80,128]{1,0:T(8,128)(2,1)S(1)} %get-tuple-element.37), channel_id=1, source_target_pairs={{0,14},{2,0},{4,2},{6,4},{8,6},{10,8},{12,10},{14,12},{1,15},{3,1}... | collective-permute-start | bytes 61448 | tf_op jit(solution)/shard_map/ppermute | solution.py:429
  67.0 1.5 %collective-permute-done.15.back_ref = bf16[80,128]{1,0:T(8,128)(2,1)S(1)} collective-permute-done((bf16[80,128]{1,0:T(8,128)(2,1)S(1)}, bf16[80,128]{1,0:T(8,128)(2,1)S(1)}, u32[]{:S(2)}, u32[]{:S(2)}) %collective-permute-start.15) | collective-permute-done | bytes 20512 | tf_op jit(solution)/shard_map/ppermute | solution.py:429
  68.5 0.0 collective-permute-done.13.one_ref
  68.5 0.0 collective-permute-done.14.two_ref
  68.5 2.1 %shard_map.120 = (f32[16,4,128]{2,1,0:T(4,128)}, bf16[4,128,512]{2,1,0:T(8,128)(2,1)}) custom-call(s32[6]{0:T(128)S(1)} %stack.38.place_ref, f32[80,256]{1,0:T(8,128)S(1)} %get-tuple-element.34.own_ref, bf16[80,256]{1,0:T(8,128)(2,1)S(1)} %collective-permute-done.13.one_ref, bf16[80,256]{1,0:T(8,128)(2,1)S(1)} %collective-permute-done.14.two_ref, ...), custom_call_target="tpu_custom_call" | custom-call | bytes 1048576 | tf_op jit(solution)/shard_map/pallas_call | solution.py:569
  (13 shorter events, 0.1 us)
Async XLA Ops:
  0.6 12.3 %collective-permute-start.1 = (f32[16,8,128]{2,1,0:T(8,128)}, f32[16,8,128]{2,1,0:T(8,128)S(1)}, u32[]{:S(2)}, u32[]{:S(2)}) collective-permute-start(f32[16,8,128]{2,1,0:T(8,128)} %lat_ref.3), channel_id=1, source_target_pairs={{0,14},{2,0},{4,2},{6,4},{8,6},{10,8},{12,10},{14,12},{1,15},{3,1}... | collective-permute-start | bytes 196616 | tf_op jit(solution)/shard_map/ppermute | solution.py:429
  6.7 6.2 %collective-permute-start.2 = (f32[16,8,128]{2,1,0:T(8,128)}, f32[16,8,128]{2,1,0:T(8,128)S(1)}, u32[]{:S(2)}, u32[]{:S(2)}) collective-permute-start(f32[16,8,128]{2,1,0:T(8,128)} %lat_ref.3), channel_id=1, source_target_pairs={{0,12},{2,14},{4,0},{6,2},{8,4},{10,6},{12,8},{14,10},{1,13},{3,15... | collective-permute-start | bytes 196616 | tf_op jit(solution)/shard_map/ppermute | solution.py:429
  12.3 6.3 %collective-permute-start = (bf16[4,72,256]{2,1,0:T(8,128)(2,1)S(1)}, bf16[4,72,256]{2,1,0:T(8,128)(2,1)S(1)}, u32[]{:S(2)}, u32[]{:S(2)}) collective-permute-start(bf16[4,72,256]{2,1,0:T(8,128)(2,1)S(1)} %get-tuple-element.21), channel_id=1, source_target_pairs={{0,2},{2,0},{4,6},{6,4},{8,10},{10,8},{12,14},{14,12},{1,3},{3,1},... | collective-permute-start | bytes 442376 | tf_op jit(solution)/shard_map/ppermute | solution.py:456
  13.0 0.8 %copy-start.1 = (f32[16,8,128]{2,1,0:T(8,128)S(1)}, f32[16,8,128]{2,1,0:T(8,128)}, u32[]{:S(2)}) copy-start(f32[16,8,128]{2,1,0:T(8,128)} %lat_ref.3) | copy-start | bytes 196612
  19.2 4.5 %collective-permute-start.3 = (bf16[72,256]{1,0:T(8,128)(2,1)S(1)}, bf16[72,256]{1,0:T(8,128)(2,1)S(1)}, u32[]{:S(2)}, u32[]{:S(2)}) collective-permute-start(bf16[72,256]{1,0:T(8,128)(2,1)S(1)} %get-tuple-element.25), channel_id=1, source_target_pairs={{0,4},{2,6},{4,0},{6,2},{8,12},{10,14},{12,8},{14,10},{1,5},{3,7},... | collective-permute-start | bytes 110600 | tf_op jit(solution)/shard_map/ppermute | solution.py:525
  20.3 4.9 %collective-permute-start.4 = (bf16[72,256]{1,0:T(8,128)(2,1)S(1)}, bf16[72,256]{1,0:T(8,128)(2,1)S(1)}, u32[]{:S(2)}, u32[]{:S(2)}) collective-permute-start(bf16[72,256]{1,0:T(8,128)(2,1)S(1)} %get-tuple-element.26), channel_id=1, source_target_pairs={{0,8},{2,10},{4,12},{6,14},{8,0},{10,2},{12,4},{14,6},{1,9},{3,11}... | collective-permute-start | bytes 110600 | tf_op jit(solution)/shard_map/ppermute | solution.py:525
  20.8 5.8 %collective-permute-start.5 = (bf16[72,256]{1,0:T(8,128)(2,1)S(1)}, bf16[72,256]{1,0:T(8,128)(2,1)S(1)}, u32[]{:S(2)}, u32[]{:S(2)}) collective-permute-start(bf16[72,256]{1,0:T(8,128)(2,1)S(1)} %get-tuple-element.27), channel_id=1, source_target_pairs={{0,12},{2,14},{4,8},{6,10},{8,4},{10,6},{12,0},{14,2},{1,13},{3,15... | collective-permute-start | bytes 110600 | tf_op jit(solution)/shard_map/ppermute | solution.py:525
  26.6 19.4 %slice-start = ((s8[6225920]{0:T(1024)(128)(4,1)}), s8[4194304]{0:T(1024)(128)(4,1)S(1)}, s32[]{:S(2)}) async-start(s8[6225920]{0:T(1024)(128)(4,1)} %bitcast.18), calls=%async_computation | async-start | bytes 8388608
  26.6 5.8 %collective-permute-start.8 = (bf16[72,256]{1,0:T(8,128)(2,1)S(1)}, bf16[72,256]{1,0:T(8,128)(2,1)S(1)}, u32[]{:S(2)}, u32[]{:S(2)}) collective-permute-start(bf16[72,256]{1,0:T(8,128)(2,1)S(1)} %shard_map.116), channel_id=1, source_target_pairs={{0,12},{2,14},{4,8},{6,10},{8,4},{10,6},{12,0},{14,2},{1,13},{3,15... | collective-permute-start | bytes 110600 | tf_op jit(solution)/shard_map/ppermute | solution.py:448
  29.5 4.0 %collective-permute-start.6 = (bf16[72,256]{1,0:T(8,128)(2,1)S(1)}, bf16[72,256]{1,0:T(8,128)(2,1)S(1)}, u32[]{:S(2)}, u32[]{:S(2)}) collective-permute-start(bf16[72,256]{1,0:T(8,128)(2,1)S(1)} %shard_map.116), channel_id=1, source_target_pairs={{0,4},{2,6},{4,0},{6,2},{8,12},{10,14},{12,8},{14,10},{1,5},{3,7},... | collective-permute-start | bytes 110600 | tf_op jit(solution)/shard_map/ppermute | solution.py:448
  29.5 4.9 %collective-permute-start.7 = (bf16[72,256]{1,0:T(8,128)(2,1)S(1)}, bf16[72,256]{1,0:T(8,128)(2,1)S(1)}, u32[]{:S(2)}, u32[]{:S(2)}) collective-permute-start(bf16[72,256]{1,0:T(8,128)(2,1)S(1)} %shard_map.116), channel_id=1, source_target_pairs={{0,8},{2,10},{4,12},{6,14},{8,0},{10,2},{12,4},{14,6},{1,9},{3,11}... | collective-permute-start | bytes 110600 | tf_op jit(solution)/shard_map/ppermute | solution.py:448
  34.4 5.2 %collective-permute-start.10 = (bf16[4,72,256]{2,1,0:T(8,128)(2,1)S(1)}, bf16[4,72,256]{2,1,0:T(8,128)(2,1)S(1)}, u32[]{:S(2)}, u32[]{:S(2)}) collective-permute-start(bf16[4,72,256]{2,1,0:T(8,128)(2,1)S(1)} %pad_maximum_fusion.near_ref), channel_id=1, source_target_pairs={{0,2},{2,0},{4,6},{6,4},{8,10},{10,8},{12,14},{14,12},{1,3},{3,1},... | collective-permute-start | bytes 442376 | tf_op jit(solution)/shard_map/ppermute | solution.py:456
  35.9 10.1 %collective-permute-start.9 = (bf16[4,72,256]{2,1,0:T(8,128)(2,1)S(1)}, bf16[4,72,256]{2,1,0:T(8,128)(2,1)S(1)}, u32[]{:S(2)}, u32[]{:S(2)}) collective-permute-start(bf16[4,72,256]{2,1,0:T(8,128)(2,1)S(1)} %pad_maximum_fusion.near_ref), channel_id=1, source_target_pairs={{0,16},{16,0},{1,17},{17,1},{2,18},{18,2},{3,19},{19,3},{4,20},{20... | collective-permute-start | bytes 442376 | tf_op jit(solution)/shard_map/ppermute | solution.py:433
  39.6 6.4 %collective-permute-start.11 = (bf16[4,72,256]{2,1,0:T(8,128)(2,1)S(1)}, bf16[4,72,256]{2,1,0:T(8,128)(2,1)S(1)}, u32[]{:S(2)}, u32[]{:S(2)}) collective-permute-start(bf16[4,72,256]{2,1,0:T(8,128)(2,1)S(1)} %collective-permute-done.10.far_ref), channel_id=1, source_target_pairs={{0,16},{16,0},{1,17},{17,1},{2,18},{18,2},{3,19},{19,3},{4,20},{20... | collective-permute-start | bytes 442376 | tf_op jit(solution)/shard_map/ppermute | solution.py:433
  41.1 4.9 %copy-start = (bf16[64,2432]{1,0:T(8,128)(2,1)S(1)}, bf16[64,2432]{1,0:T(8,128)(2,1)}, u32[]{:S(2)}) copy-start(bf16[64,2432]{1,0:T(8,128)(2,1)} %wp_ref.5) | copy-start | bytes 933892
  41.1 5.0 %copy-start.4 = (f32[1,3,2432]{2,0,1:T(1,128)S(1)}, f32[1,3,2432]{2,0,1:T(1,128)}, u32[]{:S(2)}) copy-start(f32[1,3,2432]{2,0,1:T(1,128)} %param.14) | copy-start | bytes 87556
  41.1 5.0 %slice-start.1 = ((s8[6225920]{0:T(1024)(128)(4,1)}), s8[2031616]{0:T(1024)(128)(4,1)S(1)}, s32[]{:S(2)}) async-start(s8[6225920]{0:T(1024)(128)(4,1)} %bitcast.18), calls=%async_computation.1 | async-start | bytes 4063232
  41.1 5.0 %copy-start.6 = (bf16[2432,64]{0,1:T(8,128)(2,1)S(1)}, bf16[2432,64]{0,1:T(8,128)(2,1)}, u32[]{:S(2)}) copy-start(bf16[2432,64]{0,1:T(8,128)(2,1)} %param.18) | copy-start | bytes 933892
  46.1 13.2 %copy-start.2 = (f32[16,8,128]{2,1,0:T(8,128)S(1)}, f32[16,8,128]{2,1,0:T(8,128)}, u32[]{:S(2)}) copy-start(f32[16,8,128]{2,1,0:T(8,128)} %lat_ref.3) | copy-start | bytes 196612
  46.1 22.4 %copy-start.3 = (bf16[144,512]{1,0:T(8,128)(2,1)S(1)}, bf16[144,512]{1,0:T(8,128)(2,1)}, u32[]{:S(2)}) copy-start(bf16[144,512]{1,0:T(8,128)(2,1)} %w_ref.3) | copy-start | bytes 442372
  46.1 22.4 %copy-start.5 = (s32[128]{0:T(128)S(1)}, s32[128]{0:T(128)}, u32[]{:S(2)}) copy-start(s32[128]{0:T(128)} %param.12) | copy-start | bytes 1540
  58.0 1.3 %collective-permute-start.12 = (bf16[5,16,256]{2,1,0:T(8,128)(2,1)S(1)}, bf16[5,16,256]{2,1,0:T(8,128)(2,1)S(1)}, u32[]{:S(2)}, u32[]{:S(2)}) collective-permute-start(bf16[5,16,256]{2,1,0:T(8,128)(2,1)S(1)} %get-tuple-element.33), channel_id=1, source_target_pairs={{0,1},{1,0},{2,3},{3,2},{4,5},{5,4},{6,7},{7,6},{8,9},{9,8},{10,11... | collective-permute-start | bytes 122888 | tf_op jit(solution)/shard_map/ppermute | solution.py:433
  60.2 8.3 %collective-permute-start.13 = (bf16[80,256]{1,0:T(8,128)(2,1)S(1)}, bf16[80,256]{1,0:T(8,128)(2,1)S(1)}, u32[]{:S(2)}, u32[]{:S(2)}) collective-permute-start(bf16[80,256]{1,0:T(8,128)(2,1)S(1)} %get-tuple-element.35), channel_id=1, source_target_pairs={{0,2},{2,4},{4,6},{6,8},{8,10},{10,12},{12,14},{14,0},{1,3},{3,5},... | collective-permute-start | bytes 122888 | tf_op jit(solution)/shard_map/ppermute | solution.py:429
  61.6 6.8 %collective-permute-start.14 = (bf16[80,256]{1,0:T(8,128)(2,1)S(1)}, bf16[80,256]{1,0:T(8,128)(2,1)S(1)}, u32[]{:S(2)}, u32[]{:S(2)}) collective-permute-start(bf16[80,256]{1,0:T(8,128)(2,1)S(1)} %get-tuple-element.36), channel_id=1, source_target_pairs={{0,4},{2,6},{4,8},{6,10},{8,12},{10,14},{12,0},{14,2},{1,5},{3,7},... | collective-permute-start | bytes 122888 | tf_op jit(solution)/shard_map/ppermute | solution.py:429
  63.7 4.8 %collective-permute-start.15 = (bf16[80,128]{1,0:T(8,128)(2,1)S(1)}, bf16[80,128]{1,0:T(8,128)(2,1)S(1)}, u32[]{:S(2)}, u32[]{:S(2)}) collective-permute-start(bf16[80,128]{1,0:T(8,128)(2,1)S(1)} %get-tuple-element.37), channel_id=1, source_target_pairs={{0,14},{2,0},{4,2},{6,4},{8,6},{10,8},{12,10},{14,12},{1,15},{3,1}... | collective-permute-start | bytes 61448 | tf_op jit(solution)/shard_map/ppermute | solution.py:429

commit v5 on v4

--- a/solution.py
+++ b/solution.py
@@ -6,6 +6,7 @@
 from jax.experimental import pallas as pl
 from jax.experimental.pallas import tpu as pltpu
 from jax.sharding import PartitionSpec as P
+
 
 HEADS = 20
 HEAD = 64
@@ -47,6 +48,16 @@
 
 def iota(shape, dim):
     return lax.broadcasted_iota(jnp.int32, shape, dim)
+
+
+def layout(local_pairs, depth, slots, fold):
+    whole = local_pairs // fold
+    sides = [[(y * whole + j, sub) for j in range(whole) for sub in range(3)] for y in range(fold)]
+    for pair in range(fold * whole, local_pairs):
+        for sub in range(3):
+            y = next(y for y in range(fold) if len(sides[y]) < depth * slots)
+            sides[y].append((pair, sub))
+    return whole, sides
 
 
 def split(values):
@@ -74,7 +85,7 @@
     feats, model = wp_ref.shape
     rows = w_buf.shape[1]
     window = min(model, -(-(rows + LANES - 1) // LANES) * LANES)
-    begin = place_ref[3] * rows
+    begin = place_ref[2] * rows
     low = jnp.minimum(begin // LANES * LANES, model - window)
     cols = pl.ds(pl.multiple_of(low, LANES), window)
     loads[0].wait()
@@ -89,13 +100,15 @@
     a = jnp.concatenate(split(stacked), axis=0)[:, :rows]
     for one in loads[2:]:
         one.wait()
-    side = place_ref[3] % fold
+    side = place_ref[2] % fold
+    _, sides = layout(local_pairs, width // fold, slots, fold)
     for owner in range(width):
+        z, y = divmod(owner, fold)
         pieces = []
         for slot in range(slots):
-            tile = owner * slots + slot
-            if tile < 3 * local_pairs:
-                pair, sub = divmod(tile, 3)
+            spot = z * slots + slot
+            if spot < len(sides[y]):
+                pair, sub = sides[y][spot]
                 both = dot(a, w_buf[PARTS[sub], :, pair * LANES : (pair + 1) * LANES])
                 pieces.append(both[:ROWS] + both[ROWS:])
             else:
@@ -104,7 +117,6 @@
         if not direct:
             out_refs[0][owner] = value.astype(bf16)
             continue
-        z, y = divmod(owner, fold)
 
         @pl.when(side == y)
         def _():
@@ -123,7 +135,7 @@
 
 
 def first_sum_kernel(place_ref, keep_ref, came_ref, own_ref, *send_refs):
-    key = place_ref[5]
+    key = place_ref[3]
     own_ref[...] = keep_ref[key] + came_ref[key].astype(f32)
     for d, ref in enumerate(send_refs):
         at = key ^ (d + 1)
@@ -139,14 +151,14 @@
 
 
 def window_kernel(
-    place_ref, own_ref, right_ref, further_ref, wp_ref,
-    x_ref, xt_ref, var_ref, varrow_ref,
-    rows_buf, xt_buf, hid_buf, w_ref, sem,
+    place_ref, start_ref, own_ref, right_ref, further_ref, wp_ref,
+    x_ref, xt_ref, var_ref, varrow_ref, hid_ref,
+    rows_buf, xt_buf, w_ref, sem,
 ):
     load = pltpu.make_async_copy(wp_ref, w_ref, sem.at[0])
     load.start()
     channels, height, columns = own_ref.shape
-    offset = place_ref[1]
+    offset = start_ref[0] - place_ref[2] * columns
     for r in range(height):
         at = slice(r * channels, (r + 1) * channels)
         rows_buf[at, :columns] = own_ref[:, r, :].astype(bf16)
@@ -173,11 +185,11 @@
     block = 64
     x_bf = xrow[:, :feats].astype(bf16)
     load.wait()
-    hid_buf[...] = dot(x_bf, w_ref[...])
+    hid_ref[...] = dot(x_bf, w_ref[...])
 
     def stats(i, carry):
         at = pl.ds(pl.multiple_of(i * block, block), block)
-        h = hid_buf[at, :]
+        h = hid_ref[at, :]
         mean = jnp.sum(h, axis=1, keepdims=True) * (1.0 / model)
         c = h - mean
         v = jnp.sum(c * c, axis=1, keepdims=True) * (1.0 / model)
@@ -199,35 +211,43 @@
     xt_ref[...] = jnp.concatenate([xt, tail], axis=0).astype(bf16)
 
 
-def attend_pairs(place_ref, near_ref, far_ref, x_ref, xt_ref, var_ref, varrow_ref, put, slots, pairs, fold):
+def attend_units(place_ref, near_ref, far_ref, x_ref, xt_ref, var_ref, varrow_ref, put, units, slots, pairs, fold):
     tokens = x_ref.shape[0]
-    key = place_ref[5]
-    side = place_ref[3] % fold
+    key = place_ref[3]
+    side = place_ref[2] % fold
+    whole, sides = layout(pairs, near_ref.shape[0], slots, fold)
     x = x_ref[:, :ROWS]
-    xt = xt_ref[...]
-    var = var_ref[...]
-    eps_col = epsilon * (var + epsilon)
-    rstd = lax.rsqrt(var + epsilon)
-    eps_row = epsilon * (varrow_ref[:1, :] + epsilon)
-    low = iota((tokens, LANES), 1) < HEAD
     scale = LOG2E * HEAD**-0.5
 
-    def tile(t):
-        owner, slot = divmod(t, slots)
-        z, y = divmod(owner, fold)
-        at = (z ^ key, slice(None), slice(slot * LANES, (slot + 1) * LANES))
-        return jnp.where(side == y, near_ref[at], far_ref[at])
-
-    for pair in range(pairs):
-        mq, mv, mk = (tile(3 * pair + sub) for sub in range(3))
+    def tile(unit, sub):
+        far = jnp.logical_and(unit >= whole, unit < fold * whole)
+        spot = 3 * (unit - jnp.where(far, whole, 0)) + sub
+        for pair in range(fold * whole, pairs):
+            y = next(y for y in range(fold) if (pair, sub) in sides[y])
+            mine = unit == pair
+            far = jnp.where(mine, side != y, far)
+            spot = jnp.where(mine, sides[y].index((pair, sub)), spot)
+        at = (
+            (spot // slots) ^ key,
+            slice(None),
+            pl.ds(pl.multiple_of(spot % slots * LANES, LANES), LANES),
+        )
+        return jnp.where(far, far_ref[at], near_ref[at])
+
+    def one(unit, carry):
+        mq, mv, mk = (tile(unit, sub) for sub in range(3))
+        low = iota((tokens, LANES), 1) < HEAD
+        var = var_ref[...]
         both = dot(x, jnp.concatenate([mq, mv], axis=1))
         uq = both[:, :LANES]
-        uv = both[:, LANES:] * rstd
-        uk = dot(mk, xt, ((0,), (0,)))
+        uv = both[:, LANES:] * lax.rsqrt(var + epsilon)
+        uk = dot(mk, xt_ref[...], ((0,), (0,)))
         sq = uq * uq
         sum_low = jnp.sum(jnp.where(low, sq, 0.0), axis=1, keepdims=True)
         sum_high = jnp.sum(jnp.where(low, 0.0, sq), axis=1, keepdims=True)
-        q = uq * lax.rsqrt(jnp.where(low, sum_low, sum_high) * (1.0 / HEAD) + eps_col)
+        mean = jnp.where(low, sum_low, sum_high) * (1.0 / HEAD)
+        q = uq * lax.rsqrt(mean + epsilon * (var + epsilon))
+        eps_row = epsilon * (varrow_ref[:1, :] + epsilon)
         keys = []
         for half in range(2):
             k = uk[half * HEAD : (half + 1) * HEAD]
@@ -243,41 +263,56 @@
             outs.append(dot(weights, vh))
         top = jnp.where(low, outs[0], outs[1])
         sums = pltpu.roll(jnp.where(low, outs[1], outs[0]), HEAD, 1)
-        put(pair, (top / sums).astype(bf16))
-
-
-def first_kernel(
-    place_ref, near_ref, far_ref, x_ref, xt_ref, var_ref, varrow_ref, att_ref, *, slots, pairs, fold
+        put(unit, (top / sums).astype(bf16))
+        return carry
+
+    lax.fori_loop(*units, one, 0)
+
+
+def attend_kernel(
+    place_ref, near_ref, far_ref, x_ref, xt_ref, var_ref, varrow_ref, att_ref, *, units, slots, pairs, fold
 ):
-    def put(pair, value):
-        att_ref[:, pair * LANES : (pair + 1) * LANES] = value
-
-    attend_pairs(place_ref, near_ref, far_ref, x_ref, xt_ref, var_ref, varrow_ref, put, slots, pairs, fold)
+    def put(unit, value):
+        att_ref[:, pl.ds(pl.multiple_of((unit - units[0]) * LANES, LANES), LANES)] = value
+
+    attend_units(
+        place_ref, near_ref, far_ref, x_ref, xt_ref, var_ref, varrow_ref, put, units, slots, pairs, fold
+    )
+
+
+def near_kernel(place_ref, near_ref, x_ref, xt_ref, var_ref, varrow_ref, att_ref, **sizes):
+    attend_kernel(place_ref, near_ref, near_ref, x_ref, xt_ref, var_ref, varrow_ref, att_ref, **sizes)
 
 
 def second_kernel(
-    place_ref, near_ref, far_ref, x_ref, xt_ref, var_ref, varrow_ref, att_ref, wp_ref, mod_ref, wf_ref, wo_ref,
-    mine_ref, send_ref,
-    att_buf, res_buf, fin_buf, sum_buf,
-    *, slots, pairs, channels, height, columns, halves, fold,
+    place_ref, near_ref, far_ref, x_ref, xt_ref, var_ref, varrow_ref, hid_ref, mod_ref, wf_ref, wo_ref, *refs,
+    slots, pairs, channels, height, columns, halves, fold, whole,
 ):
+    *att_refs, mine_ref, send_ref, att_buf, res_buf, fin_buf, sum_buf = refs
     group = place_ref[0]
-    guide = place_ref[2]
-    span = pairs * LANES
-    first = pl.multiple_of(group * span, LANES) if halves == 2 else 0
-    att_buf[:, pl.ds(first, span)] = att_ref[...]
+    guide = place_ref[1]
+    side = place_ref[2] % fold
+
+    def lanes(half, unit):
+        far = jnp.logical_and(unit >= whole, unit < fold * whole)
+        at = jnp.where(far, unit - whole + (1 - side) * whole, unit + side * whole)
+        at = jnp.where(unit >= fold * whole, unit, at) + half * pairs
+        return pl.ds(pl.multiple_of(at * LANES, LANES), LANES)
+
+    unit = 0
+    for ref in att_refs:
+        for at in range(0, ref.shape[1], LANES):
+            att_buf[:, lanes(group, unit)] = ref[:, at : at + LANES]
+            unit += 1
     if halves == 2:
-        other = (1 - group) * span
-
-        def put(pair, value):
-            at = pl.multiple_of(other + pair * LANES, LANES)
-            att_buf[:, pl.ds(at, LANES)] = value
-
-        attend_pairs(place_ref, near_ref, far_ref, x_ref, xt_ref, var_ref, varrow_ref, put, slots, pairs, fold)
-    tokens = x_ref.shape[0]
-    feats, model = wp_ref.shape
-    x = x_ref[:, :feats]
-    tiles = [(at, min(2 * LANES, model - at)) for at in range(0, model, 2 * LANES)]
+
+        def put(unit, value):
+            att_buf[:, lanes(1 - group, unit)] = value
+
+        attend_units(
+            place_ref, near_ref, far_ref, x_ref, xt_ref, var_ref, varrow_ref, put, (0, pairs), slots, pairs, fold
+        )
+    _, model = hid_ref.shape
     sum_buf[...] = jnp.zeros(sum_buf.shape, f32)
 
     def folded(value):
@@ -286,19 +321,33 @@
             total = total + value[:, at : at + LANES]
         return total
 
-    for at, size in tiles:
-        cols = slice(at, at + size)
+    def project(cols):
         mixed = dot(att_buf[...], wo_ref[:, cols])
-        value = dot(x, wp_ref[:, cols]) + mod_ref[2, :, cols] * mixed
+        value = hid_ref[:, cols] + mod_ref[2, :, cols] * mixed
         res_buf[:, cols] = value
         sum_buf[...] = sum_buf[...] + folded(value)
+
+    def sweep(step):
+        size = 2 * LANES
+
+        def body(i, carry):
+            step(pl.ds(pl.multiple_of(i * size, LANES), size))
+            return carry
+
+        lax.fori_loop(0, model // size, body, 0)
+        if model % size:
+            step(slice(model // size * size, model))
+
+    sweep(project)
     mean = jnp.sum(sum_buf[...], axis=1, keepdims=True) * (1.0 / model)
     sum_buf[...] = jnp.zeros(sum_buf.shape, f32)
-    for at, size in tiles:
-        cols = slice(at, at + size)
+
+    def center(cols):
         value = res_buf[:, cols] - mean
         fin_buf[:, cols] = value.astype(bf16)
         sum_buf[...] = sum_buf[...] + folded(value * value)
+
+    sweep(center)
     spread = jnp.sum(sum_buf[...], axis=1, keepdims=True) * (1.0 / model)
     result = dot(fin_buf[...], wf_ref[...], ((1,), (1,))) * lax.rsqrt(spread + epsilon)
     near = height // 2 + 1
@@ -321,11 +370,14 @@
                     send_ref[r - give, :, b * columns : (b + 1) * columns] = piece.astype(bf16)
 
 
-def spread_kernel(place_ref, mine_ref, theirs_ref, lat_ref, own_ref, one_ref, two_ref, back_ref):
-    offset = place_ref[1]
-    guide = place_ref[2]
+def spread_kernel(
+    place_ref, start_ref, mine_ref, theirs_ref, lat_ref, own_ref, odd_ref, two_ref, even_ref
+):
+    guide = place_ref[1]
+    place = place_ref[2]
     near, channels, wide = mine_ref.shape
     columns = wide // 2
+    offset = start_ref[0] - place * columns
     flat = near * channels
     first = guide * (near - 2)
     mine = mine_ref[...].reshape(flat, wide)
@@ -342,7 +394,7 @@
     target = jnp.where(lane > columns + 1, -4 * wide, target)
     edge = iota((flat, columns), 1)
 
-    def place(distance):
+    def spots(distance):
         return jnp.where(col == target + distance * columns, 1.0, 0.0).astype(bf16)
 
     def flagged(values, distance):
@@ -364,35 +416,40 @@
             values = jnp.where(edge == 4 + at, moved, values)
         return values
 
-    here = place(0)
+    here = spots(0)
     own = dot(high, here) + dot(low, here)
     own_ref[:, :columns] = own[:, :columns]
     own_ref[:, columns:] = flagged(own[:, columns:], 0)
-    one = dot(high, place(1))
-    one_ref[:, :columns] = one[:, :columns].astype(bf16)
-    one_ref[:, columns:] = border(flagged(one[:, columns:], 1), columns - 1).astype(bf16)
-    two = dot(high, place(2))
+    one = dot(high, spots(1))
+    one_edge = border(flagged(one[:, columns:], 1), columns - 1)
+    two = dot(high, spots(2))
     two_ref[:, :columns] = two[:, :columns].astype(bf16)
     two_ref[:, columns:] = flagged(two[:, columns:], 2).astype(bf16)
-    back = dot(high, place(-1)[:, columns:])
-    back_ref[...] = border(flagged(back, -1), 0).astype(bf16)
+    back = dot(high, spots(-1)[:, columns:])
+    back_edge = border(flagged(back, -1), 0)
+    odd = place % 2 == 1
+    odd_ref[:, :columns] = one[:, :columns].astype(bf16)
+    even_ref[:, :columns] = one[:, :columns].astype(bf16)
+    odd_ref[:, columns:] = jnp.where(odd, one_edge, back_edge).astype(bf16)
+    even_ref[:, columns:] = jnp.where(odd, back_edge, one_edge).astype(bf16)
 
 
 def decode_kernel(
-    place_ref, own_ref, one_ref, two_ref, back_ref, lat_ref, count_ref, w_ref, den_ref, feat_ref, pad_buf,
+    place_ref, step_ref, own_ref, odd_ref, two_ref, even_ref, lat_ref, count_ref, w_ref, den_ref, feat_ref, pad_buf,
     *, width,
 ):
-    guide = place_ref[2]
-    place = place_ref[3]
+    guide = place_ref[1]
+    place = place_ref[2]
     channels, height, columns = lat_ref.shape
     half = height // 2
     near = half + 1
     flat = near * channels
     first = guide * (near - 2)
-    fraction = (jnp.full((1, columns), place_ref[4], jnp.int32).astype(f32) + 1.0) / STEPS
+    fraction = (jnp.full((1, columns), step_ref[0], jnp.int32).astype(f32) + 1.0) / STEPS
     sigma = 3.0 * fraction / (1.0 + 2.0 * fraction)
-    one = one_ref[...].astype(f32)
-    back = back_ref[...].astype(f32)
+    odd = place % 2 == 1
+    one = jnp.where(odd, even_ref[...], odd_ref[...]).astype(f32)
+    back = jnp.where(odd, odd_ref[:, columns:], even_ref[:, columns:]).astype(f32)
     total = own_ref[...] + one + two_ref[...].astype(f32)
     latent = jnp.concatenate(
         [lat_ref[:, pl.ds(first + i, 1), :].reshape(channels, columns) for i in range(near)], axis=0
@@ -433,25 +490,26 @@
     return lax.ppermute(x, axis, [(0, 1), (1, 0)])
 
 
-def major_route(width, fold, d):
-    return [(i, (i // fold ^ d) * fold + i % fold) for i in range(width)]
+def spread_major(pieces, fold):
+    width = lax.axis_size("width")
+    got = []
+    for d in range(len(pieces), 0, -1):
+        route = [(i, (i // fold ^ d) * fold + i % fold) for i in range(width)]
+        got.append(lax.ppermute(pieces[d - 1], "width", route))
+    return got[::-1]
 
 
 def gather_major(chunk, fold, direct):
     width = lax.axis_size("width")
+    depth = width // fold
     if not direct:
         every = lax.all_gather(chunk, "width")
-        every = every.reshape((width // fold, fold) + chunk.shape)
+        every = every.reshape((depth, fold) + chunk.shape)
         return lax.dynamic_index_in_dim(every, lax.axis_index("width") % fold, 1, False)
-    pieces = [chunk]
-    for d in range(1, width // fold):
-        pieces.append(lax.ppermute(chunk, "width", major_route(width, fold, d)))
-    return jnp.stack(pieces)
-
-
-def swap_minor(stack, fold):
-    if fold == 1:
-        return stack
+    return jnp.stack([chunk] + spread_major([chunk] * (depth - 1), fold))
+
+
+def swap_minor(stack):
     width = lax.axis_size("width")
     return lax.ppermute(stack, "width", [(i, i ^ 1) for i in range(width)])
 
@@ -472,13 +530,12 @@
     if halves == 1:
         group = group * 0
     rows = w_qkv.shape[0]
-    fold = 2 if width % 2 == 0 else 1
+    fold = 2
     depth = width // fold
-    direct = fold == 2 and depth <= 8 and depth & (depth - 1) == 0
+    direct = depth <= 8 and depth & (depth - 1) == 0
     changes = jnp.swapaxes(cond_mod, 0, 1)
-    offset = starts[0] - place * columns
     key = place // fold if direct else 0
-    scalars = jnp.stack([group, offset, guide, place, step_index[0], key]).astype(jnp.int32)
+    scalars = jnp.stack([group, guide, place, key]).astype(jnp.int32)
 
     right = shift(latent, -1)
     further = shift(latent, -2)
@@ -502,47 +559,57 @@
     near = height // 2 + 1
     tokens = height // 2 * columns
     if direct:
-        came = swap_minor(parts[1], fold)
+        came = swap_minor(parts[1])
     else:
         came = lax.all_to_all(parts[0], "width", 0, 0, tiled=True)
-    x, xt, var, varrow = call(
+    x, xt, var, varrow, hidden = call(
         window_kernel,
-        [((tokens, LANES), bf16), ((ROWS, tokens), bf16), ((tokens, LANES), f32), ((8, tokens), f32)],
+        [
+            ((tokens, LANES), bf16), ((ROWS, tokens), bf16), ((tokens, LANES), f32), ((8, tokens), f32),
+            ((tokens, model), f32),
+        ],
         scratch=[
             pltpu.VMEM((height * channels, 3 * columns), bf16),
             pltpu.VMEM((feats, tokens), f32),
-            pltpu.VMEM((tokens, model), f32),
             pltpu.VMEM(w_patch.shape, bf16),
             pltpu.SemaphoreType.DMA((1,)),
         ],
-        anys=(4,), smem=(0,), count=5, flops=5e9,
-    )(scalars, latent, right, further, in_hbm(w_patch))
+        anys=(5,), smem=(0, 1), count=6, flops=5e9,
+    )(scalars, starts, latent, right, further, in_hbm(w_patch))
     came, x = lax.optimization_barrier((came, x))
     if direct:
         own, *sends = call(
             first_sum_kernel, [(slab, f32)] + [(slab, bf16)] * (depth - 1), smem=(0,), count=3, limit=4
         )(scalars, parts[0], came)
-        got = [lax.ppermute(v, "width", major_route(width, fold, d + 1)) for d, v in enumerate(sends)]
+        got = spread_major(sends, fold)
         (chunk,) = call(last_sum_kernel, [(slab, bf16)], count=depth, limit=4)(own, *got)
     else:
         (chunk,) = call(
             functools.partial(sum_kernel, width=width), [(slab, bf16)], count=1, limit=4
         )(came)
     stack = gather_major(chunk, fold, direct)
-    side = swap_minor(stack, fold)
+    side = swap_minor(stack)
+    stack_x = swap(stack, "groups") if halves == 2 else stack
+    whole = local_pairs // fold
+    sizes = dict(slots=slots, pairs=local_pairs, fold=fold)
+    (att_near,) = call(
+        functools.partial(near_kernel, units=(0, whole), **sizes),
+        [((tokens, whole * LANES), bf16)],
+        smem=(0,), count=6, flops=2e9,
+    )(scalars, stack, x, xt, var, varrow)
+    side, att_near = lax.optimization_barrier((side, att_near))
     if halves == 2:
-        stack_x, side_x = swap(stack, "groups"), swap(side, "groups")
+        side_x = swap(side, "groups")
     else:
-        stack_x, side_x = stack, side
-    (att,) = call(
-        functools.partial(first_kernel, slots=slots, pairs=local_pairs, fold=fold),
-        [((tokens, local_pairs * LANES), bf16)],
-        smem=(0,), count=7, flops=6e9,
+        side_x = side
+    (att_far,) = call(
+        functools.partial(attend_kernel, units=(whole, local_pairs), **sizes),
+        [((tokens, (local_pairs - whole) * LANES), bf16)],
+        smem=(0,), count=7, flops=3e9,
     )(scalars, stack, side, x, xt, var, varrow)
     mine_v, send_v = call(
         functools.partial(
-            second_kernel, slots=slots, pairs=local_pairs, channels=channels, height=height,
-            columns=columns, halves=halves, fold=fold,
+            second_kernel, channels=channels, height=height, columns=columns, halves=halves, whole=whole, **sizes
         ),
         [((near, channels, 2 * columns), f32), ((near, channels, 2 * columns), bf16)],
         scratch=[
@@ -551,27 +618,30 @@
             pltpu.VMEM((tokens, model), bf16),
             pltpu.VMEM((tokens, LANES), f32),
         ],
-        smem=(0,), count=12, flops=12e9, limit=22,
-    )(scalars, stack_x, side_x, x, xt, var, varrow, att, w_patch, changes, w_final.T, w_out)
+        smem=(0,), count=13, flops=12e9, limit=22,
+    )(scalars, stack_x, side_x, x, xt, var, varrow, hidden, changes, w_final.T, w_out, att_near, att_far)
     theirs = swap(send_v, "guide")
     flat = near * channels
-    own, one, two, back = call(
+    own, odd, two, even = call(
         spread_kernel,
         [
             ((flat, 2 * columns), f32), ((flat, 2 * columns), bf16),
-            ((flat, 2 * columns), bf16), ((flat, columns), bf16),
+            ((flat, 2 * columns), bf16), ((flat, 2 * columns), bf16),
         ],
-        smem=(0,), count=4, limit=8,
-    )(scalars, mine_v, theirs, latent)
-    one = shift(one, 1)
-    two = shift(two, 2)
-    back = shift(back, -1)
+        smem=(0, 1), count=5, limit=8,
+    )(scalars, starts, mine_v, theirs, latent)
+    ups = [(i, (i + 1) % width) for i in range(width)]
+    turns = [[pair for pair in ups if pair[0] % 2 == side] for side in range(2)]
+    turns = [pairs + [(b, a) for a, b in pairs] for pairs in turns]
+    odd = lax.ppermute(odd, "width", turns[1])
+    two = lax.ppermute(two, "width", [(i, (i + 2) % width) for i in range(width)])
+    even = lax.ppermute(even, "width", turns[0])
     return call(
         functools.partial(decode_kernel, width=width),
         [((channels, height // 2, columns), f32), ((height // 2, columns, w_dec.shape[1]), bf16)],
         scratch=[pltpu.VMEM((3, near + 2, channels, columns), f32)],
-        smem=(0,), count=8, limit=8,
-    )(scalars, own, one, two, back, latent, counts[None], w_dec)
+        smem=(0, 1), count=9, limit=8,
+    )(scalars, step_index, own, odd, two, even, latent, counts[None], w_dec)
 
 
 def solution(mesh):

time: 70.8 us -> 72.6 us (1.025)
  starting transfers between devices: 27.5 us -> 22.5 us
  Pallas kernels: 28.8 us -> 33 us
  waiting for transfers between devices: 11.2 us -> 13.7 us
    ppermute x5 -> x2, starting transfers between devices: 13.3 us -> 6.54 us  [shift(): lax.ppermute(x, 'width', [(i, (i + by) % peers) for i in range(peers)])]
    ppermute x6 -> x9, waiting for transfers between devices: 6.23 us -> 12.5 us  [the longest x6 8.15 us: spread_major(): got.append(lax.ppermute(pieces[d - 1], 'width', route))]
    pallas_call x2 -> x3, Pallas kernels: 16.8 us -> 21.1 us  [the longest x1 14.3 us: shards(): call(functools.partial(second_kernel, channels=channels, height=height, c...]
    ppermute x6 -> x9, starting transfers between devices: 8.9 us -> 11.4 us  [the longest x6 8.9 us: spread_major(): got.append(lax.ppermute(pieces[d - 1], 'width', route))]
    ppermute x2, waiting for transfers between devices: 2.24 us -> 0.01 us  [swap_minor(): return lax.ppermute(stack, 'width', [(i, i ^ 1) for i in range(width)])]
    ppermute x5 -> x2, waiting for transfers between devices: 1.49 us -> 0.01 us  [shift(): lax.ppermute(x, 'width', [(i, (i + by) % peers) for i in range(peers)])]
  transfers between devices with their start and end apart: 16 -> 16, of which waited for: 8 -> 7; matrix products, arithmetic and copies ran while one was open for 0% -> 0% of each run, Pallas kernels for 19% -> 21%
where the time goes in v5:
time: 72.6 us; the launch traced here: 72.3 us
  Pallas kernels  33 us (45%)
  starting transfers between devices  22.5 us (31%)
  waiting for transfers between devices  13.7 us (19%)
  between operations  2.16 us (3%)
  local copies, waits for them, and re-layouts  0.88 us (1%)
    pallas_call x1, Pallas kernels, shards(): call(functools.partial(second_kernel, channels=channels, height=height, c...  14.3 us
    ppermute x6, starting transfers between devices, spread_major(): got.append(lax.ppermute(pieces[d - 1], 'width', route))  8.9 us
    ppermute x6, waiting for transfers between devices, spread_major(): got.append(lax.ppermute(pieces[d - 1], 'width', route))  8.15 us
    ppermute x2, starting transfers between devices, shift(): lax.ppermute(x, 'width', [(i, (i + by) % peers) for i in range(peers)])  6.54 us
    pallas_call x1, Pallas kernels, shards(): call(window_kernel, [((tokens, LANES), bf16), ((ROWS, tokens), bf16), ((t...  4.65 us
    pallas_call x1, Pallas kernels, shards(): call(functools.partial(attend_kernel, units=(whole, local_pairs), **sizes...  3.97 us
    ppermute x1, waiting for transfers between devices, shards(): odd = lax.ppermute(odd, 'width', turns[1])  3.79 us
    pallas_call x1, Pallas kernels, shards(): call(functools.partial(partial_kernel, width=width, slots=slots, local_pa...  3.7 us
  transfers between devices with their start and end apart: 16, of which 7 were waited for; matrix products, arithmetic and copies ran while one was open for 0% of the time, Pallas kernels for 21%

profile of v5, /device:TPU:0, one launch (start us, length us, event | category | flops | bytes accessed | tf_op | source)
XLA Modules:
  0.0 72.3 jit_solution(1977671557282571176)
XLA Ops:
  0.6 6.1 %collective-permute-start.1 = (f32[16,8,128]{2,1,0:T(8,128)}, f32[16,8,128]{2,1,0:T(8,128)S(1)}, u32[]{:S(2)}, u32[]{:S(2)}) collective-permute-start(f32[16,8,128]{2,1,0:T(8,128)} %lat_ref.3), channel_id=1, source_target_pairs={{0,14},{2,0},{4,2},{6,4},{8,6},{10,8},{12,10},{14,12},{1,15},{3,1}... | collective-permute-start | bytes 196616 | tf_op jit(solution)/shard_map/ppermute | solution.py:486
  6.7 0.4 collective-permute-start.2
  7.2 0.1 pad_add_fusion.place_ref
  7.2 3.7 %shard_map.113 = (f32[4,72,256]{2,1,0:T(8,128)S(1)}, bf16[4,72,256]{2,1,0:T(8,128)(2,1)S(1)}) custom-call(s32[4]{0:T(128)S(1)} %pad_add_fusion.place_ref, f32[3,1,2432]{2,1,0:T(1,128)} %bitcast.12, bf16[64,2432]{1,0:T(8,128)(2,1)} %wp_ref.3, bf16[304,3840]{1,0:T(8,128)(2,1)} %w_ref.2), custom_call_target="tpu_custom_call" | custom-call | bytes 1048576 | tf_op jit(solution)/shard_map/pallas_call | solution.py:545
  11.0 0.7 collective-permute-start
  12.3 0.0 collective-permute-done.1.right_ref
  12.3 0.0 collective-permute-done.2.further_ref
  12.3 0.0 copy-start
  12.3 0.8 %copy-done = f32[16,8,128]{2,1,0:T(8,128)S(1)} copy-done((f32[16,8,128]{2,1,0:T(8,128)S(1)}, f32[16,8,128]{2,1,0:T(8,128)}, u32[]{:S(2)}) %copy-start) | copy-done | bytes 65560
  13.2 4.7 %shard_map.114 = (bf16[512,128]{1,0:T(8,128)(2,1)S(1)}, bf16[72,512]{1,0:T(8,128)(2,1)S(1)}, f32[512,128]{1,0:T(8,128)S(1)}, f32[8,512]{1,0:T(8,128)S(1)}, f32[512,2432]{1,0:T(8,128)S(1)}) custom-call(s32[4]{0:T(128)S(1)} %pad_add_fusion.place_ref, s32[1]{0:T(128)S(6)} %copy.12.start_ref, f32[16,8,128]{2,1,0:T(8,128)S(1)} %copy-done, ...), custom_call_target="tpu_custom_call" | custom-call | flops 5000000000 | bytes 1048576 | tf_op jit(solution)/shard_map/pallas_call | solution.py:565
  17.8 0.0 collective-permute-done.came_ref
  17.8 0.6 shard_map.115
  18.4 1.0 %collective-permute-start.3 = (bf16[72,256]{1,0:T(8,128)(2,1)S(1)}, bf16[72,256]{1,0:T(8,128)(2,1)S(1)}, u32[]{:S(2)}, u32[]{:S(2)}) collective-permute-start(bf16[72,256]{1,0:T(8,128)(2,1)S(1)} %get-tuple-element.28), channel_id=1, source_target_pairs={{0,4},{2,6},{4,0},{6,2},{8,12},{10,14},{12,8},{14,10},{1,5},{3,7},... | collective-permute-start | bytes 110600 | tf_op jit(solution)/shard_map/ppermute | solution.py:498
  19.4 1.2 %collective-permute-start.4 = (bf16[72,256]{1,0:T(8,128)(2,1)S(1)}, bf16[72,256]{1,0:T(8,128)(2,1)S(1)}, u32[]{:S(2)}, u32[]{:S(2)}) collective-permute-start(bf16[72,256]{1,0:T(8,128)(2,1)S(1)} %get-tuple-element.29), channel_id=1, source_target_pairs={{0,8},{2,10},{4,12},{6,14},{8,0},{10,2},{12,4},{14,6},{1,9},{3,11}... | collective-permute-start | bytes 110600 | tf_op jit(solution)/shard_map/ppermute | solution.py:498
  20.7 2.2 %collective-permute-start.5 = (bf16[72,256]{1,0:T(8,128)(2,1)S(1)}, bf16[72,256]{1,0:T(8,128)(2,1)S(1)}, u32[]{:S(2)}, u32[]{:S(2)}) collective-permute-start(bf16[72,256]{1,0:T(8,128)(2,1)S(1)} %get-tuple-element.30), channel_id=1, source_target_pairs={{0,12},{2,14},{4,8},{6,10},{8,4},{10,6},{12,0},{14,2},{1,13},{3,15... | collective-permute-start | bytes 110600 | tf_op jit(solution)/shard_map/ppermute | solution.py:498
  22.9 0.0 collective-permute-done.3.refs_1_
  22.9 1.4 %collective-permute-done.4.refs_2_ = bf16[72,256]{1,0:T(8,128)(2,1)S(1)} collective-permute-done((bf16[72,256]{1,0:T(8,128)(2,1)S(1)}, bf16[72,256]{1,0:T(8,128)(2,1)S(1)}, u32[]{:S(2)}, u32[]{:S(2)}) %collective-permute-start.4) | collective-permute-done | bytes 36896 | tf_op jit(solution)/shard_map/ppermute | solution.py:498
  24.3 2.2 %collective-permute-done.5.refs_3_ = bf16[72,256]{1,0:T(8,128)(2,1)S(1)} collective-permute-done((bf16[72,256]{1,0:T(8,128)(2,1)S(1)}, bf16[72,256]{1,0:T(8,128)(2,1)S(1)}, u32[]{:S(2)}, u32[]{:S(2)}) %collective-permute-start.5) | collective-permute-done | bytes 36896 | tf_op jit(solution)/shard_map/ppermute | solution.py:498
  26.5 0.1 collective-permute-start.6
  26.6 3.2 %collective-permute-start.7 = (bf16[72,256]{1,0:T(8,128)(2,1)S(1)}, bf16[72,256]{1,0:T(8,128)(2,1)S(1)}, u32[]{:S(2)}, u32[]{:S(2)}) collective-permute-start(bf16[72,256]{1,0:T(8,128)(2,1)S(1)} %shard_map.116), channel_id=1, source_target_pairs={{0,8},{2,10},{4,12},{6,14},{8,0},{10,2},{12,4},{14,6},{1,9},{3,11}... | collective-permute-start | bytes 110600 | tf_op jit(solution)/shard_map/ppermute | solution.py:498
  29.7 1.2 %collective-permute-start.8 = (bf16[72,256]{1,0:T(8,128)(2,1)S(1)}, bf16[72,256]{1,0:T(8,128)(2,1)S(1)}, u32[]{:S(2)}, u32[]{:S(2)}) collective-permute-start(bf16[72,256]{1,0:T(8,128)(2,1)S(1)} %shard_map.116), channel_id=1, source_target_pairs={{0,12},{2,14},{4,8},{6,10},{8,4},{10,6},{12,0},{14,2},{1,13},{3,15... | collective-permute-start | bytes 110600 | tf_op jit(solution)/shard_map/ppermute | solution.py:498
  31.0 0.0 collective-permute-done.6
  31.0 0.7 collective-permute-done.7
  31.7 3.8 %collective-permute-done.8 = bf16[72,256]{1,0:T(8,128)(2,1)S(1)} collective-permute-done((bf16[72,256]{1,0:T(8,128)(2,1)S(1)}, bf16[72,256]{1,0:T(8,128)(2,1)S(1)}, u32[]{:S(2)}, u32[]{:S(2)}) %collective-permute-start.8) | collective-permute-done | bytes 36896 | tf_op jit(solution)/shard_map/ppermute | solution.py:498
  35.5 1.0 %collective-permute-start.10 = (bf16[4,72,256]{2,1,0:T(8,128)(2,1)S(1)}, bf16[4,72,256]{2,1,0:T(8,128)(2,1)S(1)}, u32[]{:S(2)}, u32[]{:S(2)}) collective-permute-start(bf16[4,72,256]{2,1,0:T(8,128)(2,1)S(1)} %pad_maximum_fusion.near_ref), channel_id=1, source_target_pairs={{0,2},{2,0},{4,6},{6,4},{8,10},{10,8},{12,14},{14,12},{1,3},{3,1},... | collective-permute-start | bytes 442376 | tf_op jit(solution)/shard_map/ppermute | solution.py:514
  36.5 1.5 %collective-permute-start.9 = (bf16[4,72,256]{2,1,0:T(8,128)(2,1)S(1)}, bf16[4,72,256]{2,1,0:T(8,128)(2,1)S(1)}, u32[]{:S(2)}, u32[]{:S(2)}) collective-permute-start(bf16[4,72,256]{2,1,0:T(8,128)(2,1)S(1)} %pad_maximum_fusion.near_ref), channel_id=1, source_target_pairs={{0,16},{16,0},{1,17},{17,1},{2,18},{18,2},{3,19},{19,3},{4,20},{20... | collective-permute-start | bytes 442376 | tf_op jit(solution)/shard_map/ppermute | solution.py:490
  38.0 2.8 %shard_map.117.refs_0_ = bf16[512,256]{1,0:T(8,128)(2,1)S(1)} custom-call(s32[4]{0:T(128)S(1)} %pad_add_fusion.place_ref, bf16[4,72,256]{2,1,0:T(8,128)(2,1)S(1)} %pad_maximum_fusion.near_ref, bf16[512,128]{1,0:T(8,128)(2,1)S(1)} %get-tuple-element.31.x_ref, bf16[72,512]{1,0:T(8,128)(2,1)S(1)} %get-tuple-element.32.xt_ref, ...), custom_call_target="tpu_custom_call" | custom-call | flops 2000000000 | bytes 1048576 | tf_op jit(solution)/shard_map/pallas_call | solution.py:595
  40.9 0.0 copy-start.3
  40.9 0.0 slice-start.1
  40.9 0.0 copy-start.5
  40.9 0.0 collective-permute-done.10.far_ref
  40.9 1.3 %collective-permute-start.11 = (bf16[4,72,256]{2,1,0:T(8,128)(2,1)S(1)}, bf16[4,72,256]{2,1,0:T(8,128)(2,1)S(1)}, u32[]{:S(2)}, u32[]{:S(2)}) collective-permute-start(bf16[4,72,256]{2,1,0:T(8,128)(2,1)S(1)} %collective-permute-done.10.far_ref), channel_id=1, source_target_pairs={{0,16},{16,0},{1,17},{17,1},{2,18},{18,2},{3,19},{19,3},{4,20},{20... | collective-permute-start | bytes 442376 | tf_op jit(solution)/shard_map/ppermute | solution.py:490
  42.2 4.0 %shard_map.118.refs_1_ = bf16[512,384]{1,0:T(8,128)(2,1)S(1)} custom-call(s32[4]{0:T(128)S(1)} %pad_add_fusion.place_ref, bf16[4,72,256]{2,1,0:T(8,128)(2,1)S(1)} %pad_maximum_fusion.near_ref, bf16[4,72,256]{2,1,0:T(8,128)(2,1)S(1)} %collective-permute-done.10.far_ref, bf16[512,128]{1,0:T(8,128)(2,1)S(1)} %get-tuple-element.31.x_ref, ...), custom_call_target="tpu_custom_call" | custom-call | flops 3000000000 | bytes 1048576 | tf_op jit(solution)/shard_map/pallas_call | solution.py:605
  46.2 0.0 collective-permute-done.9.near_ref
  46.2 0.0 collective-permute-done.11.far_ref
  46.3 0.0 copy-start.1
  46.3 0.0 copy-start.2
  46.3 0.0 copy-start.4
  46.3 14.3 %shard_map.119 = (f32[5,16,256]{2,1,0:T(8,128)S(1)}, bf16[5,16,256]{2,1,0:T(8,128)(2,1)S(1)}) custom-call(s32[4]{0:T(128)S(1)} %pad_add_fusion.place_ref, bf16[4,72,256]{2,1,0:T(8,128)(2,1)S(1)} %collective-permute-done.9.near_ref, bf16[4,72,256]{2,1,0:T(8,128)(2,1)S(1)} %collective-permute-done.11.far_ref, bf16[512,128]{1,0:T(8,128)(2,1)S(1)} %get-tuple-element.31.x_ref, ...), custom_call_target="tpu_custom_call" | custom-call | flops 12000000000 | bytes 1048576 | tf_op jit(solution)/shard_map/pallas_call | solution.py:610
  60.6 0.1 collective-permute-start.12
  60.7 1.2 %collective-permute-done.12.theirs_ref = bf16[5,16,256]{2,1,0:T(8,128)(2,1)S(1)} collective-permute-done((bf16[5,16,256]{2,1,0:T(8,128)(2,1)S(1)}, bf16[5,16,256]{2,1,0:T(8,128)(2,1)S(1)}, u32[]{:S(2)}, u32[]{:S(2)}) %collective-permute-start.12) | collective-permute-done | bytes 40992 | tf_op jit(solution)/shard_map/ppermute | solution.py:490
  61.9 0.8 %shard_map.120 = (f32[80,256]{1,0:T(8,128)S(1)}, bf16[80,256]{1,0:T(8,128)(2,1)S(1)}, bf16[80,256]{1,0:T(8,128)(2,1)S(1)}, bf16[80,256]{1,0:T(8,128)(2,1)S(1)}) custom-call(s32[4]{0:T(128)S(1)} %pad_add_fusion.place_ref, s32[1]{0:T(128)S(6)} %copy.12.start_ref, f32[5,16,256]{2,1,0:T(8,128)S(1)} %get-tuple-element.38.mine_ref, ...), custom_call_target="tpu_custom_call" | custom-call | bytes 1048576 | tf_op jit(solution)/shard_map/pallas_call | solution.py:625
  62.8 1.7 %collective-permute-start.13 = (bf16[80,256]{1,0:T(8,128)(2,1)S(1)}, bf16[80,256]{1,0:T(8,128)(2,1)S(1)}, u32[]{:S(2)}, u32[]{:S(2)}) collective-permute-start(bf16[80,256]{1,0:T(8,128)(2,1)S(1)} %get-tuple-element.41), channel_id=1, source_target_pairs={{2,4},{6,8},{10,12},{14,0},{4,2},{8,6},{12,10},{0,14},{3,5},{7,9},... | collective-permute-start | bytes 122888 | tf_op jit(solution)/shard_map/ppermute | solution.py:636
  64.5 0.8 %collective-permute-start.14 = (bf16[80,256]{1,0:T(8,128)(2,1)S(1)}, bf16[80,256]{1,0:T(8,128)(2,1)S(1)}, u32[]{:S(2)}, u32[]{:S(2)}) collective-permute-start(bf16[80,256]{1,0:T(8,128)(2,1)S(1)} %get-tuple-element.42), channel_id=1, source_target_pairs={{0,4},{2,6},{4,8},{6,10},{8,12},{10,14},{12,0},{14,2},{1,5},{3,7},... | collective-permute-start | bytes 122888 | tf_op jit(solution)/shard_map/ppermute | solution.py:637
  65.3 0.0 collective-permute-start.15
  65.9 3.8 %collective-permute-done.13.odd_ref = bf16[80,256]{1,0:T(8,128)(2,1)S(1)} collective-permute-done((bf16[80,256]{1,0:T(8,128)(2,1)S(1)}, bf16[80,256]{1,0:T(8,128)(2,1)S(1)}, u32[]{:S(2)}, u32[]{:S(2)}) %collective-permute-start.13) | collective-permute-done | bytes 40992 | tf_op jit(solution)/shard_map/ppermute | solution.py:636
  69.7 0.6 collective-permute-done.14.two_ref
  70.3 2.1 %shard_map.121 = (f32[16,4,128]{2,1,0:T(4,128)}, bf16[4,128,512]{2,1,0:T(8,128)(2,1)}) custom-call(s32[4]{0:T(128)S(1)} %pad_add_fusion.place_ref, s32[1]{0:T(128)S(6)} %copy.13.step_ref, f32[80,256]{1,0:T(8,128)S(1)} %get-tuple-element.40.own_ref, bf16[80,256]{1,0:T(8,128)(2,1)S(1)} %collective-permute-done.13.odd_ref, ...), custom_call_target="tpu_custom_call" | custom-call | bytes 1048576 | tf_op jit(solution)/shard_map/pallas_call | solution.py:639
  (12 shorter events, 0.1 us)
Async XLA Ops:
  0.6 11.7 %collective-permute-start.1 = (f32[16,8,128]{2,1,0:T(8,128)}, f32[16,8,128]{2,1,0:T(8,128)S(1)}, u32[]{:S(2)}, u32[]{:S(2)}) collective-permute-start(f32[16,8,128]{2,1,0:T(8,128)} %lat_ref.3), channel_id=1, source_target_pairs={{0,14},{2,0},{4,2},{6,4},{8,6},{10,8},{12,10},{14,12},{1,15},{3,1}... | collective-permute-start | bytes 196616 | tf_op jit(solution)/shard_map/ppermute | solution.py:486
  6.7 5.6 %collective-permute-start.2 = (f32[16,8,128]{2,1,0:T(8,128)}, f32[16,8,128]{2,1,0:T(8,128)S(1)}, u32[]{:S(2)}, u32[]{:S(2)}) collective-permute-start(f32[16,8,128]{2,1,0:T(8,128)} %lat_ref.3), channel_id=1, source_target_pairs={{0,12},{2,14},{4,0},{6,2},{8,4},{10,6},{12,8},{14,10},{1,13},{3,15... | collective-permute-start | bytes 196616 | tf_op jit(solution)/shard_map/ppermute | solution.py:486
  11.0 6.9 %collective-permute-start = (bf16[4,72,256]{2,1,0:T(8,128)(2,1)S(1)}, bf16[4,72,256]{2,1,0:T(8,128)(2,1)S(1)}, u32[]{:S(2)}, u32[]{:S(2)}) collective-permute-start(bf16[4,72,256]{2,1,0:T(8,128)(2,1)S(1)} %get-tuple-element.24), channel_id=1, source_target_pairs={{0,2},{2,0},{4,6},{6,4},{8,10},{10,8},{12,14},{14,12},{1,3},{3,1},... | collective-permute-start | bytes 442376 | tf_op jit(solution)/shard_map/ppermute | solution.py:514
  12.3 0.8 %copy-start = (f32[16,8,128]{2,1,0:T(8,128)S(1)}, f32[16,8,128]{2,1,0:T(8,128)}, u32[]{:S(2)}) copy-start(f32[16,8,128]{2,1,0:T(8,128)} %lat_ref.3) | copy-start | bytes 196612
  18.4 4.5 %collective-permute-start.3 = (bf16[72,256]{1,0:T(8,128)(2,1)S(1)}, bf16[72,256]{1,0:T(8,128)(2,1)S(1)}, u32[]{:S(2)}, u32[]{:S(2)}) collective-permute-start(bf16[72,256]{1,0:T(8,128)(2,1)S(1)} %get-tuple-element.28), channel_id=1, source_target_pairs={{0,4},{2,6},{4,0},{6,2},{8,12},{10,14},{12,8},{14,10},{1,5},{3,7},... | collective-permute-start | bytes 110600 | tf_op jit(solution)/shard_map/ppermute | solution.py:498
  19.4 4.9 %collective-permute-start.4 = (bf16[72,256]{1,0:T(8,128)(2,1)S(1)}, bf16[72,256]{1,0:T(8,128)(2,1)S(1)}, u32[]{:S(2)}, u32[]{:S(2)}) collective-permute-start(bf16[72,256]{1,0:T(8,128)(2,1)S(1)} %get-tuple-element.29), channel_id=1, source_target_pairs={{0,8},{2,10},{4,12},{6,14},{8,0},{10,2},{12,4},{14,6},{1,9},{3,11}... | collective-permute-start | bytes 110600 | tf_op jit(solution)/shard_map/ppermute | solution.py:498
  20.7 5.8 %collective-permute-start.5 = (bf16[72,256]{1,0:T(8,128)(2,1)S(1)}, bf16[72,256]{1,0:T(8,128)(2,1)S(1)}, u32[]{:S(2)}, u32[]{:S(2)}) collective-permute-start(bf16[72,256]{1,0:T(8,128)(2,1)S(1)} %get-tuple-element.30), channel_id=1, source_target_pairs={{0,12},{2,14},{4,8},{6,10},{8,4},{10,6},{12,0},{14,2},{1,13},{3,15... | collective-permute-start | bytes 110600 | tf_op jit(solution)/shard_map/ppermute | solution.py:498
  26.5 4.5 %collective-permute-start.6 = (bf16[72,256]{1,0:T(8,128)(2,1)S(1)}, bf16[72,256]{1,0:T(8,128)(2,1)S(1)}, u32[]{:S(2)}, u32[]{:S(2)}) collective-permute-start(bf16[72,256]{1,0:T(8,128)(2,1)S(1)} %shard_map.116), channel_id=1, source_target_pairs={{0,4},{2,6},{4,0},{6,2},{8,12},{10,14},{12,8},{14,10},{1,5},{3,7},... | collective-permute-start | bytes 110600 | tf_op jit(solution)/shard_map/ppermute | solution.py:498
  26.6 5.1 %collective-permute-start.7 = (bf16[72,256]{1,0:T(8,128)(2,1)S(1)}, bf16[72,256]{1,0:T(8,128)(2,1)S(1)}, u32[]{:S(2)}, u32[]{:S(2)}) collective-permute-start(bf16[72,256]{1,0:T(8,128)(2,1)S(1)} %shard_map.116), channel_id=1, source_target_pairs={{0,8},{2,10},{4,12},{6,14},{8,0},{10,2},{12,4},{14,6},{1,9},{3,11}... | collective-permute-start | bytes 110600 | tf_op jit(solution)/shard_map/ppermute | solution.py:498
  29.7 5.8 %collective-permute-start.8 = (bf16[72,256]{1,0:T(8,128)(2,1)S(1)}, bf16[72,256]{1,0:T(8,128)(2,1)S(1)}, u32[]{:S(2)}, u32[]{:S(2)}) collective-permute-start(bf16[72,256]{1,0:T(8,128)(2,1)S(1)} %shard_map.116), channel_id=1, source_target_pairs={{0,12},{2,14},{4,8},{6,10},{8,4},{10,6},{12,0},{14,2},{1,13},{3,15... | collective-permute-start | bytes 110600 | tf_op jit(solution)/shard_map/ppermute | solution.py:498
  35.5 5.4 %collective-permute-start.10 = (bf16[4,72,256]{2,1,0:T(8,128)(2,1)S(1)}, bf16[4,72,256]{2,1,0:T(8,128)(2,1)S(1)}, u32[]{:S(2)}, u32[]{:S(2)}) collective-permute-start(bf16[4,72,256]{2,1,0:T(8,128)(2,1)S(1)} %pad_maximum_fusion.near_ref), channel_id=1, source_target_pairs={{0,2},{2,0},{4,6},{6,4},{8,10},{10,8},{12,14},{14,12},{1,3},{3,1},... | collective-permute-start | bytes 442376 | tf_op jit(solution)/shard_map/ppermute | solution.py:514
  36.5 9.7 %collective-permute-start.9 = (bf16[4,72,256]{2,1,0:T(8,128)(2,1)S(1)}, bf16[4,72,256]{2,1,0:T(8,128)(2,1)S(1)}, u32[]{:S(2)}, u32[]{:S(2)}) collective-permute-start(bf16[4,72,256]{2,1,0:T(8,128)(2,1)S(1)} %pad_maximum_fusion.near_ref), channel_id=1, source_target_pairs={{0,16},{16,0},{1,17},{17,1},{2,18},{18,2},{3,19},{19,3},{4,20},{20... | collective-permute-start | bytes 442376 | tf_op jit(solution)/shard_map/ppermute | solution.py:490
  38.0 8.2 %slice-start = ((s8[6225920]{0:T(1024)(128)(4,1)}), s8[4194304]{0:T(1024)(128)(4,1)S(1)}, s32[]{:S(2)}) async-start(s8[6225920]{0:T(1024)(128)(4,1)} %bitcast.15), calls=%async_computation | async-start | bytes 8388608
  40.9 5.4 %copy-start.3 = (f32[1,3,2432]{2,0,1:T(1,128)S(1)}, f32[1,3,2432]{2,0,1:T(1,128)}, u32[]{:S(2)}) copy-start(f32[1,3,2432]{2,0,1:T(1,128)} %param.14) | copy-start | bytes 87556
  40.9 5.4 %slice-start.1 = ((s8[6225920]{0:T(1024)(128)(4,1)}), s8[2031616]{0:T(1024)(128)(4,1)S(1)}, s32[]{:S(2)}) async-start(s8[6225920]{0:T(1024)(128)(4,1)} %bitcast.15), calls=%async_computation.1 | async-start | bytes 4063232
  40.9 5.4 %copy-start.5 = (bf16[2432,64]{0,1:T(8,128)(2,1)S(1)}, bf16[2432,64]{0,1:T(8,128)(2,1)}, u32[]{:S(2)}) copy-start(bf16[2432,64]{0,1:T(8,128)(2,1)} %param.18) | copy-start | bytes 933892
  40.9 5.3 %collective-permute-start.11 = (bf16[4,72,256]{2,1,0:T(8,128)(2,1)S(1)}, bf16[4,72,256]{2,1,0:T(8,128)(2,1)S(1)}, u32[]{:S(2)}, u32[]{:S(2)}) collective-permute-start(bf16[4,72,256]{2,1,0:T(8,128)(2,1)S(1)} %collective-permute-done.10.far_ref), channel_id=1, source_target_pairs={{0,16},{16,0},{1,17},{17,1},{2,18},{18,2},{3,19},{19,3},{4,20},{20... | collective-permute-start | bytes 442376 | tf_op jit(solution)/shard_map/ppermute | solution.py:490
  46.3 15.7 %copy-start.1 = (f32[16,8,128]{2,1,0:T(8,128)S(1)}, f32[16,8,128]{2,1,0:T(8,128)}, u32[]{:S(2)}) copy-start(f32[16,8,128]{2,1,0:T(8,128)} %lat_ref.3) | copy-start | bytes 196612
  46.3 24.0 %copy-start.2 = (bf16[144,512]{1,0:T(8,128)(2,1)S(1)}, bf16[144,512]{1,0:T(8,128)(2,1)}, u32[]{:S(2)}) copy-start(bf16[144,512]{1,0:T(8,128)(2,1)} %w_ref.3) | copy-start | bytes 442372
  46.3 24.0 %copy-start.4 = (s32[128]{0:T(128)S(1)}, s32[128]{0:T(128)}, u32[]{:S(2)}) copy-start(s32[128]{0:T(128)} %param.12) | copy-start | bytes 1540
  60.6 1.3 %collective-permute-start.12 = (bf16[5,16,256]{2,1,0:T(8,128)(2,1)S(1)}, bf16[5,16,256]{2,1,0:T(8,128)(2,1)S(1)}, u32[]{:S(2)}, u32[]{:S(2)}) collective-permute-start(bf16[5,16,256]{2,1,0:T(8,128)(2,1)S(1)} %get-tuple-element.39), channel_id=1, source_target_pairs={{0,1},{1,0},{2,3},{3,2},{4,5},{5,4},{6,7},{7,6},{8,9},{9,8},{10,11... | collective-permute-start | bytes 122888 | tf_op jit(solution)/shard_map/ppermute | solution.py:490
  62.8 6.9 %collective-permute-start.13 = (bf16[80,256]{1,0:T(8,128)(2,1)S(1)}, bf16[80,256]{1,0:T(8,128)(2,1)S(1)}, u32[]{:S(2)}, u32[]{:S(2)}) collective-permute-start(bf16[80,256]{1,0:T(8,128)(2,1)S(1)} %get-tuple-element.41), channel_id=1, source_target_pairs={{2,4},{6,8},{10,12},{14,0},{4,2},{8,6},{12,10},{0,14},{3,5},{7,9},... | collective-permute-start | bytes 122888 | tf_op jit(solution)/shard_map/ppermute | solution.py:636
  64.5 5.8 %collective-permute-start.14 = (bf16[80,256]{1,0:T(8,128)(2,1)S(1)}, bf16[80,256]{1,0:T(8,128)(2,1)S(1)}, u32[]{:S(2)}, u32[]{:S(2)}) collective-permute-start(bf16[80,256]{1,0:T(8,128)(2,1)S(1)} %get-tuple-element.42), channel_id=1, source_target_pairs={{0,4},{2,6},{4,8},{6,10},{8,12},{10,14},{12,0},{14,2},{1,5},{3,7},... | collective-permute-start | bytes 122888 | tf_op jit(solution)/shard_map/ppermute | solution.py:637
  65.3 5.0 %collective-permute-start.15 = (bf16[80,256]{1,0:T(8,128)(2,1)S(1)}, bf16[80,256]{1,0:T(8,128)(2,1)S(1)}, u32[]{:S(2)}, u32[]{:S(2)}) collective-permute-start(bf16[80,256]{1,0:T(8,128)(2,1)S(1)} %get-tuple-element.43), channel_id=1, source_target_pairs={{0,2},{4,6},{8,10},{12,14},{2,0},{6,4},{10,8},{14,12},{1,3},{5,7},... | collective-permute-start | bytes 122888 | tf_op jit(solution)/shard_map/ppermute | solution.py:638

commit v6 on v5

--- a/solution.py
+++ b/solution.py
@@ -14,6 +14,7 @@
 LANES = 128
 ROWS = 72
 
+
 guidance = 4.0
 epsilon = 1e-06
 
@@ -27,7 +28,7 @@
     return lax.dot_general(a, b, (dims, ((), ())), preferred_element_type=f32)
 
 
-def call(body, outs, scratch=(), anys=(), smem=(), count=0, limit=16, flops=0):
+def call(body, outs, scratch=(), anys=(), smem=(), count=0, limit=16, flops=0, hbm_outs=()):
     def spec(i):
         if i in anys:
             return pl.BlockSpec(memory_space=pltpu.HBM)
@@ -39,7 +40,9 @@
         body,
         out_shape=tuple(jax.ShapeDtypeStruct(s, t) for s, t in outs),
         in_specs=[spec(i) for i in range(count)],
-        out_specs=tuple(pl.BlockSpec(memory_space=pltpu.VMEM) for _ in outs),
+        out_specs=tuple(
+            pl.BlockSpec(memory_space=pltpu.HBM if i in hbm_outs else pltpu.VMEM) for i in range(len(outs))
+        ),
         scratch_shapes=list(scratch),
         compiler_params=pltpu.CompilerParams(vmem_limit_bytes=limit << 20),
         cost_estimate=pl.CostEstimate(flops=int(flops), bytes_accessed=1 << 20, transcendentals=0),
@@ -68,7 +71,7 @@
 def partial_kernel(
     place_ref, mod_ref, wp_ref, w_ref, *refs, width, slots, local_pairs, features, fold, direct
 ):
-    *out_refs, w_buf, mod_buf, wp_buf, sems = refs
+    *out_refs, w_buf, mod_buf, wp_buf, all_buf, sems = refs
     group = place_ref[0]
     span = local_pairs * LANES
     loads = [
@@ -100,7 +103,7 @@
     a = jnp.concatenate(split(stacked), axis=0)[:, :rows]
     for one in loads[2:]:
         one.wait()
-    side = place_ref[2] % fold
+    place = place_ref[2]
     _, sides = layout(local_pairs, width // fold, slots, fold)
     for owner in range(width):
         z, y = divmod(owner, fold)
@@ -114,17 +117,13 @@
             else:
                 pieces.append(jnp.zeros((ROWS, LANES), f32))
         value = jnp.concatenate(pieces, axis=1)
-        if not direct:
+        if direct:
+            all_buf[owner ^ place] = value
+        else:
             out_refs[0][owner] = value.astype(bf16)
-            continue
-
-        @pl.when(side == y)
-        def _():
-            out_refs[0][z] = value
-
-        @pl.when(side != y)
-        def _():
-            out_refs[1][z] = value.astype(bf16)
+    if direct:
+        for d, ref in enumerate(out_refs):
+            ref[...] = all_buf[d].astype(ref.dtype)
 
 
 def sum_kernel(parts_ref, out_ref, *, width):
@@ -134,15 +133,7 @@
     out_ref[...] = total.astype(bf16)
 
 
-def first_sum_kernel(place_ref, keep_ref, came_ref, own_ref, *send_refs):
-    key = place_ref[3]
-    own_ref[...] = keep_ref[key] + came_ref[key].astype(f32)
-    for d, ref in enumerate(send_refs):
-        at = key ^ (d + 1)
-        ref[...] = (keep_ref[at] + came_ref[at].astype(f32)).astype(bf16)
-
-
-def last_sum_kernel(*refs):
+def direct_sum_kernel(*refs):
     *parts, out_ref = refs
     total = parts[0][...]
     for ref in parts[1:]:
@@ -153,17 +144,22 @@
 def window_kernel(
     place_ref, start_ref, own_ref, right_ref, further_ref, wp_ref,
     x_ref, xt_ref, var_ref, varrow_ref, hid_ref,
-    rows_buf, xt_buf, w_ref, sem,
+    rows_buf, xt_buf, w_ref, own_buf, sem,
 ):
     load = pltpu.make_async_copy(wp_ref, w_ref, sem.at[0])
+    load_own = pltpu.make_async_copy(own_ref, own_buf, sem.at[1])
+    load_own.start()
     load.start()
     channels, height, columns = own_ref.shape
-    offset = start_ref[0] - place_ref[2] * columns
+    offset = start_ref[...] - place_ref[2] * columns
     for r in range(height):
         at = slice(r * channels, (r + 1) * channels)
-        rows_buf[at, :columns] = own_ref[:, r, :].astype(bf16)
         rows_buf[at, columns : 2 * columns] = right_ref[:, r, :].astype(bf16)
         rows_buf[at, 2 * columns :] = further_ref[:, r, :].astype(bf16)
+    load_own.wait()
+    for r in range(height):
+        at = slice(r * channels, (r + 1) * channels)
+        rows_buf[at, :columns] = own_buf[:, r, :].astype(bf16)
     col = iota((3 * columns, 2 * columns), 0)
     spot = iota((3 * columns, 2 * columns), 1)
     b = (spot >= columns).astype(jnp.int32)
@@ -219,61 +215,63 @@
     x = x_ref[:, :ROWS]
     scale = LOG2E * HEAD**-0.5
 
+    xt = xt_ref[...]
+    var = var_ref[...]
+    rstd = lax.rsqrt(var + epsilon)
+    eps_col = epsilon * (var + epsilon)
+    eps_row = epsilon * (varrow_ref[:1, :] + epsilon)
+    low = iota((tokens, LANES), 1) < HEAD
+    ones = jnp.where(low, 1.0, 0.0).astype(bf16)
+    other = jnp.where(low, 0.0, 1.0).astype(bf16)
+    blank = jnp.zeros((HEAD, tokens), bf16)
+
+    def read(ref, spot):
+        slot = spot % slots
+        return ref[(spot // slots) ^ key, :, slot * LANES : (slot + 1) * LANES]
+
     def tile(unit, sub):
-        far = jnp.logical_and(unit >= whole, unit < fold * whole)
-        spot = 3 * (unit - jnp.where(far, whole, 0)) + sub
-        for pair in range(fold * whole, pairs):
-            y = next(y for y in range(fold) if (pair, sub) in sides[y])
-            mine = unit == pair
-            far = jnp.where(mine, side != y, far)
-            spot = jnp.where(mine, sides[y].index((pair, sub)), spot)
-        at = (
-            (spot // slots) ^ key,
-            slice(None),
-            pl.ds(pl.multiple_of(spot % slots * LANES, LANES), LANES),
-        )
-        return jnp.where(far, far_ref[at], near_ref[at])
-
-    def one(unit, carry):
+        if unit < whole:
+            return read(near_ref, 3 * unit + sub)
+        if unit < fold * whole:
+            return read(far_ref, 3 * (unit - whole) + sub)
+        y = next(y for y in range(fold) if (unit, sub) in sides[y])
+        spot = sides[y].index((unit, sub))
+        return jnp.where(side == y, read(near_ref, spot), read(far_ref, spot))
+
+    for unit in range(*units):
         mq, mv, mk = (tile(unit, sub) for sub in range(3))
-        low = iota((tokens, LANES), 1) < HEAD
-        var = var_ref[...]
         both = dot(x, jnp.concatenate([mq, mv], axis=1))
         uq = both[:, :LANES]
-        uv = both[:, LANES:] * lax.rsqrt(var + epsilon)
-        uk = dot(mk, xt_ref[...], ((0,), (0,)))
+        uv = both[:, LANES:] * rstd
+        uk = dot(mk, xt, ((0,), (0,)))
         sq = uq * uq
         sum_low = jnp.sum(jnp.where(low, sq, 0.0), axis=1, keepdims=True)
         sum_high = jnp.sum(jnp.where(low, 0.0, sq), axis=1, keepdims=True)
-        mean = jnp.where(low, sum_low, sum_high) * (1.0 / HEAD)
-        q = uq * lax.rsqrt(mean + epsilon * (var + epsilon))
-        eps_row = epsilon * (varrow_ref[:1, :] + epsilon)
-        keys = []
+        q = (uq * lax.rsqrt(jnp.where(low, sum_low, sum_high) * (1.0 / HEAD) + eps_col)).astype(bf16)
+        weights = []
         for half in range(2):
             k = uk[half * HEAD : (half + 1) * HEAD]
             mean = jnp.sum(k * k, axis=0, keepdims=True) * (1.0 / HEAD)
-            keys.append((k * lax.rsqrt(mean + eps_row)).astype(bf16))
-        kt = jnp.concatenate(keys, axis=0)
-        outs = []
-        for half in range(2):
-            mine = low if half == 0 else jnp.logical_not(low)
-            qh = jnp.where(mine, q, 0.0).astype(bf16)
-            vh = jnp.where(mine, uv, 1.0).astype(bf16)
-            weights = jnp.exp2(dot(qh, kt) * scale).astype(bf16)
-            outs.append(dot(weights, vh))
-        top = jnp.where(low, outs[0], outs[1])
-        sums = pltpu.roll(jnp.where(low, outs[1], outs[0]), HEAD, 1)
-        put(unit, (top / sums).astype(bf16))
-        return carry
-
-    lax.fori_loop(*units, one, 0)
+            k = (k * lax.rsqrt(mean + eps_row)).astype(bf16)
+            kt = jnp.concatenate([k, blank] if half == 0 else [blank, k], axis=0)
+            weights.append(jnp.exp2(dot(q, kt) * scale).astype(bf16))
+        values = jnp.concatenate(
+            [
+                jnp.concatenate([jnp.where(low, uv, 0.0).astype(bf16), ones], axis=1),
+                jnp.concatenate([jnp.where(low, 0.0, uv).astype(bf16), other], axis=1),
+            ],
+            axis=0,
+        )
+        mixed = dot(jnp.concatenate(weights, axis=1), values)
+        put(unit, (mixed[:, :LANES] / mixed[:, LANES:]).astype(bf16))
 
 
 def attend_kernel(
     place_ref, near_ref, far_ref, x_ref, xt_ref, var_ref, varrow_ref, att_ref, *, units, slots, pairs, fold
 ):
     def put(unit, value):
-        att_ref[:, pl.ds(pl.multiple_of((unit - units[0]) * LANES, LANES), LANES)] = value
+        at = (unit - units[0]) * LANES
+        att_ref[:, at : at + LANES] = value
 
     attend_units(
         place_ref, near_ref, far_ref, x_ref, xt_ref, var_ref, varrow_ref, put, units, slots, pairs, fold
@@ -328,15 +326,8 @@
         sum_buf[...] = sum_buf[...] + folded(value)
 
     def sweep(step):
-        size = 2 * LANES
-
-        def body(i, carry):
-            step(pl.ds(pl.multiple_of(i * size, LANES), size))
-            return carry
-
-        lax.fori_loop(0, model // size, body, 0)
-        if model % size:
-            step(slice(model // size * size, model))
+        for at in range(0, model, 2 * LANES):
+            step(slice(at, min(at + 2 * LANES, model)))
 
     sweep(project)
     mean = jnp.sum(sum_buf[...], axis=1, keepdims=True) * (1.0 / model)
@@ -377,7 +368,7 @@
     place = place_ref[2]
     near, channels, wide = mine_ref.shape
     columns = wide // 2
-    offset = start_ref[0] - place * columns
+    offset = start_ref[...] - place * columns
     flat = near * channels
     first = guide * (near - 2)
     mine = mine_ref[...].reshape(flat, wide)
@@ -435,7 +426,7 @@
 
 
 def decode_kernel(
-    place_ref, step_ref, own_ref, odd_ref, two_ref, even_ref, lat_ref, count_ref, w_ref, den_ref, feat_ref, pad_buf,
+    place_ref, step_ref, own_ref, odd_ref, two_ref, even_ref, lat_ref, count_ref, w_ref, den_ref, feat_out, pad_buf, feat_ref, sems,
     *, width,
 ):
     guide = place_ref[1]
@@ -445,7 +436,7 @@
     near = half + 1
     flat = near * channels
     first = guide * (near - 2)
-    fraction = (jnp.full((1, columns), step_ref[0], jnp.int32).astype(f32) + 1.0) / STEPS
+    fraction = (jnp.broadcast_to(step_ref[...], (1, columns)).astype(f32) + 1.0) / STEPS
     sigma = 3.0 * fraction / (1.0 + 2.0 * fraction)
     odd = place % 2 == 1
     one = jnp.where(odd, even_ref[...], odd_ref[...]).astype(f32)
@@ -471,6 +462,7 @@
         pad_buf[b, near + 1] = zero
         for i in range(near):
             pad_buf[b, i + 1] = value[i * channels : (i + 1) * channels]
+    saves = []
     for r in range(half):
         at = guide + r
         den_ref[:, r, :] = pad_buf[1, at + 1]
@@ -479,6 +471,10 @@
         ).astype(bf16)
         summed = dot(stacked, w_ref[...], ((0,), (0,)))
         feat_ref[r] = (summed / (1.0 + jnp.exp(-summed))).astype(bf16)
+        saves.append(pltpu.make_async_copy(feat_ref.at[r], feat_out.at[r], sems.at[r]))
+        saves[-1].start()
+    for one in saves:
+        one.wait()
 
 
 def shift(x, by):
@@ -490,13 +486,9 @@
     return lax.ppermute(x, axis, [(0, 1), (1, 0)])
 
 
-def spread_major(pieces, fold):
+def send_xor(x, d):
     width = lax.axis_size("width")
-    got = []
-    for d in range(len(pieces), 0, -1):
-        route = [(i, (i // fold ^ d) * fold + i % fold) for i in range(width)]
-        got.append(lax.ppermute(pieces[d - 1], "width", route))
-    return got[::-1]
+    return lax.ppermute(x, "width", [(i, i ^ d) for i in range(width)])
 
 
 def gather_major(chunk, fold, direct):
@@ -506,7 +498,8 @@
         every = lax.all_gather(chunk, "width")
         every = every.reshape((depth, fold) + chunk.shape)
         return lax.dynamic_index_in_dim(every, lax.axis_index("width") % fold, 1, False)
-    return jnp.stack([chunk] + spread_major([chunk] * (depth - 1), fold))
+    got = [send_xor(chunk, d * fold) for d in range(depth - 1, 0, -1)]
+    return jnp.stack([chunk] + got[::-1])
 
 
 def swap_minor(stack):
@@ -531,8 +524,7 @@
         group = group * 0
     rows = w_qkv.shape[0]
     fold = 2
-    depth = width // fold
-    direct = depth <= 8 and depth & (depth - 1) == 0
+    direct = width <= 8 and width & (width - 1) == 0
     changes = jnp.swapaxes(cond_mod, 0, 1)
     key = place // fold if direct else 0
     scalars = jnp.stack([group, guide, place, key]).astype(jnp.int32)
@@ -547,11 +539,12 @@
             partial_kernel, width=width, slots=slots, local_pairs=local_pairs, features=features,
             fold=fold, direct=direct,
         ),
-        [((depth,) + slab, f32), ((depth,) + slab, bf16)] if direct else [((width,) + slab, bf16)],
+        [(slab, f32)] + [(slab, bf16)] * (width - 1) if direct else [((width,) + slab, bf16)],
         scratch=[
             pltpu.VMEM((3, rows, local_pairs * LANES), bf16),
             pltpu.VMEM(changes.shape, f32),
             pltpu.VMEM(w_patch.shape, bf16),
+            pltpu.VMEM((width,) + slab if direct else slab, f32),
             pltpu.SemaphoreType.DMA((5,)),
         ],
         anys=(1, 2, 3), smem=(0,), count=4, limit=8,
@@ -559,7 +552,7 @@
     near = height // 2 + 1
     tokens = height // 2 * columns
     if direct:
-        came = swap_minor(parts[1])
+        came = [send_xor(parts[d], d) for d in range(width - 1, 0, -1)]
     else:
         came = lax.all_to_all(parts[0], "width", 0, 0, tiled=True)
     x, xt, var, varrow, hidden = call(
@@ -572,17 +565,14 @@
             pltpu.VMEM((height * channels, 3 * columns), bf16),
             pltpu.VMEM((feats, tokens), f32),
             pltpu.VMEM(w_patch.shape, bf16),
-            pltpu.SemaphoreType.DMA((1,)),
+            pltpu.VMEM(latent.shape, f32),
+            pltpu.SemaphoreType.DMA((2,)),
         ],
-        anys=(5,), smem=(0, 1), count=6, flops=5e9,
-    )(scalars, starts, latent, right, further, in_hbm(w_patch))
+        anys=(2, 5), smem=(0,), count=6, flops=5e9,
+    )(scalars, starts[None], in_hbm(latent), right, further, in_hbm(w_patch))
     came, x = lax.optimization_barrier((came, x))
     if direct:
-        own, *sends = call(
-            first_sum_kernel, [(slab, f32)] + [(slab, bf16)] * (depth - 1), smem=(0,), count=3, limit=4
-        )(scalars, parts[0], came)
-        got = spread_major(sends, fold)
-        (chunk,) = call(last_sum_kernel, [(slab, bf16)], count=depth, limit=4)(own, *got)
+        (chunk,) = call(direct_sum_kernel, [(slab, bf16)], count=width, limit=4)(parts[0], *came)
     else:
         (chunk,) = call(
             functools.partial(sum_kernel, width=width), [(slab, bf16)], count=1, limit=4
@@ -628,8 +618,8 @@
             ((flat, 2 * columns), f32), ((flat, 2 * columns), bf16),
             ((flat, 2 * columns), bf16), ((flat, 2 * columns), bf16),
         ],
-        smem=(0, 1), count=5, limit=8,
-    )(scalars, starts, mine_v, theirs, latent)
+        smem=(0,), count=5, limit=8,
+    )(scalars, starts[None], mine_v, theirs, latent)
     ups = [(i, (i + 1) % width) for i in range(width)]
     turns = [[pair for pair in ups if pair[0] % 2 == side] for side in range(2)]
     turns = [pairs + [(b, a) for a, b in pairs] for pairs in turns]
@@ -639,9 +629,13 @@
     return call(
         functools.partial(decode_kernel, width=width),
         [((channels, height // 2, columns), f32), ((height // 2, columns, w_dec.shape[1]), bf16)],
-        scratch=[pltpu.VMEM((3, near + 2, channels, columns), f32)],
-        smem=(0, 1), count=9, limit=8,
-    )(scalars, step_index, own, odd, two, even, latent, counts[None], w_dec)
+        scratch=[
+            pltpu.VMEM((3, near + 2, channels, columns), f32),
+            pltpu.VMEM((height // 2, columns, w_dec.shape[1]), bf16),
+            pltpu.SemaphoreType.DMA((height // 2,)),
+        ],
+        smem=(0,), count=9, limit=8, hbm_outs=(1,),
+    )(scalars, step_index[None], own, odd, two, even, latent, counts[None], w_dec)
 
 
 def solution(mesh):

time: 72.6 us -> 68.4 us (0.942)
  starting transfers between devices: 22.5 us -> 28.6 us
  Pallas kernels: 33 us -> 27.6 us
  waiting for transfers between devices: 13.7 us -> 9.52 us
  local copies, waits for them, and re-layouts: 0.88 us -> 0.04 us
    ppermute x6 -> x10, starting transfers between devices: 8.9 us -> 13.6 us  [send_xor(): return lax.ppermute(x, 'width', [(i, i ^ d) for i in range(width)])]
    ppermute x6 -> x10, waiting for transfers between devices: 8.15 us -> 4.52 us  [send_xor(): return lax.ppermute(x, 'width', [(i, i ^ d) for i in range(width)])]
    pallas_call x1, Pallas kernels: 14.3 us -> 11 us  [shards(): call(functools.partial(second_kernel, channels=channels, height=height, c...]
    ppermute x1, waiting for transfers between devices: 3.79 us -> 1.6 us  [shards(): odd = lax.ppermute(odd, 'width', turns[1])]
    ppermute x1, starting transfers between devices: 0.01 us -> 2.17 us  [shards(): even = lax.ppermute(even, 'width', turns[0])]
    pallas_call x1, Pallas kernels: 3.7 us -> 2.67 us  [shards(): call(functools.partial(partial_kernel, width=width, slots=slots, local_pa...]
    unnamed x16 -> x14, local copies, waits for them, and re-layouts: 0.88 us -> 0.04 us
    ppermute x2 -> x1, starting transfers between devices: 1.69 us -> 0.87 us  [swap_minor(): return lax.ppermute(stack, 'width', [(i, i ^ 1) for i in range(width)])]
  transfers between devices with their start and end apart: 16 -> 19, of which waited for: 7 -> 8; matrix products, arithmetic and copies ran while one was open for 0% -> 0% of each run, Pallas kernels for 21% -> 19%
where the time goes in v6:
time: 68.4 us; the launch traced here: 68.2 us
  starting transfers between devices  28.6 us (42%)
  Pallas kernels  27.6 us (40%)
  waiting for transfers between devices  9.52 us (14%)
  between operations  2.29 us (3%)
    ppermute x10, starting transfers between devices, send_xor(): return lax.ppermute(x, 'width', [(i, i ^ d) for i in range(width)])  13.6 us
    pallas_call x1, Pallas kernels, shards(): call(functools.partial(second_kernel, channels=channels, height=height, c...  11 us
    ppermute x2, starting transfers between devices, shift(): lax.ppermute(x, 'width', [(i, (i + by) % peers) for i in range(peers)])  6.54 us
    pallas_call x1, Pallas kernels, shards(): call(window_kernel, [((tokens, LANES), bf16), ((ROWS, tokens), bf16), ((t...  4.84 us
    ppermute x10, waiting for transfers between devices, send_xor(): return lax.ppermute(x, 'width', [(i, i ^ d) for i in range(width)])  4.52 us
    pallas_call x1, Pallas kernels, shards(): call(functools.partial(attend_kernel, units=(whole, local_pairs), **sizes...  3.17 us
    ppermute x3, starting transfers between devices, swap(): return lax.ppermute(x, axis, [(0, 1), (1, 0)])  3.06 us
    pallas_call x1, Pallas kernels, shards(): call(functools.partial(partial_kernel, width=width, slots=slots, local_pa...  2.67 us
  transfers between devices with their start and end apart: 19, of which 8 were waited for; matrix products, arithmetic and copies ran while one was open for 0% of the time, Pallas kernels for 19%

profile of v6, /device:TPU:0, one launch (start us, length us, event | category | flops | bytes accessed | tf_op | source)
XLA Modules:
  0.0 68.2 jit_solution(17592320182651640039)
XLA Ops:
  0.6 6.1 %collective-permute-start.7 = (f32[16,8,128]{2,1,0:T(8,128)}, f32[16,8,128]{2,1,0:T(8,128)S(1)}, u32[]{:S(2)}, u32[]{:S(2)}) collective-permute-start(f32[16,8,128]{2,1,0:T(8,128)} %lat_ref.3), channel_id=1, source_target_pairs={{0,14},{2,0},{4,2},{6,4},{8,6},{10,8},{12,10},{14,12},{1,15},{3,1}... | collective-permute-start | bytes 196616 | tf_op jit(solution)/shard_map/ppermute | solution.py:482
  6.7 0.4 collective-permute-start.8
  7.2 0.1 pad_add_fusion.place_ref
  7.2 2.7 %shard_map.113 = (f32[72,256]{1,0:T(8,128)S(1)}, bf16[72,256]{1,0:T(8,128)(2,1)S(1)}, bf16[72,256]{1,0:T(8,128)(2,1)S(1)}, bf16[72,256]{1,0:T(8,128)(2,1)S(1)}, ...) custom-call(s32[4]{0:T(128)S(1)} %pad_add_fusion.place_ref, ...), custom_call_target="tpu_custom_call" | custom-call | bytes 1048576 | tf_op jit(solution)/shard_map/pallas_call | solution.py:537
  9.9 0.6 collective-permute-start
  10.5 3.4 %collective-permute-start.1 = (bf16[72,256]{1,0:T(8,128)(2,1)S(1)}, bf16[72,256]{1,0:T(8,128)(2,1)S(1)}, u32[]{:S(2)}, u32[]{:S(2)}) collective-permute-start(bf16[72,256]{1,0:T(8,128)(2,1)S(1)} %get-tuple-element.33), channel_id=1, source_target_pairs={{0,12},{2,14},{4,8},{6,10},{8,4},{10,6},{12,0},{14,2},{1,13},{3,15... | collective-permute-start | bytes 110600 | tf_op jit(solution)/shard_map/ppermute | solution.py:491
  13.9 0.1 collective-permute-start.2
  14.6 2.2 %collective-permute-done.refs_1_ = bf16[72,256]{1,0:T(8,128)(2,1)S(1)} collective-permute-done((bf16[72,256]{1,0:T(8,128)(2,1)S(1)}, bf16[72,256]{1,0:T(8,128)(2,1)S(1)}, u32[]{:S(2)}, u32[]{:S(2)}) %collective-permute-start) | collective-permute-done | bytes 36896 | tf_op jit(solution)/shard_map/ppermute | solution.py:491
  16.7 1.6 %collective-permute-start.3 = (bf16[72,256]{1,0:T(8,128)(2,1)S(1)}, bf16[72,256]{1,0:T(8,128)(2,1)S(1)}, u32[]{:S(2)}, u32[]{:S(2)}) collective-permute-start(bf16[72,256]{1,0:T(8,128)(2,1)S(1)} %get-tuple-element.35), channel_id=1, source_target_pairs={{0,8},{2,10},{4,12},{6,14},{8,0},{10,2},{12,4},{14,6},{1,9},{3,11}... | collective-permute-start | bytes 110600 | tf_op jit(solution)/shard_map/ppermute | solution.py:491
  18.4 0.0 collective-permute-done.1.refs_2_
  18.4 0.5 collective-permute-start.4
  18.9 0.0 collective-permute-done.7.right_ref
  18.9 1.6 %collective-permute-start.5 = (bf16[72,256]{1,0:T(8,128)(2,1)S(1)}, bf16[72,256]{1,0:T(8,128)(2,1)S(1)}, u32[]{:S(2)}, u32[]{:S(2)}) collective-permute-start(bf16[72,256]{1,0:T(8,128)(2,1)S(1)} %get-tuple-element.37), channel_id=1, source_target_pairs={{0,4},{2,6},{4,0},{6,2},{8,12},{10,14},{12,8},{14,10},{1,5},{3,7},... | collective-permute-start | bytes 110600 | tf_op jit(solution)/shard_map/ppermute | solution.py:491
  20.5 0.0 collective-permute-done.8.further_ref
  20.5 1.4 %collective-permute-start.6 = (bf16[72,256]{1,0:T(8,128)(2,1)S(1)}, bf16[72,256]{1,0:T(8,128)(2,1)S(1)}, u32[]{:S(2)}, u32[]{:S(2)}) collective-permute-start(bf16[72,256]{1,0:T(8,128)(2,1)S(1)} %get-tuple-element.38), channel_id=1, source_target_pairs={{0,2},{2,0},{4,6},{6,4},{8,10},{10,8},{12,14},{14,12},{1,3},{3,1},... | collective-permute-start | bytes 110600 | tf_op jit(solution)/shard_map/ppermute | solution.py:491
  21.9 4.8 %shard_map.114 = (bf16[512,128]{1,0:T(8,128)(2,1)S(1)}, bf16[72,512]{1,0:T(8,128)(2,1)S(1)}, f32[512,128]{1,0:T(8,128)S(1)}, f32[8,512]{1,0:T(8,128)S(1)}, f32[512,2432]{1,0:T(8,128)S(1)}) custom-call(s32[4]{0:T(128)S(1)} %pad_add_fusion.place_ref, s32[1,1]{1,0:T(1,128)} %bitcast.13.start_ref, f32[16,8,128]{2,1,0:T(8,128)} %lat_ref.3, ...), custom_call_target="tpu_custom_call" | custom-call | flops 5000000000 | bytes 1048576 | tf_op jit(solution)/shard_map/pallas_call | solution.py:558
  26.7 0.0 collective-permute-done.3.refs_4_
  26.7 0.0 collective-permute-done.4.refs_5_
  26.8 0.0 collective-permute-done.6.refs_7_
  26.8 1.3 %collective-permute-start.11 = (bf16[72,256]{1,0:T(8,128)(2,1)S(1)}, bf16[72,256]{1,0:T(8,128)(2,1)S(1)}, u32[]{:S(2)}, u32[]{:S(2)}) collective-permute-start(bf16[72,256]{1,0:T(8,128)(2,1)S(1)} %shard_map.115), channel_id=1, source_target_pairs={{0,12},{2,14},{4,8},{6,10},{8,4},{10,6},{12,0},{14,2},{1,13},{3,15... | collective-permute-start | bytes 110600 | tf_op jit(solution)/shard_map/ppermute | solution.py:491
  28.2 0.6 collective-permute-start.9
  28.8 2.5 %collective-permute-start.10 = (bf16[72,256]{1,0:T(8,128)(2,1)S(1)}, bf16[72,256]{1,0:T(8,128)(2,1)S(1)}, u32[]{:S(2)}, u32[]{:S(2)}) collective-permute-start(bf16[72,256]{1,0:T(8,128)(2,1)S(1)} %shard_map.115), channel_id=1, source_target_pairs={{0,8},{2,10},{4,12},{6,14},{8,0},{10,2},{12,4},{14,6},{1,9},{3,11}... | collective-permute-start | bytes 110600 | tf_op jit(solution)/shard_map/ppermute | solution.py:491
  31.3 1.4 %collective-permute-done.11 = bf16[72,256]{1,0:T(8,128)(2,1)S(1)} collective-permute-done((bf16[72,256]{1,0:T(8,128)(2,1)S(1)}, bf16[72,256]{1,0:T(8,128)(2,1)S(1)}, u32[]{:S(2)}, u32[]{:S(2)}) %collective-permute-start.11) | collective-permute-done | bytes 36896 | tf_op jit(solution)/shard_map/ppermute | solution.py:491
  32.6 0.0 collective-permute-done.9
  32.6 1.0 %collective-permute-done.10 = bf16[72,256]{1,0:T(8,128)(2,1)S(1)} collective-permute-done((bf16[72,256]{1,0:T(8,128)(2,1)S(1)}, bf16[72,256]{1,0:T(8,128)(2,1)S(1)}, u32[]{:S(2)}, u32[]{:S(2)}) %collective-permute-start.10) | collective-permute-done | bytes 36896 | tf_op jit(solution)/shard_map/ppermute | solution.py:491
  33.6 0.9 %collective-permute-start.13 = (bf16[4,72,256]{2,1,0:T(8,128)(2,1)S(1)}, bf16[4,72,256]{2,1,0:T(8,128)(2,1)S(1)}, u32[]{:S(2)}, u32[]{:S(2)}) collective-permute-start(bf16[4,72,256]{2,1,0:T(8,128)(2,1)S(1)} %pad_maximum_fusion.near_ref), channel_id=1, source_target_pairs={{0,2},{2,0},{4,6},{6,4},{8,10},{10,8},{12,14},{14,12},{1,3},{3,1},... | collective-permute-start | bytes 442376 | tf_op jit(solution)/shard_map/ppermute | solution.py:507
  34.5 1.5 %collective-permute-start.12 = (bf16[4,72,256]{2,1,0:T(8,128)(2,1)S(1)}, bf16[4,72,256]{2,1,0:T(8,128)(2,1)S(1)}, u32[]{:S(2)}, u32[]{:S(2)}) collective-permute-start(bf16[4,72,256]{2,1,0:T(8,128)(2,1)S(1)} %pad_maximum_fusion.near_ref), channel_id=1, source_target_pairs={{0,16},{16,0},{1,17},{17,1},{2,18},{18,2},{3,19},{19,3},{4,20},{20... | collective-permute-start | bytes 442376 | tf_op jit(solution)/shard_map/ppermute | solution.py:486
  36.0 2.4 %shard_map.116.refs_0_ = bf16[512,256]{1,0:T(8,128)(2,1)S(1)} custom-call(s32[4]{0:T(128)S(1)} %pad_add_fusion.place_ref, bf16[4,72,256]{2,1,0:T(8,128)(2,1)S(1)} %pad_maximum_fusion.near_ref, bf16[512,128]{1,0:T(8,128)(2,1)S(1)} %get-tuple-element.47.x_ref, bf16[72,512]{1,0:T(8,128)(2,1)S(1)} %get-tuple-element.48.xt_ref, ...), custom_call_target="tpu_custom_call" | custom-call | flops 2000000000 | bytes 1048576 | tf_op jit(solution)/shard_map/pallas_call | solution.py:585
  38.4 0.0 copy-start.2
  38.4 0.0 slice-start.1
  38.4 0.0 copy-start.4
  38.5 0.4 collective-permute-done.13.far_ref
  38.8 1.5 %collective-permute-start.14 = (bf16[4,72,256]{2,1,0:T(8,128)(2,1)S(1)}, bf16[4,72,256]{2,1,0:T(8,128)(2,1)S(1)}, u32[]{:S(2)}, u32[]{:S(2)}) collective-permute-start(bf16[4,72,256]{2,1,0:T(8,128)(2,1)S(1)} %collective-permute-done.13.far_ref), channel_id=1, source_target_pairs={{0,16},{16,0},{1,17},{17,1},{2,18},{18,2},{3,19},{19,3},{4,20},{20... | collective-permute-start | bytes 442376 | tf_op jit(solution)/shard_map/ppermute | solution.py:486
  40.3 3.2 %shard_map.117.refs_1_ = bf16[512,384]{1,0:T(8,128)(2,1)S(1)} custom-call(s32[4]{0:T(128)S(1)} %pad_add_fusion.place_ref, bf16[4,72,256]{2,1,0:T(8,128)(2,1)S(1)} %pad_maximum_fusion.near_ref, bf16[4,72,256]{2,1,0:T(8,128)(2,1)S(1)} %collective-permute-done.13.far_ref, bf16[512,128]{1,0:T(8,128)(2,1)S(1)} %get-tuple-element.47.x_ref, ...), custom_call_target="tpu_custom_call" | custom-call | flops 3000000000 | bytes 1048576 | tf_op jit(solution)/shard_map/pallas_call | solution.py:595
  43.5 0.5 collective-permute-done.14.far_ref
  44.0 0.0 copy-start
  44.0 0.0 copy-start.1
  44.0 0.0 copy-start.3
  44.1 11.0 %shard_map.118 = (f32[5,16,256]{2,1,0:T(8,128)S(1)}, bf16[5,16,256]{2,1,0:T(8,128)(2,1)S(1)}) custom-call(s32[4]{0:T(128)S(1)} %pad_add_fusion.place_ref, bf16[4,72,256]{2,1,0:T(8,128)(2,1)S(1)} %collective-permute-done.12.near_ref, bf16[4,72,256]{2,1,0:T(8,128)(2,1)S(1)} %collective-permute-done.14.far_ref, bf16[512,128]{1,0:T(8,128)(2,1)S(1)} %get-tuple-element.47.x_ref, ...), custom_call_target="tpu_custom_call" | custom-call | flops 12000000000 | bytes 1048576 | tf_op jit(solution)/shard_map/pallas_call | solution.py:600
  55.0 0.1 collective-permute-start.15
  55.1 1.2 %collective-permute-done.15.theirs_ref = bf16[5,16,256]{2,1,0:T(8,128)(2,1)S(1)} collective-permute-done((bf16[5,16,256]{2,1,0:T(8,128)(2,1)S(1)}, bf16[5,16,256]{2,1,0:T(8,128)(2,1)S(1)}, u32[]{:S(2)}, u32[]{:S(2)}) %collective-permute-start.15) | collective-permute-done | bytes 40992 | tf_op jit(solution)/shard_map/ppermute | solution.py:486
  56.3 0.9 %shard_map.119 = (f32[80,256]{1,0:T(8,128)S(1)}, bf16[80,256]{1,0:T(8,128)(2,1)S(1)}, bf16[80,256]{1,0:T(8,128)(2,1)S(1)}, bf16[80,256]{1,0:T(8,128)(2,1)S(1)}) custom-call(s32[4]{0:T(128)S(1)} %pad_add_fusion.place_ref, s32[1,1]{1,0:T(1,128)} %bitcast.14.start_ref, f32[5,16,256]{2,1,0:T(8,128)S(1)} %get-tuple-element.54.mine_ref, ...), custom_call_target="tpu_custom_call" | custom-call | bytes 1048576 | tf_op jit(solution)/shard_map/pallas_call | solution.py:615
  57.3 2.4 %collective-permute-start.16 = (bf16[80,256]{1,0:T(8,128)(2,1)S(1)}, bf16[80,256]{1,0:T(8,128)(2,1)S(1)}, u32[]{:S(2)}, u32[]{:S(2)}) collective-permute-start(bf16[80,256]{1,0:T(8,128)(2,1)S(1)} %get-tuple-element.57), channel_id=1, source_target_pairs={{2,4},{6,8},{10,12},{14,0},{4,2},{8,6},{12,10},{0,14},{3,5},{7,9},... | collective-permute-start | bytes 122888 | tf_op jit(solution)/shard_map/ppermute | solution.py:626
  59.7 0.1 collective-permute-start.17
  59.7 2.2 %collective-permute-start.18 = (bf16[80,256]{1,0:T(8,128)(2,1)S(1)}, bf16[80,256]{1,0:T(8,128)(2,1)S(1)}, u32[]{:S(2)}, u32[]{:S(2)}) collective-permute-start(bf16[80,256]{1,0:T(8,128)(2,1)S(1)} %get-tuple-element.59), channel_id=1, source_target_pairs={{0,2},{4,6},{8,10},{12,14},{2,0},{6,4},{10,8},{14,12},{1,3},{5,7},... | collective-permute-start | bytes 122888 | tf_op jit(solution)/shard_map/ppermute | solution.py:628
  62.5 1.6 %collective-permute-done.16.odd_ref = bf16[80,256]{1,0:T(8,128)(2,1)S(1)} collective-permute-done((bf16[80,256]{1,0:T(8,128)(2,1)S(1)}, bf16[80,256]{1,0:T(8,128)(2,1)S(1)}, u32[]{:S(2)}, u32[]{:S(2)}) %collective-permute-start.16) | collective-permute-done | bytes 40992 | tf_op jit(solution)/shard_map/ppermute | solution.py:626
  64.1 1.3 %collective-permute-done.17.two_ref = bf16[80,256]{1,0:T(8,128)(2,1)S(1)} collective-permute-done((bf16[80,256]{1,0:T(8,128)(2,1)S(1)}, bf16[80,256]{1,0:T(8,128)(2,1)S(1)}, u32[]{:S(2)}, u32[]{:S(2)}) %collective-permute-start.17) | collective-permute-done | bytes 40992 | tf_op jit(solution)/shard_map/ppermute | solution.py:627
  65.5 2.6 %shard_map.120 = (f32[16,4,128]{2,1,0:T(4,128)}, bf16[4,128,512]{2,1,0:T(8,128)(2,1)}) custom-call(s32[4]{0:T(128)S(1)} %pad_add_fusion.place_ref, s32[1,1]{1,0:T(1,128)} %bitcast.15.step_ref, f32[80,256]{1,0:T(8,128)S(1)} %get-tuple-element.56.own_ref, bf16[80,256]{1,0:T(8,128)(2,1)S(1)} %collective-permute-done.16.odd_ref, ...), custom_call_target="tpu_custom_call" | custom-call | bytes 1048576 | tf_op jit(solution)/shard_map/pallas_call | solution.py:629
  (15 shorter events, 0.1 us)
Async XLA Ops:
  0.6 18.2 %collective-permute-start.7 = (f32[16,8,128]{2,1,0:T(8,128)}, f32[16,8,128]{2,1,0:T(8,128)S(1)}, u32[]{:S(2)}, u32[]{:S(2)}) collective-permute-start(f32[16,8,128]{2,1,0:T(8,128)} %lat_ref.3), channel_id=1, source_target_pairs={{0,14},{2,0},{4,2},{6,4},{8,6},{10,8},{12,10},{14,12},{1,15},{3,1}... | collective-permute-start | bytes 196616 | tf_op jit(solution)/shard_map/ppermute | solution.py:482
  6.7 13.8 %collective-permute-start.8 = (f32[16,8,128]{2,1,0:T(8,128)}, f32[16,8,128]{2,1,0:T(8,128)S(1)}, u32[]{:S(2)}, u32[]{:S(2)}) collective-permute-start(f32[16,8,128]{2,1,0:T(8,128)} %lat_ref.3), channel_id=1, source_target_pairs={{0,12},{2,14},{4,0},{6,2},{8,4},{10,6},{12,8},{14,10},{1,13},{3,15... | collective-permute-start | bytes 196616 | tf_op jit(solution)/shard_map/ppermute | solution.py:482
  9.9 6.8 %collective-permute-start = (bf16[72,256]{1,0:T(8,128)(2,1)S(1)}, bf16[72,256]{1,0:T(8,128)(2,1)S(1)}, u32[]{:S(2)}, u32[]{:S(2)}) collective-permute-start(bf16[72,256]{1,0:T(8,128)(2,1)S(1)} %get-tuple-element.32), channel_id=1, source_target_pairs={{0,14},{2,12},{4,10},{6,8},{8,6},{10,4},{12,2},{14,0},{1,15},{3,13... | collective-permute-start | bytes 110600 | tf_op jit(solution)/shard_map/ppermute | solution.py:491
  10.5 7.9 %collective-permute-start.1 = (bf16[72,256]{1,0:T(8,128)(2,1)S(1)}, bf16[72,256]{1,0:T(8,128)(2,1)S(1)}, u32[]{:S(2)}, u32[]{:S(2)}) collective-permute-start(bf16[72,256]{1,0:T(8,128)(2,1)S(1)} %get-tuple-element.33), channel_id=1, source_target_pairs={{0,12},{2,14},{4,8},{6,10},{8,4},{10,6},{12,0},{14,2},{1,13},{3,15... | collective-permute-start | bytes 110600 | tf_op jit(solution)/shard_map/ppermute | solution.py:491
  13.9 12.8 %collective-permute-start.2 = (bf16[72,256]{1,0:T(8,128)(2,1)S(1)}, bf16[72,256]{1,0:T(8,128)(2,1)S(1)}, u32[]{:S(2)}, u32[]{:S(2)}) collective-permute-start(bf16[72,256]{1,0:T(8,128)(2,1)S(1)} %get-tuple-element.34), channel_id=1, source_target_pairs={{0,10},{2,8},{4,14},{6,12},{8,2},{10,0},{12,6},{14,4},{1,11},{3,9}... | collective-permute-start | bytes 110600 | tf_op jit(solution)/shard_map/ppermute | solution.py:491
  16.7 10.0 %collective-permute-start.3 = (bf16[72,256]{1,0:T(8,128)(2,1)S(1)}, bf16[72,256]{1,0:T(8,128)(2,1)S(1)}, u32[]{:S(2)}, u32[]{:S(2)}) collective-permute-start(bf16[72,256]{1,0:T(8,128)(2,1)S(1)} %get-tuple-element.35), channel_id=1, source_target_pairs={{0,8},{2,10},{4,12},{6,14},{8,0},{10,2},{12,4},{14,6},{1,9},{3,11}... | collective-permute-start | bytes 110600 | tf_op jit(solution)/shard_map/ppermute | solution.py:491
  18.4 8.4 %collective-permute-start.4 = (bf16[72,256]{1,0:T(8,128)(2,1)S(1)}, bf16[72,256]{1,0:T(8,128)(2,1)S(1)}, u32[]{:S(2)}, u32[]{:S(2)}) collective-permute-start(bf16[72,256]{1,0:T(8,128)(2,1)S(1)} %get-tuple-element.36), channel_id=1, source_target_pairs={{0,6},{2,4},{4,2},{6,0},{8,14},{10,12},{12,10},{14,8},{1,7},{3,5},... | collective-permute-start | bytes 110600 | tf_op jit(solution)/shard_map/ppermute | solution.py:491
  18.9 7.9 %collective-permute-start.5 = (bf16[72,256]{1,0:T(8,128)(2,1)S(1)}, bf16[72,256]{1,0:T(8,128)(2,1)S(1)}, u32[]{:S(2)}, u32[]{:S(2)}) collective-permute-start(bf16[72,256]{1,0:T(8,128)(2,1)S(1)} %get-tuple-element.37), channel_id=1, source_target_pairs={{0,4},{2,6},{4,0},{6,2},{8,12},{10,14},{12,8},{14,10},{1,5},{3,7},... | collective-permute-start | bytes 110600 | tf_op jit(solution)/shard_map/ppermute | solution.py:491
  20.5 6.3 %collective-permute-start.6 = (bf16[72,256]{1,0:T(8,128)(2,1)S(1)}, bf16[72,256]{1,0:T(8,128)(2,1)S(1)}, u32[]{:S(2)}, u32[]{:S(2)}) collective-permute-start(bf16[72,256]{1,0:T(8,128)(2,1)S(1)} %get-tuple-element.38), channel_id=1, source_target_pairs={{0,2},{2,0},{4,6},{6,4},{8,10},{10,8},{12,14},{14,12},{1,3},{3,1},... | collective-permute-start | bytes 110600 | tf_op jit(solution)/shard_map/ppermute | solution.py:491
  26.8 5.8 %collective-permute-start.11 = (bf16[72,256]{1,0:T(8,128)(2,1)S(1)}, bf16[72,256]{1,0:T(8,128)(2,1)S(1)}, u32[]{:S(2)}, u32[]{:S(2)}) collective-permute-start(bf16[72,256]{1,0:T(8,128)(2,1)S(1)} %shard_map.115), channel_id=1, source_target_pairs={{0,12},{2,14},{4,8},{6,10},{8,4},{10,6},{12,0},{14,2},{1,13},{3,15... | collective-permute-start | bytes 110600 | tf_op jit(solution)/shard_map/ppermute | solution.py:491
  28.2 4.5 %collective-permute-start.9 = (bf16[72,256]{1,0:T(8,128)(2,1)S(1)}, bf16[72,256]{1,0:T(8,128)(2,1)S(1)}, u32[]{:S(2)}, u32[]{:S(2)}) collective-permute-start(bf16[72,256]{1,0:T(8,128)(2,1)S(1)} %shard_map.115), channel_id=1, source_target_pairs={{0,4},{2,6},{4,0},{6,2},{8,12},{10,14},{12,8},{14,10},{1,5},{3,7},... | collective-permute-start | bytes 110600 | tf_op jit(solution)/shard_map/ppermute | solution.py:491
  28.8 4.9 %collective-permute-start.10 = (bf16[72,256]{1,0:T(8,128)(2,1)S(1)}, bf16[72,256]{1,0:T(8,128)(2,1)S(1)}, u32[]{:S(2)}, u32[]{:S(2)}) collective-permute-start(bf16[72,256]{1,0:T(8,128)(2,1)S(1)} %shard_map.115), channel_id=1, source_target_pairs={{0,8},{2,10},{4,12},{6,14},{8,0},{10,2},{12,4},{14,6},{1,9},{3,11}... | collective-permute-start | bytes 110600 | tf_op jit(solution)/shard_map/ppermute | solution.py:491
  33.6 5.2 %collective-permute-start.13 = (bf16[4,72,256]{2,1,0:T(8,128)(2,1)S(1)}, bf16[4,72,256]{2,1,0:T(8,128)(2,1)S(1)}, u32[]{:S(2)}, u32[]{:S(2)}) collective-permute-start(bf16[4,72,256]{2,1,0:T(8,128)(2,1)S(1)} %pad_maximum_fusion.near_ref), channel_id=1, source_target_pairs={{0,2},{2,0},{4,6},{6,4},{8,10},{10,8},{12,14},{14,12},{1,3},{3,1},... | collective-permute-start | bytes 442376 | tf_op jit(solution)/shard_map/ppermute | solution.py:507
  34.5 9.0 %collective-permute-start.12 = (bf16[4,72,256]{2,1,0:T(8,128)(2,1)S(1)}, bf16[4,72,256]{2,1,0:T(8,128)(2,1)S(1)}, u32[]{:S(2)}, u32[]{:S(2)}) collective-permute-start(bf16[4,72,256]{2,1,0:T(8,128)(2,1)S(1)} %pad_maximum_fusion.near_ref), channel_id=1, source_target_pairs={{0,16},{16,0},{1,17},{17,1},{2,18},{18,2},{3,19},{19,3},{4,20},{20... | collective-permute-start | bytes 442376 | tf_op jit(solution)/shard_map/ppermute | solution.py:486
  36.0 8.0 %slice-start = ((s8[6225920]{0:T(1024)(128)(4,1)}), s8[4194304]{0:T(1024)(128)(4,1)S(1)}, s32[]{:S(2)}) async-start(s8[6225920]{0:T(1024)(128)(4,1)} %bitcast.20), calls=%async_computation | async-start | bytes 8388608
  38.4 5.6 %copy-start.2 = (f32[1,3,2432]{2,0,1:T(1,128)S(1)}, f32[1,3,2432]{2,0,1:T(1,128)}, u32[]{:S(2)}) copy-start(f32[1,3,2432]{2,0,1:T(1,128)} %param.14) | copy-start | bytes 87556
  38.4 5.6 %slice-start.1 = ((s8[6225920]{0:T(1024)(128)(4,1)}), s8[2031616]{0:T(1024)(128)(4,1)S(1)}, s32[]{:S(2)}) async-start(s8[6225920]{0:T(1024)(128)(4,1)} %bitcast.20), calls=%async_computation.1 | async-start | bytes 4063232
  38.4 5.6 %copy-start.4 = (bf16[2432,64]{0,1:T(8,128)(2,1)S(1)}, bf16[2432,64]{0,1:T(8,128)(2,1)}, u32[]{:S(2)}) copy-start(bf16[2432,64]{0,1:T(8,128)(2,1)} %param.18) | copy-start | bytes 933892
  38.8 5.1 %collective-permute-start.14 = (bf16[4,72,256]{2,1,0:T(8,128)(2,1)S(1)}, bf16[4,72,256]{2,1,0:T(8,128)(2,1)S(1)}, u32[]{:S(2)}, u32[]{:S(2)}) collective-permute-start(bf16[4,72,256]{2,1,0:T(8,128)(2,1)S(1)} %collective-permute-done.13.far_ref), channel_id=1, source_target_pairs={{0,16},{16,0},{1,17},{17,1},{2,18},{18,2},{3,19},{19,3},{4,20},{20... | collective-permute-start | bytes 442376 | tf_op jit(solution)/shard_map/ppermute | solution.py:486
  44.0 12.3 %copy-start = (f32[16,8,128]{2,1,0:T(8,128)S(1)}, f32[16,8,128]{2,1,0:T(8,128)}, u32[]{:S(2)}) copy-start(f32[16,8,128]{2,1,0:T(8,128)} %lat_ref.3) | copy-start | bytes 196612
  44.0 21.4 %copy-start.1 = (bf16[144,512]{1,0:T(8,128)(2,1)S(1)}, bf16[144,512]{1,0:T(8,128)(2,1)}, u32[]{:S(2)}) copy-start(bf16[144,512]{1,0:T(8,128)(2,1)} %w_ref.3) | copy-start | bytes 442372
  44.0 21.4 %copy-start.3 = (s32[128]{0:T(128)S(1)}, s32[128]{0:T(128)}, u32[]{:S(2)}) copy-start(s32[128]{0:T(128)} %param.12) | copy-start | bytes 1540
  55.0 1.3 %collective-permute-start.15 = (bf16[5,16,256]{2,1,0:T(8,128)(2,1)S(1)}, bf16[5,16,256]{2,1,0:T(8,128)(2,1)S(1)}, u32[]{:S(2)}, u32[]{:S(2)}) collective-permute-start(bf16[5,16,256]{2,1,0:T(8,128)(2,1)S(1)} %get-tuple-element.55), channel_id=1, source_target_pairs={{0,1},{1,0},{2,3},{3,2},{4,5},{5,4},{6,7},{7,6},{8,9},{9,8},{10,11... | collective-permute-start | bytes 122888 | tf_op jit(solution)/shard_map/ppermute | solution.py:486
  57.3 6.9 %collective-permute-start.16 = (bf16[80,256]{1,0:T(8,128)(2,1)S(1)}, bf16[80,256]{1,0:T(8,128)(2,1)S(1)}, u32[]{:S(2)}, u32[]{:S(2)}) collective-permute-start(bf16[80,256]{1,0:T(8,128)(2,1)S(1)} %get-tuple-element.57), channel_id=1, source_target_pairs={{2,4},{6,8},{10,12},{14,0},{4,2},{8,6},{12,10},{0,14},{3,5},{7,9},... | collective-permute-start | bytes 122888 | tf_op jit(solution)/shard_map/ppermute | solution.py:626
  59.7 5.8 %collective-permute-start.17 = (bf16[80,256]{1,0:T(8,128)(2,1)S(1)}, bf16[80,256]{1,0:T(8,128)(2,1)S(1)}, u32[]{:S(2)}, u32[]{:S(2)}) collective-permute-start(bf16[80,256]{1,0:T(8,128)(2,1)S(1)} %get-tuple-element.58), channel_id=1, source_target_pairs={{0,4},{2,6},{4,8},{6,10},{8,12},{10,14},{12,0},{14,2},{1,5},{3,7},... | collective-permute-start | bytes 122888 | tf_op jit(solution)/shard_map/ppermute | solution.py:627
  59.7 5.7 %collective-permute-start.18 = (bf16[80,256]{1,0:T(8,128)(2,1)S(1)}, bf16[80,256]{1,0:T(8,128)(2,1)S(1)}, u32[]{:S(2)}, u32[]{:S(2)}) collective-permute-start(bf16[80,256]{1,0:T(8,128)(2,1)S(1)} %get-tuple-element.59), channel_id=1, source_target_pairs={{0,2},{4,6},{8,10},{12,14},{2,0},{6,4},{10,8},{14,12},{1,3},{5,7},... | collective-permute-start | bytes 122888 | tf_op jit(solution)/shard_map/ppermute | solution.py:628

commit v7 on v6

--- a/solution.py
+++ b/solution.py
@@ -28,7 +28,7 @@
     return lax.dot_general(a, b, (dims, ((), ())), preferred_element_type=f32)
 
 
-def call(body, outs, scratch=(), anys=(), smem=(), count=0, limit=16, flops=0, hbm_outs=()):
+def call(body, outs, scratch=(), anys=(), smem=(), count=0, limit=16, flops=0):
     def spec(i):
         if i in anys:
             return pl.BlockSpec(memory_space=pltpu.HBM)
@@ -40,9 +40,7 @@
         body,
         out_shape=tuple(jax.ShapeDtypeStruct(s, t) for s, t in outs),
         in_specs=[spec(i) for i in range(count)],
-        out_specs=tuple(
-            pl.BlockSpec(memory_space=pltpu.HBM if i in hbm_outs else pltpu.VMEM) for i in range(len(outs))
-        ),
+        out_specs=tuple(pl.BlockSpec(memory_space=pltpu.VMEM) for _ in outs),
         scratch_shapes=list(scratch),
         compiler_params=pltpu.CompilerParams(vmem_limit_bytes=limit << 20),
         cost_estimate=pl.CostEstimate(flops=int(flops), bytes_accessed=1 << 20, transcendentals=0),
@@ -51,6 +49,13 @@
 
 def iota(shape, dim):
     return lax.broadcasted_iota(jnp.int32, shape, dim)
+
+
+def folded(value):
+    total = value[:, :LANES]
+    for at in range(LANES, value.shape[1], LANES):
+        total = total + value[:, at : at + LANES]
+    return total
 
 
 def layout(local_pairs, depth, slots, fold):
@@ -118,12 +123,12 @@
                 pieces.append(jnp.zeros((ROWS, LANES), f32))
         value = jnp.concatenate(pieces, axis=1)
         if direct:
-            all_buf[owner ^ place] = value
+            all_buf[(place ^ y) % fold, z] = value
         else:
             out_refs[0][owner] = value.astype(bf16)
     if direct:
-        for d, ref in enumerate(out_refs):
-            ref[...] = all_buf[d].astype(ref.dtype)
+        for side, ref in enumerate(out_refs):
+            ref[...] = all_buf[side].astype(ref.dtype)
 
 
 def sum_kernel(parts_ref, out_ref, *, width):
@@ -133,7 +138,15 @@
     out_ref[...] = total.astype(bf16)
 
 
-def direct_sum_kernel(*refs):
+def first_sum_kernel(place_ref, keep_ref, came_ref, own_ref, *send_refs):
+    key = place_ref[3]
+    own_ref[...] = keep_ref[key] + came_ref[key].astype(f32)
+    for d, ref in enumerate(send_refs):
+        at = key ^ (d + 1)
+        ref[...] = (keep_ref[at] + came_ref[at].astype(f32)).astype(bf16)
+
+
+def last_sum_kernel(*refs):
     *parts, out_ref = refs
     total = parts[0][...]
     for ref in parts[1:]:
@@ -143,19 +156,20 @@
 
 def window_kernel(
     place_ref, start_ref, own_ref, right_ref, further_ref, wp_ref,
-    x_ref, xt_ref, var_ref, varrow_ref, hid_ref,
-    rows_buf, xt_buf, w_ref, own_buf, sem,
+    x_ref, xt_ref, var_ref, varrow_ref, hid_ref, facts_ref,
+    rows_buf, xt_buf, sum_buf, w_ref, own_buf, sem,
 ):
     load = pltpu.make_async_copy(wp_ref, w_ref, sem.at[0])
     load_own = pltpu.make_async_copy(own_ref, own_buf, sem.at[1])
     load_own.start()
     load.start()
     channels, height, columns = own_ref.shape
-    offset = start_ref[...] - place_ref[2] * columns
     for r in range(height):
         at = slice(r * channels, (r + 1) * channels)
         rows_buf[at, columns : 2 * columns] = right_ref[:, r, :].astype(bf16)
         rows_buf[at, 2 * columns :] = further_ref[:, r, :].astype(bf16)
+    offset = start_ref[0] - place_ref[2] * columns
+    facts_ref[...] = jnp.zeros(facts_ref.shape, jnp.int32) + offset
     load_own.wait()
     for r in range(height):
         at = slice(r * channels, (r + 1) * channels)
@@ -178,21 +192,21 @@
     xpad = jnp.concatenate([xt, jnp.zeros((LANES - feats, tokens), f32)], axis=0)
     xrow = xpad.T
     model = w_ref.shape[1]
-    block = 64
     x_bf = xrow[:, :feats].astype(bf16)
     load.wait()
-    hid_ref[...] = dot(x_bf, w_ref[...])
-
-    def stats(i, carry):
-        at = pl.ds(pl.multiple_of(i * block, block), block)
-        h = hid_ref[at, :]
-        mean = jnp.sum(h, axis=1, keepdims=True) * (1.0 / model)
-        c = h - mean
-        v = jnp.sum(c * c, axis=1, keepdims=True) * (1.0 / model)
-        var_ref[at, :] = jnp.broadcast_to(v, (block, LANES))
-        return carry
-
-    lax.fori_loop(0, tokens // block, stats, 0)
+    tiles = [slice(at, min(at + 2 * LANES, model)) for at in range(0, model, 2 * LANES)]
+    sum_buf[...] = jnp.zeros(sum_buf.shape, f32)
+    for cols in tiles:
+        value = dot(x_bf, w_ref[:, cols])
+        hid_ref[:, cols] = value
+        sum_buf[...] = sum_buf[...] + folded(value)
+    mean = jnp.sum(sum_buf[...], axis=1, keepdims=True) * (1.0 / model)
+    sum_buf[...] = jnp.zeros(sum_buf.shape, f32)
+    for cols in tiles:
+        value = hid_ref[:, cols] - mean
+        sum_buf[...] = sum_buf[...] + folded(value * value)
+    spread = jnp.sum(sum_buf[...], axis=1, keepdims=True) * (1.0 / model)
+    var_ref[...] = jnp.broadcast_to(spread, var_ref.shape)
     var = var_ref[...]
     std_hi, std_lo = split(jnp.sqrt(var + epsilon))
     spots = iota((tokens, LANES), 1)
@@ -313,12 +327,6 @@
     _, model = hid_ref.shape
     sum_buf[...] = jnp.zeros(sum_buf.shape, f32)
 
-    def folded(value):
-        total = value[:, :LANES]
-        for at in range(LANES, value.shape[1], LANES):
-            total = total + value[:, at : at + LANES]
-        return total
-
     def project(cols):
         mixed = dot(att_buf[...], wo_ref[:, cols])
         value = hid_ref[:, cols] + mod_ref[2, :, cols] * mixed
@@ -362,13 +370,13 @@
 
 
 def spread_kernel(
-    place_ref, start_ref, mine_ref, theirs_ref, lat_ref, own_ref, odd_ref, two_ref, even_ref
+    place_ref, facts_ref, mine_ref, theirs_ref, lat_ref, own_ref, odd_ref, two_ref, even_ref
 ):
     guide = place_ref[1]
     place = place_ref[2]
     near, channels, wide = mine_ref.shape
     columns = wide // 2
-    offset = start_ref[...] - place * columns
+    offset = facts_ref[0:1, 0:1]
     flat = near * channels
     first = guide * (near - 2)
     mine = mine_ref[...].reshape(flat, wide)
@@ -426,7 +434,7 @@
 
 
 def decode_kernel(
-    place_ref, step_ref, own_ref, odd_ref, two_ref, even_ref, lat_ref, count_ref, w_ref, den_ref, feat_out, pad_buf, feat_ref, sems,
+    place_ref, step_ref, own_ref, odd_ref, two_ref, even_ref, lat_ref, count_ref, w_ref, den_ref, feat_ref, pad_buf,
     *, width,
 ):
     guide = place_ref[1]
@@ -436,7 +444,7 @@
     near = half + 1
     flat = near * channels
     first = guide * (near - 2)
-    fraction = (jnp.broadcast_to(step_ref[...], (1, columns)).astype(f32) + 1.0) / STEPS
+    fraction = (jnp.full((1, columns), step_ref[0], jnp.int32).astype(f32) + 1.0) / STEPS
     sigma = 3.0 * fraction / (1.0 + 2.0 * fraction)
     odd = place % 2 == 1
     one = jnp.where(odd, even_ref[...], odd_ref[...]).astype(f32)
@@ -462,7 +470,6 @@
         pad_buf[b, near + 1] = zero
         for i in range(near):
             pad_buf[b, i + 1] = value[i * channels : (i + 1) * channels]
-    saves = []
     for r in range(half):
         at = guide + r
         den_ref[:, r, :] = pad_buf[1, at + 1]
@@ -471,10 +478,6 @@
         ).astype(bf16)
         summed = dot(stacked, w_ref[...], ((0,), (0,)))
         feat_ref[r] = (summed / (1.0 + jnp.exp(-summed))).astype(bf16)
-        saves.append(pltpu.make_async_copy(feat_ref.at[r], feat_out.at[r], sems.at[r]))
-        saves[-1].start()
-    for one in saves:
-        one.wait()
 
 
 def shift(x, by):
@@ -524,6 +527,7 @@
         group = group * 0
     rows = w_qkv.shape[0]
     fold = 2
+    depth = width // fold
     direct = width <= 8 and width & (width - 1) == 0
     changes = jnp.swapaxes(cond_mod, 0, 1)
     key = place // fold if direct else 0
@@ -539,12 +543,12 @@
             partial_kernel, width=width, slots=slots, local_pairs=local_pairs, features=features,
             fold=fold, direct=direct,
         ),
-        [(slab, f32)] + [(slab, bf16)] * (width - 1) if direct else [((width,) + slab, bf16)],
+        [((depth,) + slab, f32), ((depth,) + slab, bf16)] if direct else [((width,) + slab, bf16)],
         scratch=[
             pltpu.VMEM((3, rows, local_pairs * LANES), bf16),
             pltpu.VMEM(changes.shape, f32),
             pltpu.VMEM(w_patch.shape, bf16),
-            pltpu.VMEM((width,) + slab if direct else slab, f32),
+            pltpu.VMEM((fold, depth) + slab if direct else slab, f32),
             pltpu.SemaphoreType.DMA((5,)),
         ],
         anys=(1, 2, 3), smem=(0,), count=4, limit=8,
@@ -552,27 +556,32 @@
     near = height // 2 + 1
     tokens = height // 2 * columns
     if direct:
-        came = [send_xor(parts[d], d) for d in range(width - 1, 0, -1)]
+        came = send_xor(parts[1], 1)
     else:
         came = lax.all_to_all(parts[0], "width", 0, 0, tiled=True)
-    x, xt, var, varrow, hidden = call(
+    x, xt, var, varrow, hidden, facts = call(
         window_kernel,
         [
             ((tokens, LANES), bf16), ((ROWS, tokens), bf16), ((tokens, LANES), f32), ((8, tokens), f32),
-            ((tokens, model), f32),
+            ((tokens, model), f32), ((8, LANES), jnp.int32),
         ],
         scratch=[
             pltpu.VMEM((height * channels, 3 * columns), bf16),
             pltpu.VMEM((feats, tokens), f32),
+            pltpu.VMEM((tokens, LANES), f32),
             pltpu.VMEM(w_patch.shape, bf16),
             pltpu.VMEM(latent.shape, f32),
             pltpu.SemaphoreType.DMA((2,)),
         ],
-        anys=(2, 5), smem=(0,), count=6, flops=5e9,
-    )(scalars, starts[None], in_hbm(latent), right, further, in_hbm(w_patch))
+        anys=(2, 5), smem=(0, 1), count=6, flops=5e9,
+    )(scalars, starts, in_hbm(latent), right, further, in_hbm(w_patch))
     came, x = lax.optimization_barrier((came, x))
     if direct:
-        (chunk,) = call(direct_sum_kernel, [(slab, bf16)], count=width, limit=4)(parts[0], *came)
+        own, *sends = call(
+            first_sum_kernel, [(slab, f32)] + [(slab, bf16)] * (depth - 1), smem=(0,), count=3, limit=4
+        )(scalars, parts[0], came)
+        got = [send_xor(sends[d - 1], d * fold) for d in range(depth - 1, 0, -1)]
+        (chunk,) = call(last_sum_kernel, [(slab, bf16)], count=depth, limit=4)(own, *got)
     else:
         (chunk,) = call(
             functools.partial(sum_kernel, width=width), [(slab, bf16)], count=1, limit=4
@@ -619,7 +628,7 @@
             ((flat, 2 * columns), bf16), ((flat, 2 * columns), bf16),
         ],
         smem=(0,), count=5, limit=8,
-    )(scalars, starts[None], mine_v, theirs, latent)
+    )(scalars, facts, mine_v, theirs, latent)
     ups = [(i, (i + 1) % width) for i in range(width)]
     turns = [[pair for pair in ups if pair[0] % 2 == side] for side in range(2)]
     turns = [pairs + [(b, a) for a, b in pairs] for pairs in turns]
@@ -631,11 +640,9 @@
         [((channels, height // 2, columns), f32), ((height // 2, columns, w_dec.shape[1]), bf16)],
         scratch=[
             pltpu.VMEM((3, near + 2, channels, columns), f32),
-            pltpu.VMEM((height // 2, columns, w_dec.shape[1]), bf16),
-            pltpu.SemaphoreType.DMA((height // 2,)),
         ],
-        smem=(0,), count=9, limit=8, hbm_outs=(1,),
-    )(scalars, step_index[None], own, odd, two, even, latent, counts[None], w_dec)
+        smem=(0, 1), count=9, limit=8,
+    )(scalars, step_index, own, odd, two, even, latent, counts[None], w_dec)
 
 
 def solution(mesh):

time: 68.4 us -> 66 us (0.965)
  starting transfers between devices: 28.6 us -> 23 us
  waiting for transfers between devices: 9.52 us -> 14.4 us
  Pallas kernels: 27.6 us -> 26.2 us
    ppermute x10 -> x7, starting transfers between devices: 13.6 us -> 9.6 us  [send_xor(): return lax.ppermute(x, 'width', [(i, i ^ d) for i in range(width)])]
    ppermute x10 -> x7, waiting for transfers between devices: 4.52 us -> 7.21 us  [send_xor(): return lax.ppermute(x, 'width', [(i, i ^ d) for i in range(width)])]
    ppermute x1, starting transfers between devices: 2.17 us -> 0.01 us  [shards(): even = lax.ppermute(even, 'width', turns[0])]
    ppermute x1, waiting for transfers between devices: 1.6 us -> 3.3 us  [shards(): odd = lax.ppermute(odd, 'width', turns[1])]
    pallas_call x1, Pallas kernels: 4.84 us -> 3.25 us  [shards(): call(window_kernel, [((tokens, LANES), bf16), ((ROWS, tokens), bf16), ((t...]
  transfers between devices with their start and end apart: 19 -> 16, of which waited for: 8 -> 11; matrix products, arithmetic and copies ran while one was open for 0% -> 0% of each run, Pallas kernels for 19% -> 17%
where the time goes in v7:
time: 66 us; the launch traced here: 65.8 us
  Pallas kernels  26.2 us (40%)
  starting transfers between devices  23 us (35%)
  waiting for transfers between devices  14.4 us (22%)
  between operations  2.11 us (3%)
    pallas_call x1, Pallas kernels, shards(): call(functools.partial(second_kernel, channels=channels, height=height, c...  11.2 us
    ppermute x7, starting transfers between devices, send_xor(): return lax.ppermute(x, 'width', [(i, i ^ d) for i in range(width)])  9.6 us
    ppermute x7, waiting for transfers between devices, send_xor(): return lax.ppermute(x, 'width', [(i, i ^ d) for i in range(width)])  7.21 us
    ppermute x2, starting transfers between devices, shift(): lax.ppermute(x, 'width', [(i, (i + by) % peers) for i in range(peers)])  6.54 us
    ppermute x1, waiting for transfers between devices, shards(): odd = lax.ppermute(odd, 'width', turns[1])  3.3 us
    pallas_call x1, Pallas kernels, shards(): call(window_kernel, [((tokens, LANES), bf16), ((ROWS, tokens), bf16), ((t...  3.25 us
    pallas_call x1, Pallas kernels, shards(): call(functools.partial(attend_kernel, units=(whole, local_pairs), **sizes...  3.17 us
    ppermute x3, starting transfers between devices, swap(): return lax.ppermute(x, axis, [(0, 1), (1, 0)])  3.07 us
  transfers between devices with their start and end apart: 16, of which 11 were waited for; matrix products, arithmetic and copies ran while one was open for 0% of the time, Pallas kernels for 17%

profile of v7, /device:TPU:0, one launch (start us, length us, event | category | flops | bytes accessed | tf_op | source)
XLA Modules:
  0.0 65.8 jit_solution(10128388486926968418)
XLA Ops:
  0.6 6.1 %collective-permute-start = (f32[16,8,128]{2,1,0:T(8,128)}, f32[16,8,128]{2,1,0:T(8,128)S(1)}, u32[]{:S(2)}, u32[]{:S(2)}) collective-permute-start(f32[16,8,128]{2,1,0:T(8,128)} %lat_ref.3), channel_id=1, source_target_pairs={{0,14},{2,0},{4,2},{6,4},{8,6},{10,8},{12,10},{14,12},{1,15},{3,1}... | collective-permute-start | bytes 196616 | tf_op jit(solution)/shard_map/ppermute | solution.py:485
  6.7 0.4 collective-permute-start.1
  7.2 0.1 pad_add_fusion.place_ref
  7.2 2.7 %shard_map.114 = (f32[4,72,256]{2,1,0:T(8,128)S(1)}, bf16[4,72,256]{2,1,0:T(8,128)(2,1)S(1)}) custom-call(s32[4]{0:T(128)S(1)} %pad_add_fusion.place_ref, f32[3,1,2432]{2,1,0:T(1,128)} %bitcast.12, bf16[64,2432]{1,0:T(8,128)(2,1)} %wp_ref.3, bf16[304,3840]{1,0:T(8,128)(2,1)} %w_ref.2), custom_call_target="tpu_custom_call" | custom-call | bytes 1048576 | tf_op jit(solution)/shard_map/pallas_call | solution.py:541
  9.9 0.7 %collective-permute-start.2 = (bf16[4,72,256]{2,1,0:T(8,128)(2,1)S(1)}, bf16[4,72,256]{2,1,0:T(8,128)(2,1)S(1)}, u32[]{:S(2)}, u32[]{:S(2)}) collective-permute-start(bf16[4,72,256]{2,1,0:T(8,128)(2,1)S(1)} %get-tuple-element.26), channel_id=1, source_target_pairs={{0,2},{2,0},{4,6},{6,4},{8,10},{10,8},{12,14},{14,12},{1,3},{3,1},... | collective-permute-start | bytes 442376 | tf_op jit(solution)/shard_map/ppermute | solution.py:494
  11.3 0.0 collective-permute-done.right_ref
  11.3 0.0 collective-permute-done.1.further_ref
  11.3 3.2 %shard_map.113 = (bf16[512,128]{1,0:T(8,128)(2,1)S(1)}, bf16[72,512]{1,0:T(8,128)(2,1)S(1)}, f32[512,128]{1,0:T(8,128)S(1)}, f32[8,512]{1,0:T(8,128)S(1)}, f32[5...) custom-call(s32[4]{0:T(128)S(1)} %pad_add_fusion.place_ref, s32[1]{0:T(128)S(6)} %copy.12.start_ref, f32[16,8,128]{2,1,0:T(8,128)} %lat_ref.3, ...), custom_call_target="tpu_custom_call" | custom-call | flops 5000000000 | bytes 1048576 | tf_op jit(solution)/shard_map/pallas_call | solution.py:562
  14.5 0.6 collective-permute-done.2.came_ref
  15.1 0.6 shard_map.115
  15.7 2.2 %collective-permute-start.3 = (bf16[72,256]{1,0:T(8,128)(2,1)S(1)}, bf16[72,256]{1,0:T(8,128)(2,1)S(1)}, u32[]{:S(2)}, u32[]{:S(2)}) collective-permute-start(bf16[72,256]{1,0:T(8,128)(2,1)S(1)} %get-tuple-element.30), channel_id=1, source_target_pairs={{0,12},{2,14},{4,8},{6,10},{8,4},{10,6},{12,0},{14,2},{1,13},{3,15... | collective-permute-start | bytes 110600 | tf_op jit(solution)/shard_map/ppermute | solution.py:494
  17.9 0.9 %collective-permute-start.4 = (bf16[72,256]{1,0:T(8,128)(2,1)S(1)}, bf16[72,256]{1,0:T(8,128)(2,1)S(1)}, u32[]{:S(2)}, u32[]{:S(2)}) collective-permute-start(bf16[72,256]{1,0:T(8,128)(2,1)S(1)} %get-tuple-element.31), channel_id=1, source_target_pairs={{0,8},{2,10},{4,12},{6,14},{8,0},{10,2},{12,4},{14,6},{1,9},{3,11}... | collective-permute-start | bytes 110600 | tf_op jit(solution)/shard_map/ppermute | solution.py:494
  18.8 1.3 %collective-permute-start.5 = (bf16[72,256]{1,0:T(8,128)(2,1)S(1)}, bf16[72,256]{1,0:T(8,128)(2,1)S(1)}, u32[]{:S(2)}, u32[]{:S(2)}) collective-permute-start(bf16[72,256]{1,0:T(8,128)(2,1)S(1)} %get-tuple-element.32), channel_id=1, source_target_pairs={{0,4},{2,6},{4,0},{6,2},{8,12},{10,14},{12,8},{14,10},{1,5},{3,7},... | collective-permute-start | bytes 110600 | tf_op jit(solution)/shard_map/ppermute | solution.py:494
  20.2 1.6 %collective-permute-done.3.refs_1_ = bf16[72,256]{1,0:T(8,128)(2,1)S(1)} collective-permute-done((bf16[72,256]{1,0:T(8,128)(2,1)S(1)}, bf16[72,256]{1,0:T(8,128)(2,1)S(1)}, u32[]{:S(2)}, u32[]{:S(2)}) %collective-permute-start.3) | collective-permute-done | bytes 36896 | tf_op jit(solution)/shard_map/ppermute | solution.py:494
  21.7 1.0 %collective-permute-done.4.refs_2_ = bf16[72,256]{1,0:T(8,128)(2,1)S(1)} collective-permute-done((bf16[72,256]{1,0:T(8,128)(2,1)S(1)}, bf16[72,256]{1,0:T(8,128)(2,1)S(1)}, u32[]{:S(2)}, u32[]{:S(2)}) %collective-permute-start.4) | collective-permute-done | bytes 36896 | tf_op jit(solution)/shard_map/ppermute | solution.py:494
  22.8 0.7 %collective-permute-done.5.refs_3_ = bf16[72,256]{1,0:T(8,128)(2,1)S(1)} collective-permute-done((bf16[72,256]{1,0:T(8,128)(2,1)S(1)}, bf16[72,256]{1,0:T(8,128)(2,1)S(1)}, u32[]{:S(2)}, u32[]{:S(2)}) %collective-permute-start.5) | collective-permute-done | bytes 36896 | tf_op jit(solution)/shard_map/ppermute | solution.py:494
  23.5 1.0 %collective-permute-start.6 = (bf16[72,256]{1,0:T(8,128)(2,1)S(1)}, bf16[72,256]{1,0:T(8,128)(2,1)S(1)}, u32[]{:S(2)}, u32[]{:S(2)}) collective-permute-start(bf16[72,256]{1,0:T(8,128)(2,1)S(1)} %shard_map.116), channel_id=1, source_target_pairs={{0,4},{2,6},{4,0},{6,2},{8,12},{10,14},{12,8},{14,10},{1,5},{3,7},... | collective-permute-start | bytes 110600 | tf_op jit(solution)/shard_map/ppermute | solution.py:494
  24.5 1.0 %collective-permute-start.7 = (bf16[72,256]{1,0:T(8,128)(2,1)S(1)}, bf16[72,256]{1,0:T(8,128)(2,1)S(1)}, u32[]{:S(2)}, u32[]{:S(2)}) collective-permute-start(bf16[72,256]{1,0:T(8,128)(2,1)S(1)} %shard_map.116), channel_id=1, source_target_pairs={{0,8},{2,10},{4,12},{6,14},{8,0},{10,2},{12,4},{14,6},{1,9},{3,11}... | collective-permute-start | bytes 110600 | tf_op jit(solution)/shard_map/ppermute | solution.py:494
  25.5 2.5 %collective-permute-start.8 = (bf16[72,256]{1,0:T(8,128)(2,1)S(1)}, bf16[72,256]{1,0:T(8,128)(2,1)S(1)}, u32[]{:S(2)}, u32[]{:S(2)}) collective-permute-start(bf16[72,256]{1,0:T(8,128)(2,1)S(1)} %shard_map.116), channel_id=1, source_target_pairs={{0,12},{2,14},{4,8},{6,10},{8,4},{10,6},{12,0},{14,2},{1,13},{3,15... | collective-permute-start | bytes 110600 | tf_op jit(solution)/shard_map/ppermute | solution.py:494
  28.0 0.0 collective-permute-done.6
  28.0 1.4 %collective-permute-done.7 = bf16[72,256]{1,0:T(8,128)(2,1)S(1)} collective-permute-done((bf16[72,256]{1,0:T(8,128)(2,1)S(1)}, bf16[72,256]{1,0:T(8,128)(2,1)S(1)}, u32[]{:S(2)}, u32[]{:S(2)}) %collective-permute-start.7) | collective-permute-done | bytes 36896 | tf_op jit(solution)/shard_map/ppermute | solution.py:494
  29.4 1.9 %collective-permute-done.8 = bf16[72,256]{1,0:T(8,128)(2,1)S(1)} collective-permute-done((bf16[72,256]{1,0:T(8,128)(2,1)S(1)}, bf16[72,256]{1,0:T(8,128)(2,1)S(1)}, u32[]{:S(2)}, u32[]{:S(2)}) %collective-permute-start.8) | collective-permute-done | bytes 36896 | tf_op jit(solution)/shard_map/ppermute | solution.py:494
  31.3 0.9 %collective-permute-start.10 = (bf16[4,72,256]{2,1,0:T(8,128)(2,1)S(1)}, bf16[4,72,256]{2,1,0:T(8,128)(2,1)S(1)}, u32[]{:S(2)}, u32[]{:S(2)}) collective-permute-start(bf16[4,72,256]{2,1,0:T(8,128)(2,1)S(1)} %pad_maximum_fusion.near_ref), channel_id=1, source_target_pairs={{0,2},{2,0},{4,6},{6,4},{8,10},{10,8},{12,14},{14,12},{1,3},{3,1},... | collective-permute-start | bytes 442376 | tf_op jit(solution)/shard_map/ppermute | solution.py:510
  32.2 1.5 %collective-permute-start.9 = (bf16[4,72,256]{2,1,0:T(8,128)(2,1)S(1)}, bf16[4,72,256]{2,1,0:T(8,128)(2,1)S(1)}, u32[]{:S(2)}, u32[]{:S(2)}) collective-permute-start(bf16[4,72,256]{2,1,0:T(8,128)(2,1)S(1)} %pad_maximum_fusion.near_ref), channel_id=1, source_target_pairs={{0,16},{16,0},{1,17},{17,1},{2,18},{18,2},{3,19},{19,3},{4,20},{20... | collective-permute-start | bytes 442376 | tf_op jit(solution)/shard_map/ppermute | solution.py:489
  33.7 2.4 %shard_map.117.refs_0_ = bf16[512,256]{1,0:T(8,128)(2,1)S(1)} custom-call(s32[4]{0:T(128)S(1)} %pad_add_fusion.place_ref, bf16[4,72,256]{2,1,0:T(8,128)(2,1)S(1)} %pad_maximum_fusion.near_ref, bf16[512,128]{1,0:T(8,128)(2,1)S(1)} %get-tuple-element.33.x_ref, bf16[72,512]{1,0:T(8,128)(2,1)S(1)} %get-tuple-element.34.xt_ref, ...), custom_call_target="tpu_custom_call" | custom-call | flops 2000000000 | bytes 1048576 | tf_op jit(solution)/shard_map/pallas_call | solution.py:594
  36.1 0.0 copy-start.2
  36.1 0.0 slice-start.1
  36.1 0.0 copy-start.4
  36.1 0.4 collective-permute-done.10.far_ref
  36.5 1.5 %collective-permute-start.11 = (bf16[4,72,256]{2,1,0:T(8,128)(2,1)S(1)}, bf16[4,72,256]{2,1,0:T(8,128)(2,1)S(1)}, u32[]{:S(2)}, u32[]{:S(2)}) collective-permute-start(bf16[4,72,256]{2,1,0:T(8,128)(2,1)S(1)} %collective-permute-done.10.far_ref), channel_id=1, source_target_pairs={{0,16},{16,0},{1,17},{17,1},{2,18},{18,2},{3,19},{19,3},{4,20},{20... | collective-permute-start | bytes 442376 | tf_op jit(solution)/shard_map/ppermute | solution.py:489
  38.0 3.2 %shard_map.118.refs_1_ = bf16[512,384]{1,0:T(8,128)(2,1)S(1)} custom-call(s32[4]{0:T(128)S(1)} %pad_add_fusion.place_ref, bf16[4,72,256]{2,1,0:T(8,128)(2,1)S(1)} %pad_maximum_fusion.near_ref, bf16[4,72,256]{2,1,0:T(8,128)(2,1)S(1)} %collective-permute-done.10.far_ref, bf16[512,128]{1,0:T(8,128)(2,1)S(1)} %get-tuple-element.33.x_ref, ...), custom_call_target="tpu_custom_call" | custom-call | flops 3000000000 | bytes 1048576 | tf_op jit(solution)/shard_map/pallas_call | solution.py:604
  41.2 0.0 collective-permute-done.9.near_ref
  41.2 0.5 collective-permute-done.11.far_ref
  41.6 0.0 copy-done.2
  41.7 0.0 copy-start
  41.7 0.0 copy-start.1
  41.7 0.0 copy-start.3
  41.7 11.2 %shard_map.119 = (f32[5,16,256]{2,1,0:T(8,128)S(1)}, bf16[5,16,256]{2,1,0:T(8,128)(2,1)S(1)}) custom-call(s32[4]{0:T(128)S(1)} %pad_add_fusion.place_ref, bf16[4,72,256]{2,1,0:T(8,128)(2,1)S(1)} %collective-permute-done.9.near_ref, bf16[4,72,256]{2,1,0:T(8,128)(2,1)S(1)} %collective-permute-done.11.far_ref, bf16[512,128]{1,0:T(8,128)(2,1)S(1)} %get-tuple-element.33.x_ref, ...), custom_call_target="tpu_custom_call" | custom-call | flops 12000000000 | bytes 1048576 | tf_op jit(solution)/shard_map/pallas_call | solution.py:609
  52.9 0.1 collective-permute-start.12
  53.0 1.2 %collective-permute-done.12.theirs_ref = bf16[5,16,256]{2,1,0:T(8,128)(2,1)S(1)} collective-permute-done((bf16[5,16,256]{2,1,0:T(8,128)(2,1)S(1)}, bf16[5,16,256]{2,1,0:T(8,128)(2,1)S(1)}, u32[]{:S(2)}, u32[]{:S(2)}) %collective-permute-start.12) | collective-permute-done | bytes 40992 | tf_op jit(solution)/shard_map/ppermute | solution.py:489
  54.2 0.9 %shard_map.120 = (f32[80,256]{1,0:T(8,128)S(1)}, bf16[80,256]{1,0:T(8,128)(2,1)S(1)}, bf16[80,256]{1,0:T(8,128)(2,1)S(1)}, bf16[80,256]{1,0:T(8,128)(2,1)S(1)}) custom-call(s32[4]{0:T(128)S(1)} %pad_add_fusion.place_ref, s32[8,128]{1,0:T(8,128)S(1)} %get-tuple-element.24.facts_ref, f32[5,16,256]{2,1,0:T(8,128)S(1)} %get-tuple-element.40.mine_ref, ...), custom_call_target="tpu_custom_call" | custom-call | bytes 1048576 | tf_op jit(solution)/shard_map/pallas_call | solution.py:624
  55.1 2.9 %collective-permute-start.13 = (bf16[80,256]{1,0:T(8,128)(2,1)S(1)}, bf16[80,256]{1,0:T(8,128)(2,1)S(1)}, u32[]{:S(2)}, u32[]{:S(2)}) collective-permute-start(bf16[80,256]{1,0:T(8,128)(2,1)S(1)} %get-tuple-element.43), channel_id=1, source_target_pairs={{2,4},{6,8},{10,12},{14,0},{4,2},{8,6},{12,10},{0,14},{3,5},{7,9},... | collective-permute-start | bytes 122888 | tf_op jit(solution)/shard_map/ppermute | solution.py:635
  58.0 0.0 collective-permute-start.14
  58.0 0.0 collective-permute-start.15
  58.6 3.3 %collective-permute-done.13.odd_ref = bf16[80,256]{1,0:T(8,128)(2,1)S(1)} collective-permute-done((bf16[80,256]{1,0:T(8,128)(2,1)S(1)}, bf16[80,256]{1,0:T(8,128)(2,1)S(1)}, u32[]{:S(2)}, u32[]{:S(2)}) %collective-permute-start.13) | collective-permute-done | bytes 40992 | tf_op jit(solution)/shard_map/ppermute | solution.py:635
  61.9 1.8 %collective-permute-done.14.two_ref = bf16[80,256]{1,0:T(8,128)(2,1)S(1)} collective-permute-done((bf16[80,256]{1,0:T(8,128)(2,1)S(1)}, bf16[80,256]{1,0:T(8,128)(2,1)S(1)}, u32[]{:S(2)}, u32[]{:S(2)}) %collective-permute-start.14) | collective-permute-done | bytes 40992 | tf_op jit(solution)/shard_map/ppermute | solution.py:636
  63.8 0.0 collective-permute-done.15.even_ref
  63.8 2.1 %shard_map.121 = (f32[16,4,128]{2,1,0:T(4,128)}, bf16[4,128,512]{2,1,0:T(8,128)(2,1)}) custom-call(s32[4]{0:T(128)S(1)} %pad_add_fusion.place_ref, s32[1]{0:T(128)S(6)} %copy.13.step_ref, f32[80,256]{1,0:T(8,128)S(1)} %get-tuple-element.42.own_ref, bf16[80,256]{1,0:T(8,128)(2,1)S(1)} %collective-permute-done.13.odd_ref, ...), custom_call_target="tpu_custom_call" | custom-call | bytes 1048576 | tf_op jit(solution)/shard_map/pallas_call | solution.py:638
  (10 shorter events, 0.1 us)
Async XLA Ops:
  0.6 10.6 %collective-permute-start = (f32[16,8,128]{2,1,0:T(8,128)}, f32[16,8,128]{2,1,0:T(8,128)S(1)}, u32[]{:S(2)}, u32[]{:S(2)}) collective-permute-start(f32[16,8,128]{2,1,0:T(8,128)} %lat_ref.3), channel_id=1, source_target_pairs={{0,14},{2,0},{4,2},{6,4},{8,6},{10,8},{12,10},{14,12},{1,15},{3,1}... | collective-permute-start | bytes 196616 | tf_op jit(solution)/shard_map/ppermute | solution.py:485
  6.7 4.6 %collective-permute-start.1 = (f32[16,8,128]{2,1,0:T(8,128)}, f32[16,8,128]{2,1,0:T(8,128)S(1)}, u32[]{:S(2)}, u32[]{:S(2)}) collective-permute-start(f32[16,8,128]{2,1,0:T(8,128)} %lat_ref.3), channel_id=1, source_target_pairs={{0,12},{2,14},{4,0},{6,2},{8,4},{10,6},{12,8},{14,10},{1,13},{3,15... | collective-permute-start | bytes 196616 | tf_op jit(solution)/shard_map/ppermute | solution.py:485
  9.9 5.2 %collective-permute-start.2 = (bf16[4,72,256]{2,1,0:T(8,128)(2,1)S(1)}, bf16[4,72,256]{2,1,0:T(8,128)(2,1)S(1)}, u32[]{:S(2)}, u32[]{:S(2)}) collective-permute-start(bf16[4,72,256]{2,1,0:T(8,128)(2,1)S(1)} %get-tuple-element.26), channel_id=1, source_target_pairs={{0,2},{2,0},{4,6},{6,4},{8,10},{10,8},{12,14},{14,12},{1,3},{3,1},... | collective-permute-start | bytes 442376 | tf_op jit(solution)/shard_map/ppermute | solution.py:494
  15.7 6.0 %collective-permute-start.3 = (bf16[72,256]{1,0:T(8,128)(2,1)S(1)}, bf16[72,256]{1,0:T(8,128)(2,1)S(1)}, u32[]{:S(2)}, u32[]{:S(2)}) collective-permute-start(bf16[72,256]{1,0:T(8,128)(2,1)S(1)} %get-tuple-element.30), channel_id=1, source_target_pairs={{0,12},{2,14},{4,8},{6,10},{8,4},{10,6},{12,0},{14,2},{1,13},{3,15... | collective-permute-start | bytes 110600 | tf_op jit(solution)/shard_map/ppermute | solution.py:494
  17.9 4.9 %collective-permute-start.4 = (bf16[72,256]{1,0:T(8,128)(2,1)S(1)}, bf16[72,256]{1,0:T(8,128)(2,1)S(1)}, u32[]{:S(2)}, u32[]{:S(2)}) collective-permute-start(bf16[72,256]{1,0:T(8,128)(2,1)S(1)} %get-tuple-element.31), channel_id=1, source_target_pairs={{0,8},{2,10},{4,12},{6,14},{8,0},{10,2},{12,4},{14,6},{1,9},{3,11}... | collective-permute-start | bytes 110600 | tf_op jit(solution)/shard_map/ppermute | solution.py:494
  18.8 4.7 %collective-permute-start.5 = (bf16[72,256]{1,0:T(8,128)(2,1)S(1)}, bf16[72,256]{1,0:T(8,128)(2,1)S(1)}, u32[]{:S(2)}, u32[]{:S(2)}) collective-permute-start(bf16[72,256]{1,0:T(8,128)(2,1)S(1)} %get-tuple-element.32), channel_id=1, source_target_pairs={{0,4},{2,6},{4,0},{6,2},{8,12},{10,14},{12,8},{14,10},{1,5},{3,7},... | collective-permute-start | bytes 110600 | tf_op jit(solution)/shard_map/ppermute | solution.py:494
  23.5 4.5 %collective-permute-start.6 = (bf16[72,256]{1,0:T(8,128)(2,1)S(1)}, bf16[72,256]{1,0:T(8,128)(2,1)S(1)}, u32[]{:S(2)}, u32[]{:S(2)}) collective-permute-start(bf16[72,256]{1,0:T(8,128)(2,1)S(1)} %shard_map.116), channel_id=1, source_target_pairs={{0,4},{2,6},{4,0},{6,2},{8,12},{10,14},{12,8},{14,10},{1,5},{3,7},... | collective-permute-start | bytes 110600 | tf_op jit(solution)/shard_map/ppermute | solution.py:494
  24.5 4.9 %collective-permute-start.7 = (bf16[72,256]{1,0:T(8,128)(2,1)S(1)}, bf16[72,256]{1,0:T(8,128)(2,1)S(1)}, u32[]{:S(2)}, u32[]{:S(2)}) collective-permute-start(bf16[72,256]{1,0:T(8,128)(2,1)S(1)} %shard_map.116), channel_id=1, source_target_pairs={{0,8},{2,10},{4,12},{6,14},{8,0},{10,2},{12,4},{14,6},{1,9},{3,11}... | collective-permute-start | bytes 110600 | tf_op jit(solution)/shard_map/ppermute | solution.py:494
  25.5 5.8 %collective-permute-start.8 = (bf16[72,256]{1,0:T(8,128)(2,1)S(1)}, bf16[72,256]{1,0:T(8,128)(2,1)S(1)}, u32[]{:S(2)}, u32[]{:S(2)}) collective-permute-start(bf16[72,256]{1,0:T(8,128)(2,1)S(1)} %shard_map.116), channel_id=1, source_target_pairs={{0,12},{2,14},{4,8},{6,10},{8,4},{10,6},{12,0},{14,2},{1,13},{3,15... | collective-permute-start | bytes 110600 | tf_op jit(solution)/shard_map/ppermute | solution.py:494
  31.3 5.2 %collective-permute-start.10 = (bf16[4,72,256]{2,1,0:T(8,128)(2,1)S(1)}, bf16[4,72,256]{2,1,0:T(8,128)(2,1)S(1)}, u32[]{:S(2)}, u32[]{:S(2)}) collective-permute-start(bf16[4,72,256]{2,1,0:T(8,128)(2,1)S(1)} %pad_maximum_fusion.near_ref), channel_id=1, source_target_pairs={{0,2},{2,0},{4,6},{6,4},{8,10},{10,8},{12,14},{14,12},{1,3},{3,1},... | collective-permute-start | bytes 442376 | tf_op jit(solution)/shard_map/ppermute | solution.py:510
  32.2 9.0 %collective-permute-start.9 = (bf16[4,72,256]{2,1,0:T(8,128)(2,1)S(1)}, bf16[4,72,256]{2,1,0:T(8,128)(2,1)S(1)}, u32[]{:S(2)}, u32[]{:S(2)}) collective-permute-start(bf16[4,72,256]{2,1,0:T(8,128)(2,1)S(1)} %pad_maximum_fusion.near_ref), channel_id=1, source_target_pairs={{0,16},{16,0},{1,17},{17,1},{2,18},{18,2},{3,19},{19,3},{4,20},{20... | collective-permute-start | bytes 442376 | tf_op jit(solution)/shard_map/ppermute | solution.py:489
  33.7 8.0 %slice-start = ((s8[6225920]{0:T(1024)(128)(4,1)}), s8[4194304]{0:T(1024)(128)(4,1)S(1)}, s32[]{:S(2)}) async-start(s8[6225920]{0:T(1024)(128)(4,1)} %bitcast.15), calls=%async_computation | async-start | bytes 8388608
  36.1 5.5 %copy-start.2 = (f32[1,3,2432]{2,0,1:T(1,128)S(1)}, f32[1,3,2432]{2,0,1:T(1,128)}, u32[]{:S(2)}) copy-start(f32[1,3,2432]{2,0,1:T(1,128)} %param.14) | copy-start | bytes 87556
  36.1 5.5 %slice-start.1 = ((s8[6225920]{0:T(1024)(128)(4,1)}), s8[2031616]{0:T(1024)(128)(4,1)S(1)}, s32[]{:S(2)}) async-start(s8[6225920]{0:T(1024)(128)(4,1)} %bitcast.15), calls=%async_computation.1 | async-start | bytes 4063232
  36.1 5.5 %copy-start.4 = (bf16[2432,64]{0,1:T(8,128)(2,1)S(1)}, bf16[2432,64]{0,1:T(8,128)(2,1)}, u32[]{:S(2)}) copy-start(bf16[2432,64]{0,1:T(8,128)(2,1)} %param.18) | copy-start | bytes 933892
  36.5 5.1 %collective-permute-start.11 = (bf16[4,72,256]{2,1,0:T(8,128)(2,1)S(1)}, bf16[4,72,256]{2,1,0:T(8,128)(2,1)S(1)}, u32[]{:S(2)}, u32[]{:S(2)}) collective-permute-start(bf16[4,72,256]{2,1,0:T(8,128)(2,1)S(1)} %collective-permute-done.10.far_ref), channel_id=1, source_target_pairs={{0,16},{16,0},{1,17},{17,1},{2,18},{18,2},{3,19},{19,3},{4,20},{20... | collective-permute-start | bytes 442376 | tf_op jit(solution)/shard_map/ppermute | solution.py:489
  41.7 12.5 %copy-start = (f32[16,8,128]{2,1,0:T(8,128)S(1)}, f32[16,8,128]{2,1,0:T(8,128)}, u32[]{:S(2)}) copy-start(f32[16,8,128]{2,1,0:T(8,128)} %lat_ref.3) | copy-start | bytes 196612
  41.7 22.1 %copy-start.1 = (bf16[144,512]{1,0:T(8,128)(2,1)S(1)}, bf16[144,512]{1,0:T(8,128)(2,1)}, u32[]{:S(2)}) copy-start(bf16[144,512]{1,0:T(8,128)(2,1)} %w_ref.3) | copy-start | bytes 442372
  41.7 22.1 %copy-start.3 = (s32[128]{0:T(128)S(1)}, s32[128]{0:T(128)}, u32[]{:S(2)}) copy-start(s32[128]{0:T(128)} %param.12) | copy-start | bytes 1540
  52.9 1.3 %collective-permute-start.12 = (bf16[5,16,256]{2,1,0:T(8,128)(2,1)S(1)}, bf16[5,16,256]{2,1,0:T(8,128)(2,1)S(1)}, u32[]{:S(2)}, u32[]{:S(2)}) collective-permute-start(bf16[5,16,256]{2,1,0:T(8,128)(2,1)S(1)} %get-tuple-element.41), channel_id=1, source_target_pairs={{0,1},{1,0},{2,3},{3,2},{4,5},{5,4},{6,7},{7,6},{8,9},{9,8},{10,11... | collective-permute-start | bytes 122888 | tf_op jit(solution)/shard_map/ppermute | solution.py:489
  55.1 6.8 %collective-permute-start.13 = (bf16[80,256]{1,0:T(8,128)(2,1)S(1)}, bf16[80,256]{1,0:T(8,128)(2,1)S(1)}, u32[]{:S(2)}, u32[]{:S(2)}) collective-permute-start(bf16[80,256]{1,0:T(8,128)(2,1)S(1)} %get-tuple-element.43), channel_id=1, source_target_pairs={{2,4},{6,8},{10,12},{14,0},{4,2},{8,6},{12,10},{0,14},{3,5},{7,9},... | collective-permute-start | bytes 122888 | tf_op jit(solution)/shard_map/ppermute | solution.py:635
  58.0 5.8 %collective-permute-start.14 = (bf16[80,256]{1,0:T(8,128)(2,1)S(1)}, bf16[80,256]{1,0:T(8,128)(2,1)S(1)}, u32[]{:S(2)}, u32[]{:S(2)}) collective-permute-start(bf16[80,256]{1,0:T(8,128)(2,1)S(1)} %get-tuple-element.44), channel_id=1, source_target_pairs={{0,4},{2,6},{4,8},{6,10},{8,12},{10,14},{12,0},{14,2},{1,5},{3,7},... | collective-permute-start | bytes 122888 | tf_op jit(solution)/shard_map/ppermute | solution.py:636
  58.0 5.8 %collective-permute-start.15 = (bf16[80,256]{1,0:T(8,128)(2,1)S(1)}, bf16[80,256]{1,0:T(8,128)(2,1)S(1)}, u32[]{:S(2)}, u32[]{:S(2)}) collective-permute-start(bf16[80,256]{1,0:T(8,128)(2,1)S(1)} %get-tuple-element.45), channel_id=1, source_target_pairs={{0,2},{4,6},{8,10},{12,14},{2,0},{6,4},{10,8},{14,12},{1,3},{5,7},... | collective-permute-start | bytes 122888 | tf_op jit(solution)/shard_map/ppermute | solution.py:637
